TPU v7x, 32 devices: a whole 2x2x4 slice. The times are simulated.
32 devices in a mesh: rep: 8 (over y, x, core), shard: 4 (over z).
Axes of the slice: x: 2, y: 2, z: 4, core: 2. Of those that a mesh axis runs over, the one named last changes fastest.
Arguments:
- hidden_in: bfloat16 [8, 512, 2048], P('rep', 'shard'), may hold values from -6 to 6
- segment_ids: int32 [8, 512], P('rep', 'shard'), may hold values from 0 to 7, never falling along the last dimension, each value on 1 to 320 neighbouring positions
- out_grad: bfloat16 [8, 512, 2048], P('rep', 'shard'), may hold values from -6 to 6
- qkv_weight_state: float32 [3, 2048, 6144], P(None, ('rep', 'shard')), as said below
- qkv_bias_state: float32 [3, 6144], P(None, ('rep', 'shard')), as said below
- dense_weight_state: float32 [3, 2048, 2048], P(None, ('rep', 'shard')), as said below
- up_weight_state: float32 [3, 2048, 8192], P(None, ('rep', 'shard')), as said below
- up_bias_state: float32 [3, 8192], P(None, ('rep', 'shard')), as said below
- down_weight_state: float32 [3, 8192, 2048], P(None, ('rep', 'shard')), as said below
- vector_state: float32 [3, 2048, 4], P(None, ('rep', 'shard')), as said below
Outputs:
- output: bfloat16 [8, 512, 2048], P('rep', 'shard')
- input_grad: float32 [8, 512, 2048], P('rep', 'shard')
- qkv_weight_grad: float32 [2048, 6144], P(('rep', 'shard'))
- qkv_bias_grad: float32 [6144], P(('rep', 'shard'))
- dense_weight_grad: float32 [2048, 2048], P(('rep', 'shard'))
- up_weight_grad: float32 [2048, 8192], P(('rep', 'shard'))
- up_bias_grad: float32 [8192], P(('rep', 'shard'))
- down_weight_grad: float32 [8192, 2048], P(('rep', 'shard'))
- vector_grad: float32 [2048, 4], P(('rep', 'shard'))
- weights_new: float32 [8, 4, 1573568], P('rep', 'shard')
- first_moments_new: float32 [8, 4, 1573568], P('rep', 'shard')
- second_moments_new: float32 [8, 4, 1573568], P('rep', 'shard')
Inputs may be any that keep to these rules, and one draw needn't show every extreme that they name: `qkv_weight_state`: entry 0 along dimension 0 is the weight, entries 1 and 2 its first and second moment estimates; second moments are positive. `qkv_bias_state`: entry 0 is the bias, entries 1 and 2 its moment estimates; second moments are positive. `dense_weight_state`: entry 0 is the weight, entries 1 and 2 its moment estimates; second moments are positive. `up_weight_state`: entry 0 is the weight, entries 1 and 2 its moment estimates; second moments are positive. `up_bias_state`: entry 0 is the bias, entries 1 and 2 its moment estimates; second moments are positive. `down_weight_state`: entry 0 is the weight, entries 1 and 2 its moment estimates; second moments are positive. `vector_state`: entry 0 holds the vectors, entries 1 and 2 their moment estimates; the gains are positive, second moments are positive.
All inputs are finite; a program needn't handle non-finite values.
Results may differ from a plain program's by a relative error of at most 0.012.
Values may be sent and summed in bfloat16 or wider, within the bound.
A program may use at most 320 MiB of HBM per device.

v0:
```python
from functools import partial
import math

import jax
import jax.numpy as jnp
from jax import lax
from jax.sharding import PartitionSpec as P

D = 2048
HD = 64
ROT = 32
FF = 8192
STEP = 5


learn_rate = 0.02
beta_one = 0.9
beta_two = 0.95
adam_eps = 1e-08
weight_decay = 0.1
norm_eps = 1e-05
big_negative = -1e30


def layer_norm(x, norm_gain, norm_shift):
    center = x - jnp.mean(x, axis=-1, keepdims=True)
    variance = jnp.mean(center * center, axis=-1, keepdims=True)
    return center * lax.rsqrt(variance + norm_eps) * norm_gain + norm_shift


def gelu_tanh(v):
    return 0.5 * v * (1.0 + jnp.tanh(0.7978845608028654 * (v + 0.044715 * v * v * v)))


def rotary(x, positions):
    half_rot = ROT // 2
    frequency = jnp.exp(jnp.arange(half_rot, dtype=jnp.float32) * (-2.0 * math.log(10000.0) / ROT))
    angles = positions.astype(jnp.float32)[:, None] * frequency[None, :]
    cosine = jnp.cos(angles)[:, None, :]
    sine_val = jnp.sin(angles)[:, None, :]
    lower_part = x[..., :half_rot]
    upper_part = x[..., half_rot:ROT]
    return jnp.concatenate(
        [
            lower_part * cosine - upper_part * sine_val,
            upper_part * cosine + lower_part * sine_val,
            x[..., ROT:],
        ],
        axis=-1,
    )


def adam_update(state, grad):
    moment_one = beta_one * state[1] + (1.0 - beta_one) * grad
    moment_two = beta_two * state[2] + (1.0 - beta_two) * grad * grad
    corrected = moment_one / (1.0 - beta_one**STEP)
    divisor = jnp.sqrt(moment_two / (1.0 - beta_two**STEP)) + adam_eps
    weight = state[0] - learn_rate * (corrected / divisor + weight_decay * state[0])
    return jnp.stack([weight, moment_one, moment_two])


def owner_entries(new_states, entry):
    return jnp.concatenate(
        [state_new[entry].reshape(-1) for state_new in new_states], axis=0
    ).reshape(1, 1, -1)


def block_mask(q_pos, q_seg, k_pos, k_seg):
    return (k_pos[None, :] <= q_pos[:, None]) & (k_seg[None, :] == q_seg[:, None])


def attend_keys(kv_all, seg_all, queries, q_pos, q_seg):
    key_count = kv_all.shape[0]
    width = kv_all.shape[1] // 2
    heads_here = queries.shape[1]
    query_rows = queries.shape[0]
    block_rows = math.gcd(key_count, 512)
    block_count = key_count // block_rows
    kv_blocks = kv_all.reshape(block_count, block_rows, 2 * width)
    seg_blocks = seg_all.reshape(block_count, block_rows)
    score_scale = 1.0 / math.sqrt(HD)

    def attend_step_block(carry, block_items):
        kv_rows, seg_rows, block_index = block_items
        row_max, totals, accumulated = carry
        key_rows = kv_rows[:, :width].reshape(block_rows, heads_here, HD)
        value_rows = kv_rows[:, width:].reshape(block_rows, heads_here, HD)
        k_pos = block_index * block_rows + jnp.arange(block_rows, dtype=jnp.int32)
        allowed = block_mask(q_pos, q_seg, k_pos, seg_rows)
        scores = (
            jnp.einsum("qhd,khd->hqk", queries, key_rows, preferred_element_type=jnp.float32)
            * score_scale
        )
        scores = jnp.where(allowed[None], scores, big_negative)
        new_max = jnp.maximum(row_max, jnp.max(scores, axis=-1))
        probabilities = jnp.where(allowed[None], jnp.exp(scores - new_max[..., None]), 0.0)
        factor = jnp.exp(row_max - new_max)
        totals = totals * factor + jnp.sum(probabilities, axis=-1)
        accumulated = accumulated * factor[..., None] + jnp.einsum(
            "hqk,khd->hqd",
            probabilities.astype(jnp.bfloat16),
            value_rows,
            preferred_element_type=jnp.float32,
        )
        return ((new_max, totals, accumulated), None)

    start_state = (
        jnp.full((heads_here, query_rows), big_negative, jnp.float32),
        jnp.zeros((heads_here, query_rows), jnp.float32),
        jnp.zeros((heads_here, query_rows, HD), jnp.float32),
    )
    running, unused = lax.scan(
        attend_step_block,
        start_state,
        (kv_blocks, seg_blocks, jnp.arange(block_count, dtype=jnp.int32)),
    )
    return running


def attention_grads(queries, kv_all, seg_all, q_pos, q_seg, grad_heads, delta_all, lse_all):
    key_count = kv_all.shape[0]
    width = kv_all.shape[1] // 2
    heads_here = queries.shape[1]
    query_rows = queries.shape[0]
    block_rows = math.gcd(key_count, 512)
    block_count = key_count // block_rows
    kv_blocks = kv_all.reshape(block_count, block_rows, 2 * width)
    seg_blocks = seg_all.reshape(block_count, block_rows)
    score_scale = 1.0 / math.sqrt(HD)

    def attention_step_block(query_grad, block_items):
        kv_rows, seg_rows, block_index = block_items
        key_rows = kv_rows[:, :width].reshape(block_rows, heads_here, HD)
        value_rows = kv_rows[:, width:].reshape(block_rows, heads_here, HD)
        k_pos = block_index * block_rows + jnp.arange(block_rows, dtype=jnp.int32)
        allowed = block_mask(q_pos, q_seg, k_pos, seg_rows)
        scores = (
            jnp.einsum("qhd,khd->hqk", queries, key_rows, preferred_element_type=jnp.float32)
            * score_scale
        )
        scores = jnp.where(allowed[None], scores, big_negative)
        probabilities = jnp.where(allowed[None], jnp.exp(scores - lse_all[..., None]), 0.0)
        value_grad = jnp.einsum(
            "hqk,qhd->khd",
            probabilities.astype(jnp.bfloat16),
            grad_heads,
            preferred_element_type=jnp.float32,
        )
        prob_grad = jnp.einsum(
            "qhd,khd->hqk", grad_heads, value_rows, preferred_element_type=jnp.float32
        )
        score_grad = (probabilities * (prob_grad - delta_all[..., None]) * score_scale).astype(
            jnp.bfloat16
        )
        query_grad = query_grad + jnp.einsum(
            "hqk,khd->hqd", score_grad, key_rows, preferred_element_type=jnp.float32
        )
        key_grad = jnp.einsum(
            "hqk,qhd->khd", score_grad, queries, preferred_element_type=jnp.float32
        )
        return (
            query_grad,
            jnp.concatenate(
                [key_grad.reshape(block_rows, width), value_grad.reshape(block_rows, width)], axis=1
            ),
        )

    query_grad, kv_grad_blocks = lax.scan(
        attention_step_block,
        jnp.zeros((heads_here, query_rows, HD), jnp.float32),
        (kv_blocks, seg_blocks, jnp.arange(block_count, dtype=jnp.int32)),
    )
    return (query_grad, kv_grad_blocks.reshape(key_count, 2 * width))


def gather_vectors(own_qkvb, own_upb, own_vec):
    return (
        lax.all_gather(own_qkvb, ("rep", "shard"), axis=0, tiled=True),
        lax.all_gather(own_upb, ("rep", "shard"), axis=0, tiled=True),
        lax.all_gather(own_vec, ("rep", "shard"), axis=0, tiled=True),
    )


def sum_vectors(qkvb_grad, upb_grad, vec_grad):
    return (
        lax.psum_scatter(qkvb_grad, ("rep", "shard"), scatter_dimension=0, tiled=True),
        lax.psum_scatter(upb_grad, ("rep", "shard"), scatter_dimension=0, tiled=True),
        lax.psum_scatter(vec_grad, ("rep", "shard"), scatter_dimension=0, tiled=True),
    )


def sum_positions(partial_rows):
    return lax.psum_scatter(partial_rows, "shard", scatter_dimension=0, tiled=True)


def attention_pass(norm_rows, qkv_w, qkv_b, positions, key_width):
    row_count = norm_rows.shape[0]
    heads_here = key_width // HD
    joined = jnp.dot(norm_rows, qkv_w, preferred_element_type=jnp.float32) + qkv_b
    q_pre = joined[:, :key_width].reshape(row_count, heads_here, HD)
    k_pre = joined[:, key_width : 2 * key_width].reshape(row_count, heads_here, HD)
    queries = rotary(q_pre, positions).astype(jnp.bfloat16)
    key_local = rotary(k_pre, positions).astype(jnp.bfloat16).reshape(row_count, key_width)
    value_local = joined[:, 2 * key_width :].astype(jnp.bfloat16)
    kv_local = jnp.concatenate([key_local, value_local], axis=1)
    return (q_pre, k_pre, queries, kv_local)


def finish_qkv_grad(q_pre, k_pre, positions, query_grad, kv_grad, key_width):
    row_count = q_pre.shape[0]
    heads_here = key_width // HD
    rotate_back = partial(rotary, positions=positions)
    query_pre = jax.vjp(rotate_back, q_pre)[1](query_grad.transpose(1, 0, 2))[0]
    key_pre = jax.vjp(rotate_back, k_pre)[1](
        kv_grad[:, :key_width].reshape(row_count, heads_here, HD)
    )[0]
    return jnp.concatenate(
        [
            query_pre.reshape(row_count, key_width),
            key_pre.reshape(row_count, key_width),
            kv_grad[:, key_width:],
        ],
        axis=1,
    )


def sliced_pass(norm_bf, q_seg, cotangent, own_mats, qkv_bb, up_bb):
    own_qkv, own_dense, own_up, own_down = own_mats
    inner_count = lax.axis_size("shard")
    outer_count = lax.axis_size("rep")
    stride = outer_count // inner_count
    place = lax.axis_index("shard")
    head_width = D // inner_count
    unit_width = FF // inner_count
    qkv_rows = own_qkv.shape[0]
    dense_rows = own_dense.shape[0]
    down_rows = own_down.shape[0]
    qkv_split = own_qkv.reshape(qkv_rows, 3, inner_count, head_width)
    up_split = own_up.reshape(qkv_rows, 1, inner_count, unit_width)
    qkv_cols, up_cols = (
        lax.all_to_all(qkv_split, "shard", split_axis=2, concat_axis=0, tiled=True),
        lax.all_to_all(up_split, "shard", split_axis=2, concat_axis=0, tiled=True),
    )
    qkv_rep, up_rep, dense_rep, down_rep = (
        lax.all_gather(qkv_cols, "rep", axis=0, tiled=True),
        lax.all_gather(up_cols, "rep", axis=0, tiled=True),
        lax.all_gather(own_dense[None], "rep", axis=0, tiled=True),
        lax.all_gather(own_down[None], "rep", axis=0, tiled=True),
    )
    dense_grid = dense_rep.reshape(inner_count, stride, 1, dense_rows, D)
    down_grid = down_rep.reshape(inner_count, stride, 1, down_rows, D)
    dense_moved, down_moved = (
        lax.all_to_all(dense_grid, "shard", split_axis=0, concat_axis=2, tiled=True),
        lax.all_to_all(down_grid, "shard", split_axis=0, concat_axis=2, tiled=True),
    )
    qkv_w = qkv_rep.reshape(D, 3 * head_width)
    up_w = up_rep.reshape(D, unit_width)
    dense_w = dense_moved.reshape(head_width, D)
    down_w = down_moved.reshape(unit_width, D)
    qkv_b = lax.dynamic_index_in_dim(
        qkv_bb.astype(jnp.float32).reshape(3, inner_count, head_width), place, 1, False
    ).reshape(3 * head_width)
    up_b = lax.dynamic_slice_in_dim(up_bb.astype(jnp.float32), place * unit_width, unit_width, 0)
    norm_seq, grad_seq, seg_seq = (
        lax.all_gather(norm_bf, "shard", axis=0, tiled=True),
        lax.all_gather(cotangent, "shard", axis=0, tiled=True),
        lax.all_gather(q_seg, "shard", axis=0, tiled=True),
    )
    seq_rows = norm_seq.shape[0]
    heads_here = head_width // HD
    positions = jnp.arange(seq_rows, dtype=jnp.int32)
    q_pre, k_pre, queries, kv_seq = attention_pass(norm_seq, qkv_w, qkv_b, positions, head_width)
    row_max, totals, accumulated = attend_keys(kv_seq, seg_seq, queries, positions, seg_seq)
    lse_all = row_max + jnp.log(totals)
    out_heads = (accumulated / totals[..., None]).transpose(1, 0, 2).astype(jnp.bfloat16)
    attn_bf = out_heads.reshape(seq_rows, head_width)
    pre_act = jnp.dot(norm_seq, up_w, preferred_element_type=jnp.float32) + up_b
    hidden = gelu_tanh(pre_act).astype(jnp.bfloat16)
    partial_out = jnp.dot(attn_bf, dense_w, preferred_element_type=jnp.float32) + jnp.dot(
        hidden, down_w, preferred_element_type=jnp.float32
    )
    mixed = sum_positions(partial_out)
    grad_down = jnp.dot(hidden.T, grad_seq, preferred_element_type=jnp.float32)
    grad_dense = jnp.dot(attn_bf.T, grad_seq, preferred_element_type=jnp.float32)
    grad_hidden = jnp.dot(grad_seq, down_w.T, preferred_element_type=jnp.float32)
    grad_pre = jax.vjp(gelu_tanh, pre_act)[1](grad_hidden)[0]
    grad_pre_bf = grad_pre.astype(jnp.bfloat16)
    grad_up = jnp.dot(norm_seq.T, grad_pre_bf, preferred_element_type=jnp.float32)
    upb_part = jnp.sum(grad_pre, axis=0)
    norm_part = jnp.dot(grad_pre_bf, up_w.T, preferred_element_type=jnp.float32)
    grad_heads = (
        jnp.dot(grad_seq, dense_w.T, preferred_element_type=jnp.float32)
        .astype(jnp.bfloat16)
        .reshape(seq_rows, heads_here, HD)
    )
    delta_all = jnp.sum(grad_heads.astype(jnp.float32) * out_heads.astype(jnp.float32), axis=-1).T
    query_grad, kv_grad = attention_grads(
        queries, kv_seq, seg_seq, positions, seg_seq, grad_heads, delta_all, lse_all
    )
    grad_joined = finish_qkv_grad(q_pre, k_pre, positions, query_grad, kv_grad, head_width)
    grad_joined_bf = grad_joined.astype(jnp.bfloat16)
    grad_qkv = jnp.dot(norm_seq.T, grad_joined_bf, preferred_element_type=jnp.float32)
    qkvb_part = jnp.sum(grad_joined, axis=0)
    norm_part = norm_part + jnp.dot(grad_joined_bf, qkv_w.T, preferred_element_type=jnp.float32)
    grad_norm = sum_positions(norm_part)
    dense_grid_grad = grad_dense.reshape(1, stride, inner_count, dense_rows, D)
    down_grid_grad = grad_down.reshape(1, stride, inner_count, down_rows, D)
    dense_back, down_back = (
        lax.all_to_all(dense_grid_grad, "shard", split_axis=2, concat_axis=0, tiled=True),
        lax.all_to_all(down_grid_grad, "shard", split_axis=2, concat_axis=0, tiled=True),
    )
    qkv_sum, up_sum, dense_sum, down_sum = (
        lax.psum_scatter(
            grad_qkv.reshape(D, 3, 1, head_width), "rep", scatter_dimension=0, tiled=True
        ),
        lax.psum_scatter(
            grad_up.reshape(D, 1, 1, unit_width), "rep", scatter_dimension=0, tiled=True
        ),
        lax.psum_scatter(
            dense_back.reshape(outer_count, dense_rows, D), "rep", scatter_dimension=0, tiled=True
        ),
        lax.psum_scatter(
            down_back.reshape(outer_count, down_rows, D), "rep", scatter_dimension=0, tiled=True
        ),
    )
    qkv_home, up_home = (
        lax.all_to_all(qkv_sum, "shard", split_axis=0, concat_axis=2, tiled=True),
        lax.all_to_all(up_sum, "shard", split_axis=0, concat_axis=2, tiled=True),
    )
    qkv_own = qkv_home.reshape(qkv_rows, 3 * D)
    up_own = up_home.reshape(qkv_rows, FF)
    dense_own = dense_sum.reshape(dense_rows, D)
    down_own = down_sum.reshape(down_rows, D)
    selector = (jnp.arange(inner_count, dtype=jnp.int32) == place).astype(jnp.float32)
    qkvb_grad = (selector[None, :, None] * qkvb_part.reshape(3, 1, head_width)).reshape(3 * D)
    upb_grad = (selector[:, None] * upb_part[None, :]).reshape(FF)
    return (mixed, grad_norm, (qkv_own, dense_own, up_own, down_own), qkvb_grad, upb_grad)


def body(
    hidden_in,
    segment_ids,
    out_grad,
    qkv_weight_state,
    qkv_bias_state,
    dense_weight_state,
    up_weight_state,
    up_bias_state,
    down_weight_state,
    vector_state,
):
    own_mats = (
        qkv_weight_state[0].astype(jnp.bfloat16),
        dense_weight_state[0].astype(jnp.bfloat16),
        up_weight_state[0].astype(jnp.bfloat16),
        down_weight_state[0].astype(jnp.bfloat16),
    )
    qkv_bb, up_bb, vec_bf = gather_vectors(
        qkv_bias_state[0].astype(jnp.bfloat16),
        up_bias_state[0].astype(jnp.bfloat16),
        vector_state[0].astype(jnp.bfloat16),
    )
    vec_all = vec_bf.astype(jnp.float32)
    norm_gain = vec_all[:, 0]
    norm_shift = vec_all[:, 1]
    dense_bias = vec_all[:, 2]
    down_bias = vec_all[:, 3]
    tokens = hidden_in[0]
    q_seg = segment_ids[0]
    cotangent = out_grad[0]
    x_full = tokens.astype(jnp.float32)
    normed = layer_norm(x_full, norm_gain, norm_shift)
    norm_bf = normed.astype(jnp.bfloat16)
    mixed, grad_norm, owned, qkvb_grad, upb_grad = sliced_pass(
        norm_bf, q_seg, cotangent, own_mats, qkv_bb, up_bb
    )
    qkv_own, dense_own, up_own, down_own = owned
    output = (x_full + (mixed + dense_bias + down_bias)).astype(jnp.bfloat16)
    grad_x, grad_gain, grad_shift = jax.vjp(layer_norm, x_full, norm_gain, norm_shift)[1](grad_norm)
    out_bias_grad = jnp.sum(cotangent.astype(jnp.float32), axis=0)
    grad_vec = jnp.stack([grad_gain, grad_shift, out_bias_grad, out_bias_grad], axis=1)
    input_grad = cotangent.astype(jnp.float32) + grad_x
    qkvb_own, upb_own, vec_own = sum_vectors(qkvb_grad, upb_grad, grad_vec)
    new_states = (
        adam_update(qkv_weight_state, qkv_own),
        adam_update(qkv_bias_state, qkvb_own),
        adam_update(dense_weight_state, dense_own),
        adam_update(up_weight_state, up_own),
        adam_update(up_bias_state, upb_own),
        adam_update(down_weight_state, down_own),
        adam_update(vector_state, vec_own),
    )
    return (
        output[None],
        input_grad[None],
        qkv_own,
        qkvb_own,
        dense_own,
        up_own,
        upb_own,
        down_own,
        vec_own,
        owner_entries(new_states, 0),
        owner_entries(new_states, 1),
        owner_entries(new_states, 2),
    )


def solution(mesh):
    in_specs = (
        P("rep", "shard", None),
        P("rep", "shard"),
        P("rep", "shard", None),
        P(None, ("rep", "shard"), None),
        P(None, ("rep", "shard")),
        P(None, ("rep", "shard"), None),
        P(None, ("rep", "shard"), None),
        P(None, ("rep", "shard")),
        P(None, ("rep", "shard"), None),
        P(None, ("rep", "shard"), None),
    )
    out_specs = (
        P("rep", "shard", None),
        P("rep", "shard", None),
        P(("rep", "shard"), None),
        P(("rep", "shard")),
        P(("rep", "shard"), None),
        P(("rep", "shard"), None),
        P(("rep", "shard")),
        P(("rep", "shard"), None),
        P(("rep", "shard"), None),
        P("rep", "shard", None),
        P("rep", "shard", None),
        P("rep", "shard", None),
    )
    return jax.shard_map(body, mesh=mesh, in_specs=in_specs, out_specs=out_specs, check_vma=False)
```

profile of v0, /device:TPU:0, one launch (start us, length us, event | category | flops | bytes accessed | tf_op | source)
XLA Modules:
  0.0 1787.0 jit_solution(18287050627774750297)
XLA Ops:
  14.8 26.3 %all_to_all.126 = bf16[64,3,4,512]{3,0,1,2:T(8,128)(2,1)S(1)} all-to-all(bf16[64,3,4,512]{3,0,1,2:T(8,128)(2,1)S(1)} %copy.135), channel_id=1, replica_groups=mesh['rep'=8,'shard'=4] {'shard'}, dimensions={2} | all-to-all | bytes 1572864 | tf_op jit(solution)/shard_map/all_to_all | solution.py:241
  42.8 65.9 %all-gather.2 = bf16[32,64,4]{1,2,0:T(4,128)(2,1)S(1)} all-gather(bf16[1,64,4]{1,2,0:T(4,128)(2,1)S(1)} %fusion.75), channel_id=1, replica_groups=mesh['rep'=8,'shard'=4] {'rep','shard'}, dimensions={0}, use_global_device_ids=true | all-gather | bytes 16896 | tf_op jit(solution)/shard_map/all_gather | solution.py:180
  115.4 51.2 %all_to_all.127 = bf16[64,1,4,2048]{3,0,1,2:T(8,128)(2,1)} all-to-all(bf16[64,1,4,2048]{3,0,1,2:T(8,128)(2,1)S(1)} %copy.144), channel_id=1, replica_groups=mesh['rep'=8,'shard'=4] {'shard'}, dimensions={2} | all-to-all | bytes 2097152 | tf_op jit(solution)/shard_map/all_to_all | solution.py:242
  166.6 50.4 %all_to_all.128 = bf16[4,2,1,64,2048]{4,3,1,2,0:T(8,128)(2,1)S(1)} all-to-all(bf16[4,2,1,64,2048]{4,3,1,2,0:T(8,128)(2,1)} %bitcast.324), channel_id=1, replica_groups=mesh['rep'=8,'shard'=4] {'shard'}, dimensions={0} | all-to-all | bytes 4194304 | tf_op jit(solution)/shard_map/all_to_all | solution.py:253
  217.0 5.8 all-to-all-start.3
  224.2 235.0 %all-reduce.6 = bf16[6144]{0:T(1024)(128)(2,1)S(1)} all-reduce(bf16[6144]{0:T(1024)(128)(2,1)S(1)} %dynamic-update-slice), channel_id=1, replica_groups=mesh['rep'=8,'shard'=4] {'rep','shard'}, use_global_device_ids=true, to_apply=%add.6 | all-reduce | flops 6144 | bytes 24576
  460.3 66.2 %all-gather.3 = bf16[32,1,256]{2,1,0:T(2,128)(2,1)S(1)} all-gather(bf16[1,1,256]{2,1,0:T(2,128)(2,1)S(1)} %reshape.449), channel_id=1, replica_groups=mesh['rep'=8,'shard'=4] {'rep','shard'}, dimensions={0}, use_global_device_ids=true | all-gather | bytes 16896 | tf_op jit(solution)/shard_map/all_gather | solution.py:179
  526.6 7.7 all-gather
  536.2 4.3 fusion.48
  540.5 8.8 copy.137
  549.3 6.3 convolution_add_fusion.1
  566.5 3.8 multiply_convert_fusion
  576.5 5.0 fusion.88
  581.6 10.5 fusion.2
  592.1 8.5 copy.146
  600.7 11.4 fusion.101
  613.3 9.5 fusion.19
  622.9 2.8 convolution_bitcast_fusion.1
  628.2 4.9 all-to-all-start.5
  633.1 9.9 fusion.86
  643.0 30.7 %copy.151 = f32[2048,3,1,512]{3,2,1,0:T(1,128)} copy(f32[2048,3,1,512]{0,3,1,2:T(8,128)} %bitcast.279) | data formatting | bytes 25165824 | tf_op jit(solution)/shard_map/reshape | solution.py:314
  673.8 113.5 %all-to-all-done.5 = f32[1,2,4,64,2048]{4,3,1,0,2:T(8,128)} async-done(((f32[1,2,4,64,2048]{4,3,1,0,2:T(8,128)}), f32[1,2,4,64,2048]{4,3,1,0,2:T(8,128)}, u32[]{:S(2)}, u32[]{:S(2)}) %all-to-all-start.5) | async-done | bytes 4194336 | tf_op jit(solution)/shard_map/all_to_all | solution.py:309
  787.4 10.1 convolution_bitcast_fusion
  799.1 7.0 fusion.27
  806.1 6.4 copy.157
  812.5 7.4 all-to-all-start.7
  819.9 9.3 fusion.91
  829.3 3.4 convolution_add_fusion
  838.7 411.2 %all-to-all-done.7 = f32[1,2,4,256,2048]{4,3,1,0,2:T(8,128)} async-done(((f32[1,2,4,256,2048]{4,3,1,0,2:T(8,128)}), f32[1,2,4,256,2048]{4,3,1,0,2:T(8,128)}, u32[]{:S(2)}, u32[]{:S(2)}) %all-to-all-start.7) | async-done | bytes 16777248 | tf_op jit(solution)/shard_map/all_to_all | solution.py:310
  1251.8 3.6 constant_dynamic-slice_fusion
  1255.4 4.0 all-to-all-start.4
  1259.4 2.9 multiply_bitcast_fusion.4
  1282.9 18.1 %all-to-all-done.4 = f32[256,3,1,512]{3,2,1,0:T(1,128)S(1)} async-done(((f32[256,3,1,512]{3,2,1,0:T(1,128)}), f32[256,3,1,512]{3,2,1,0:T(1,128)S(1)}, u32[]{:S(2)}, u32[]{:S(2)}) %all-to-all-start.4) | async-done | bytes 1572896 | tf_op jit(solution)/shard_map/all_to_all | solution.py:327
  1306.4 4.4 multiply_subtract_fusion.2
  1312.7 5.2 copy.155
  1318.0 4.6 all-to-all-start.6
  1325.4 72.0 %all-reduce.10 = (f32[6144]{0:T(1024)S(1)}, f32[8192]{0:T(1024)S(1)}) all-reduce(f32[6144]{0:T(1024)S(1)} %bitcast.340, f32[8192]{0:T(1024)S(1)} %bitcast.339), channel_id=7, replica_groups=mesh['rep'=8,'shard'=4] {'rep','shard'}, use_global_device_ids=true, to_apply=%region_11.12.clone | all-reduce | flops 14336 | bytes 114688
  1398.8 3.0 fusion.60
  1401.8 13.5 reduce-scatter.19.cloned.1.call-done
  1416.8 2.9 copy.192
  1423.8 110.2 %reduce-scatter.17.cloned.1.call-done = f32[1,256,2048]{2,1,0:T(8,128)} async-done(((f32[8,256,2048]{2,1,0:T(8,128)}), f32[1,256,2048]{2,1,0:T(8,128)}) %reduce-scatter.17.cloned.1.call-update) | async-done | bytes 2097168 | tf_op jit(solution)/shard_map/reduce_scatter | solution.py:322
  1536.9 8.1 multiply_subtract_fusion
  1545.0 55.1 %concatenate.26 = f32[1573568]{0:T(1024)} concatenate(f32[393216]{0:T(1024)} %get-tuple-element.97, f32[192]{0:T(256)S(1)} %get-tuple-element.93, f32[131072]{0:T(1024)S(1)} %copy-done.15, f32[524288]{0:T(1024)} %get-tuple-element.152, f32[256]{0:T(256)S(1)} %get-tuple-element.83, f32[524288]{0:T(1024)} %get-tuple-element.80, f32[256]{0:T(256)S(1)} %reshape_squeeze_stack.6), dimensions={0} | concatenate | bytes 12588544 | tf_op jit(solution)/shard_map/concatenate | solution.py:63
  1600.1 25.1 %reshape.437 = f32[1,1,1573568]{2,1,0:T(1,128)} reshape(f32[1573568]{0:T(1024)} %concatenate.26) | data formatting | bytes 12588544 | tf_op jit(solution)/shard_map/reshape | solution.py:65
  1625.2 55.1 %concatenate.27 = f32[1573568]{0:T(1024)} concatenate(f32[393216]{0:T(1024)} %get-tuple-element.98, f32[192]{0:T(256)S(1)} %get-tuple-element.94, f32[131072]{0:T(1024)S(1)} %copy-done.14, f32[524288]{0:T(1024)} %get-tuple-element.154, f32[256]{0:T(256)S(1)} %get-tuple-element.84, f32[524288]{0:T(1024)} %get-tuple-element.81, f32[256]{0:T(256)S(1)} %reshape_squeeze_stack.7), dimensions={0} | concatenate | bytes 12588544 | tf_op jit(solution)/shard_map/concatenate | solution.py:63
  1680.3 25.0 %reshape.438 = f32[1,1,1573568]{2,1,0:T(1,128)} reshape(f32[1573568]{0:T(1024)} %concatenate.27) | data formatting | bytes 12588544 | tf_op jit(solution)/shard_map/reshape | solution.py:65
  1705.3 50.0 %concatenate.28 = f32[1573568]{0:T(1024)} concatenate(f32[393216]{0:T(1024)} %get-tuple-element.99, f32[192]{0:T(256)S(1)} %get-tuple-element.95, f32[131072]{0:T(1024)S(1)} %get-tuple-element.92, f32[524288]{0:T(1024)} %get-tuple-element.153, f32[256]{0:T(256)S(1)} %get-tuple-element.85, f32[524288]{0:T(1024)S(1)} %get-tuple-element.82, f32[256]{0:T(256)S(1)} %reshape_squeeze_stack.8), dimensions={0} | concatenate | bytes 12588544 | tf_op jit(solution)/shard_map/concatenate | solution.py:63
  1755.2 25.0 %reshape.439 = f32[1,1,1573568]{2,1,0:T(1,128)} reshape(f32[1573568]{0:T(1024)} %concatenate.28) | data formatting | bytes 12588544 | tf_op jit(solution)/shard_map/reshape | solution.py:65
  (262 shorter events, 90.6 us)
Async XLA Ops:
  7.2 159.5 %all-gather.15.cloned.1.call-start = ((), (), s32[]{:S(2)}) async-start(), calls=%async_computation.16 | async-start | bytes 2359296 | tf_op jit(solution)/shard_map/all_gather | solution.py:247
  9.0 208.0 %all-gather.19.cloned.1.call-start = ((), (), s32[]{:S(2)}) async-start(), calls=%async_computation.18 | async-start | bytes 9437184 | tf_op jit(solution)/shard_map/all_gather | solution.py:248
  11.8 524.4 %all-gather.21.cloned.1.call-start = ((), (), s32[]{:S(2)}) async-start(), calls=%async_computation.24 | async-start | bytes 2621440 | tf_op jit(solution)/shard_map/all_gather | solution.py:266
  12.5 528.0 %all-gather.13.cloned.1.call-start = ((), (), s32[]{:S(2)}) async-start(), calls=%async_computation.15 | async-start | bytes 7077888 | tf_op jit(solution)/shard_map/all_gather | solution.py:245
  14.7 94.1 %copy-start = (bf16[1,128,2048]{2,1,0:T(8,128)(2,1)S(1)}, bf16[1,128,2048]{2,1,0:T(8,128)(2,1)}, u32[]{:S(2)}) copy-start(bf16[1,128,2048]{2,1,0:T(8,128)(2,1)} %param.10) | copy-start | bytes 1572868
  42.0 507.2 %all-gather.11.cloned.1.call-start = ((), (), s32[]{:S(2)}) async-start(), calls=%async_computation.14 | async-start | bytes 2621440 | tf_op jit(solution)/shard_map/all_gather | solution.py:265
  112.3 469.3 %all-gather.17.cloned.1.call-start = ((), (), s32[]{:S(2)}) async-start(), calls=%async_computation.17 | async-start | bytes 9437184 | tf_op jit(solution)/shard_map/all_gather | solution.py:246
  217.0 5.9 copy-start.39
  217.0 242.2 %copy-start.40 = (f32[3,256]{1,0:T(4,128)S(1)}, f32[3,256]{1,0:T(4,128)}, u32[]{:S(2)}) copy-start(f32[3,256]{1,0:T(4,128)} %param.17) | copy-start | bytes 9220
  217.0 309.6 %copy-start.41 = (s32[1,128]{1,0:T(1,128)S(1)}, s32[1,128]{1,0:T(1,128)}, u32[]{:S(2)}) copy-start(s32[1,128]{1,0:T(1,128)} %param.11) | copy-start | bytes 1540
  217.0 375.1 %all-to-all-start.3 = ((bf16[4,2,1,256,2048]{4,3,1,2,0:T(8,128)(2,1)}), bf16[4,2,1,256,2048]{4,3,1,2,0:T(8,128)(2,1)}, u32[]{:S(2)}, u32[]{:S(2)}) async-start(bf16[4,2,1,256,2048]{4,3,1,2,0:T(8,128)(2,1)} %bitcast.292), calls=%async_computation.3 | async-start | bytes 16777216 | tf_op jit(solution)/shard_map/all_to_all | solution.py:254
  222.8 611.0 %reduce-scatter.11.cloned.1.call-start = ((), (), s32[]{:S(2)}) async-start(), calls=%async_computation.20 | async-start | bytes 5242880 | tf_op jit(solution)/shard_map/reduce_scatter | solution.py:193
  572.8 3.7 slice-start.4
  573.1 60.0 %copy-start.9 = (f32[512,8,64]{0,2,1:T(8,128)}, f32[512,8,64]{0,2,1:T(8,128)S(1)}, u32[]{:S(2)}) copy-start(f32[512,8,64]{0,2,1:T(8,128)S(1)} %get-tuple-element.150) | copy-start | bytes 3145732
  573.1 60.0 %copy-start.11 = (f32[512,8,64]{0,2,1:T(8,128)}, f32[512,8,64]{0,2,1:T(8,128)S(1)}, u32[]{:S(2)}) copy-start(f32[512,8,64]{0,2,1:T(8,128)S(1)} %get-tuple-element.151) | copy-start | bytes 3145732
  573.1 3.5 slice-start.5
  592.1 8.5 copy-start.44
  600.7 12.7 copy-start.49
  628.2 159.1 %all-to-all-start.5 = ((f32[1,2,4,64,2048]{4,3,1,0,2:T(8,128)}), f32[1,2,4,64,2048]{4,3,1,0,2:T(8,128)}, u32[]{:S(2)}, u32[]{:S(2)}) async-start(f32[1,2,4,64,2048]{4,3,1,0,2:T(8,128)} %copy.154), calls=%async_computation.7 | async-start | bytes 8388608 | tf_op jit(solution)/shard_map/all_to_all | solution.py:309
  633.0 618.8 %all-reduce.13.cloned.1.call-start = ((), (), s32[]{:S(2)}) async-start(), calls=%async_computation.26 | async-start | bytes 25165824
  673.8 113.6 %copy-start.46 = (bf16[512,2048]{1,0:T(8,128)(2,1)S(1)}, bf16[512,2048]{1,0:T(8,128)(2,1)}, u32[]{:S(2)}) copy-start(bf16[512,2048]{1,0:T(8,128)(2,1)} %all-gather.11.cloned.1.call-done) | copy-start | bytes 6291460
  673.8 636.9 %reduce-scatter.13.cloned.1.call-start = ((), (), s32[]{:S(2)}) async-start(), calls=%async_computation.21 | async-start | bytes 4718592 | tf_op jit(solution)/shard_map/reduce_scatter | solution.py:319
  787.3 525.3 %reduce-scatter.15.cloned.1.call-start = ((), (), s32[]{:S(2)}) async-start(), calls=%async_computation.22 | async-start | bytes 18874368 | tf_op jit(solution)/shard_map/reduce_scatter | solution.py:316
  812.5 437.4 %all-to-all-start.7 = ((f32[1,2,4,256,2048]{4,3,1,0,2:T(8,128)}), f32[1,2,4,256,2048]{4,3,1,0,2:T(8,128)}, u32[]{:S(2)}, u32[]{:S(2)}) async-start(f32[1,2,4,256,2048]{4,3,1,0,2:T(8,128)} %copy.157), calls=%async_computation.11 | async-start | bytes 33554432 | tf_op jit(solution)/shard_map/all_to_all | solution.py:310
  819.9 9.4 copy-start.5
  819.9 578.9 %reduce-scatter.9.cloned.1.call-start = ((), (), s32[]{:S(2)}) async-start(), calls=%async_computation.19 | async-start | bytes 5242880 | tf_op jit(solution)/shard_map/reduce_scatter | solution.py:193
  832.7 582.6 %reduce-scatter.19.cloned.1.call-start = ((), (), s32[]{:S(2)}) async-start(), calls=%async_computation.25 | async-start | bytes 1081344
  838.7 695.4 %reduce-scatter.17.cloned.1.call-start = ((), (), s32[]{:S(2)}) async-start(), calls=%async_computation.23 | async-start | bytes 18874368 | tf_op jit(solution)/shard_map/reduce_scatter | solution.py:322
  1255.4 45.6 %all-to-all-start.4 = ((f32[256,3,1,512]{3,2,1,0:T(1,128)}), f32[256,3,1,512]{3,2,1,0:T(1,128)S(1)}, u32[]{:S(2)}, u32[]{:S(2)}) async-start(f32[256,3,1,512]{3,2,1,0:T(1,128)} %constant_dynamic-slice_fusion), calls=%async_computation.6 | async-start | bytes 3145728 | tf_op jit(solution)/shard_map/all_to_all | solution.py:327
  1262.3 7.3 slice-start
  1265.2 4.4 slice-start.1
  1269.6 6.2 slice-start.2
  1270.7 5.1 slice-start.3
  1317.9 4.7 copy-start.16
  1317.9 79.6 %copy-start.31 = (f32[1,192]{1,0:T(1,128)S(1)}, f32[1,192]{1,0:T(1,128)}, u32[]{:S(2)}) copy-start(f32[1,192]{1,0:T(1,128)} %get-tuple-element.139) | copy-start | bytes 2308
  1317.9 79.6 %copy-start.33 = (f32[1,192]{1,0:T(1,128)S(1)}, f32[1,192]{1,0:T(1,128)}, u32[]{:S(2)}) copy-start(f32[1,192]{1,0:T(1,128)} %copy-done.32) | copy-start | bytes 2308
  1317.9 79.6 %copy-start.34 = (f32[1,192]{1,0:T(1,128)S(1)}, f32[1,192]{1,0:T(1,128)}, u32[]{:S(2)}) copy-start(f32[1,192]{1,0:T(1,128)} %get-tuple-element.141) | copy-start | bytes 2308
  1317.9 80.2 %copy-start.35 = (f32[1,256]{1,0:T(1,128)S(1)}, f32[1,256]{1,0:T(1,128)}, u32[]{:S(2)}) copy-start(f32[1,256]{1,0:T(1,128)} %get-tuple-element.136) | copy-start | bytes 3076
  1317.9 80.2 %copy-start.37 = (f32[1,256]{1,0:T(1,128)S(1)}, f32[1,256]{1,0:T(1,128)}, u32[]{:S(2)}) copy-start(f32[1,256]{1,0:T(1,128)} %copy-done.36) | copy-start | bytes 3076
  1317.9 80.2 %copy-start.38 = (f32[1,256]{1,0:T(1,128)S(1)}, f32[1,256]{1,0:T(1,128)}, u32[]{:S(2)}) copy-start(f32[1,256]{1,0:T(1,128)} %get-tuple-element.138) | copy-start | bytes 3076
  1317.9 80.9 %copy-start.2 = (f32[128,2048]{1,0:T(8,128)S(1)}, f32[128,2048]{1,0:T(8,128)}, u32[]{:S(2)}) copy-start(f32[128,2048]{1,0:T(8,128)} %reduce-scatter.11.cloned.1.call-done) | copy-start | bytes 3145732
  1317.9 80.9 %copy-start.23 = (f32[2048,1]{0,1:T(1,128)S(1)}, f32[2048,1]{0,1:T(1,128)}, u32[]{:S(2)}) copy-start(f32[2048,1]{0,1:T(1,128)} %get-tuple-element.130) | copy-start | bytes 24580
  1318.0 80.9 %copy-start.24 = (f32[2048,1]{0,1:T(1,128)S(1)}, f32[2048,1]{0,1:T(1,128)}, u32[]{:S(2)}) copy-start(f32[2048,1]{0,1:T(1,128)} %get-tuple-element.131) | copy-start | bytes 24580
  1318.0 98.8 %all-to-all-start.6 = ((f32[256,1,1,2048]{3,2,1,0:T(1,128)}), f32[256,1,1,2048]{3,2,1,0:T(1,128)}, u32[]{:S(2)}, u32[]{:S(2)}) async-start(f32[256,1,1,2048]{3,2,1,0:T(1,128)} %copy.155), calls=%async_computation.10 | async-start | bytes 4194304 | tf_op jit(solution)/shard_map/all_to_all | solution.py:328
  1325.3 90.8 %copy-start.27 = (f32[3,64,4]{1,2,0:T(4,128)S(1)}, f32[3,64,4]{1,2,0:T(4,128)}, u32[]{:S(2)}) copy-start(f32[3,64,4]{1,2,0:T(4,128)} %param.19) | copy-start | bytes 9220
  1416.1 6.1 copy-start.28
  1536.9 8.1 copy-start.15
  1600.1 25.1 %copy-start.14 = (f32[131072]{0:T(1024)S(1)}, f32[131072]{0:T(1024)}, u32[]{:S(2)}) copy-start(f32[131072]{0:T(1024)} %get-tuple-element.91) | copy-start | bytes 1572868
  (27 other events, 47.2 us)
Sparse Core Ops, SparseCore 0:
  10.4 30.4 all-gather.14
  43.4 54.3 all-gather.18
  99.4 68.1 all-gather.20
  169.9 44.0 all-gather.12
  216.0 105.7 all-gather.10
  323.5 52.8 all-gather.16
  623.0 137.4 reduce-scatter.10
  764.0 192.7 all-reduce.12
  960.7 51.2 reduce-scatter.12
  1015.5 116.1 reduce-scatter.14
  1134.5 111.5 reduce-scatter.8
  1248.2 167.0 reduce-scatter.18
  1419.5 114.5 reduce-scatter.16
where the time goes:
time: 1800 us; the launch traced here: 1790 us
  waiting for transfers between devices  667 us (37%)
  blocking collectives  575 us (32%)
  local copies, waits for them, and re-layouts  366 us (20%)
  matrix products  102 us (6%)
  other arithmetic  34.1 us (2%)
  starting transfers between devices  27.1 us (2%)
    all_to_all x1, waiting for transfers between devices, sliced_pass(): lax.all_to_all(down_grid_grad, 'shard', split_axis=2, concat_axis=0, tile...  411 us
    unnamed x2, blocking collectives  307 us
    concatenate x3, local copies, waits for them, and re-layouts, owner_entries(): jnp.concatenate([state_new[entry].reshape(-1) for state_new in new_states...  160 us
    all_to_all x1, waiting for transfers between devices, sliced_pass(): lax.all_to_all(dense_grid_grad, 'shard', split_axis=2, concat_axis=0, til...  113 us
    reduce_scatter x1, waiting for transfers between devices, sliced_pass(): lax.psum_scatter(down_back.reshape(outer_count, down_rows, D), 'rep', sca...  110 us
    reshape x3, local copies, waits for them, and re-layouts, owner_entries(): return jnp.concatenate([state_new[entry].reshape(-1) for state_new in new...  75.1 us
    all_gather x1, blocking collectives, gather_vectors(): lax.all_gather(own_upb, ('rep', 'shard'), axis=0, tiled=True)  66.2 us
    all_gather x1, blocking collectives, gather_vectors(): lax.all_gather(own_vec, ('rep', 'shard'), axis=0, tiled=True)  65.9 us
  transfers between devices with their start and end apart: 18, of which 5 were waited for; matrix products, arithmetic and copies ran while one was open for 12% of the time, Pallas kernels for 0%

commit v1 on v0

--- a/solution.py
+++ b/solution.py
@@ -4,6 +4,9 @@
 import jax
 import jax.numpy as jnp
 from jax import lax
+from jax.experimental import pallas as pl
+from jax.experimental.pallas import tpu as pltpu
+from jax.sharding import Mesh
 from jax.sharding import PartitionSpec as P
 
 D = 2048
@@ -406,6 +409,955 @@
     )
 
 
+def whole_heads(mesh):
+    owners = mesh.shape["rep"] * mesh.shape["shard"]
+    return D % owners == 0 and D // owners == HD and mesh.shape["rep"] % 2 == 0
+
+
+def rotation_tables(seq_rows):
+    half_rot = ROT // 2
+    lane = jnp.arange(2 * HD, dtype=jnp.int32) % HD
+    frequency = jnp.exp((lane % half_rot).astype(jnp.float32) * (-2.0 * math.log(10000.0) / ROT))
+    angles = jnp.arange(seq_rows, dtype=jnp.int32).astype(jnp.float32)[:, None] * frequency[None, :]
+    sine = jnp.sin(angles)
+    cosine = jnp.where(lane[None, :] < ROT, jnp.cos(angles), 1.0)
+    low = jnp.where(lane[None, :] < half_rot, -sine, 0.0)
+    high = jnp.where((lane[None, :] >= half_rot) & (lane[None, :] < ROT), sine, 0.0)
+    return cosine, low, high
+
+
+def attention_kernel(
+    fu_ref, do_ref, du_ref, seg_col_ref, seg_row_ref, cos_ref, low_ref, high_ref, o_ref, dcat_ref, sums_ref
+):
+    rows, width = do_ref.shape
+    scale = 1.0 / math.sqrt(HD)
+    row_id = lax.broadcasted_iota(jnp.int32, (rows, rows), 0)
+    col_id = lax.broadcasted_iota(jnp.int32, (rows, rows), 1)
+    allowed = (col_id <= row_id) & (seg_col_ref[...] == seg_row_ref[0])
+    cosine, low, high = cos_ref[...], low_ref[...], high_ref[...]
+    half = ROT // 2
+    lane = lax.broadcasted_iota(jnp.int32, (rows, 2 * HD), 1)
+
+    def rotate(u):
+        return (
+            u * cosine
+            + pltpu.roll(u, 2 * HD - half, 1) * low
+            + pltpu.roll(u, half, 1) * high
+        )
+
+    def rotate_back(u):
+        return (
+            u * cosine
+            - pltpu.roll(u, 2 * HD - half, 1) * low
+            - pltpu.roll(u, half, 1) * high
+        )
+
+    def dot(a, b, a_dim, b_dim):
+        return lax.dot_general(a, b, (((a_dim,), (b_dim,)), ((), ())), preferred_element_type=jnp.float32)
+
+    zero = jnp.zeros((), jnp.bfloat16)
+    for pair in range(width // (2 * HD)):
+        lanes = pl.ds(pair * 2 * HD, 2 * HD)
+        k_lanes = pl.ds(width + pair * 2 * HD, 2 * HD)
+        v_lanes = pl.ds(2 * width + pair * 2 * HD, 2 * HD)
+        q = rotate(fu_ref[:, lanes]).astype(jnp.bfloat16)
+        k = rotate(fu_ref[:, k_lanes]).astype(jnp.bfloat16)
+        v = fu_ref[:, v_lanes].astype(jnp.bfloat16)
+        do = do_ref[:, lanes]
+        o = dq = dk = dv = None
+        for head in range(2):
+            mine = (lane < HD) if head == 0 else (lane >= HD)
+            qh = jnp.where(mine, q, zero)
+            kh = jnp.where(mine, k, zero)
+            vh = jnp.where(mine, v, zero)
+            doh = jnp.where(mine, do, zero)
+            scores = jnp.where(allowed, dot(qh, k, 1, 1) * scale, big_negative)
+            row_max = jnp.max(scores, axis=1, keepdims=True)
+            probs = jnp.where(allowed, jnp.exp(scores - row_max), 0.0)
+            inverse = 1.0 / jnp.sum(probs, axis=1, keepdims=True)
+            oh = dot(probs.astype(jnp.bfloat16), vh, 1, 0) * inverse
+            delta = jnp.sum(
+                doh.astype(jnp.float32) * oh.astype(jnp.bfloat16).astype(jnp.float32), axis=1, keepdims=True
+            )
+            probs = probs * inverse
+            dvh = dot(probs.astype(jnp.bfloat16), doh, 0, 0)
+            ds = (probs * (dot(doh, v, 1, 1) - delta) * scale).astype(jnp.bfloat16)
+            dqh = dot(ds, kh, 1, 0)
+            dkh = dot(ds, qh, 0, 0)
+            if head == 0:
+                o, dq, dk, dv = oh, dqh, dkh, dvh
+            else:
+                o, dq, dk, dv = o + oh, dq + dqh, dk + dkh, dv + dvh
+        o_ref[:, lanes] = o.astype(jnp.bfloat16)
+        dq = rotate_back(dq)
+        dk = rotate_back(dk)
+        for part, place in ((dq, lanes), (dk, k_lanes), (dv, v_lanes)):
+            dcat_ref[:, place] = part.astype(jnp.bfloat16)
+            sums_ref[0, :, place] = jnp.sum(part, axis=0, keepdims=True)
+    dcat_ref[:, pl.ds(3 * width, du_ref.shape[1])] = du_ref[...]
+
+
+def attention(fu, do, du, segments):
+    count, rows = segments.shape
+    width = do.shape[1]
+    units = du.shape[1]
+    tables = rotation_tables(rows)
+    table_spec = pl.BlockSpec((rows, 2 * HD), lambda s: (0, 0))
+    o, dcat, sums = pl.pallas_call(
+        attention_kernel,
+        grid=(count,),
+        in_specs=[
+            pl.BlockSpec((rows, 3 * width), lambda s: (s, 0)),
+            pl.BlockSpec((rows, width), lambda s: (s, 0)),
+            pl.BlockSpec((rows, units), lambda s: (s, 0)),
+            pl.BlockSpec((rows, 1), lambda s: (s, 0)),
+            pl.BlockSpec((1, 1, rows), lambda s: (s, 0, 0)),
+            table_spec,
+            table_spec,
+            table_spec,
+        ],
+        out_specs=[
+            pl.BlockSpec((rows, width), lambda s: (s, 0)),
+            pl.BlockSpec((rows, 3 * width + units), lambda s: (s, 0)),
+            pl.BlockSpec((1, 1, 3 * width), lambda s: (s, 0, 0)),
+        ],
+        out_shape=[
+            jax.ShapeDtypeStruct((count * rows, width), jnp.bfloat16),
+            jax.ShapeDtypeStruct((count * rows, 3 * width + units), jnp.bfloat16),
+            jax.ShapeDtypeStruct((count, 1, 3 * width), jnp.float32),
+        ],
+        compiler_params=pltpu.CompilerParams(vmem_limit_bytes=56 << 20),
+        cost_estimate=pl.CostEstimate(
+            flops=count * (width // HD) * 10 * rows * rows * HD,
+            bytes_accessed=count * rows * (width * 20 + units * 4),
+            transcendentals=count * (width // HD) * rows * rows,
+        ),
+    )(fu, do, du, segments.reshape(count * rows, 1), segments.reshape(count, 1, rows), *tables)
+    return o, dcat, jnp.sum(sums, axis=(0, 1))
+
+
+def adam_values(weight, moment_one, moment_two, grad):
+    first = beta_one * moment_one + (1.0 - beta_one) * grad
+    second = beta_two * moment_two + (1.0 - beta_two) * grad * grad
+    corrected = first * (1.0 / (1.0 - beta_one**STEP))
+    divisor = jnp.sqrt(second * (1.0 / (1.0 - beta_two**STEP))) + adam_eps
+    return weight - learn_rate * (corrected / divisor + weight_decay * weight), first, second
+
+
+def owner_update_kernel(plan, small_plan, *refs):
+    count = len(plan)
+    small_ref = refs[2 * count]
+    outs = refs[2 * count + 1 :]
+    step = pl.program_id(0)
+    lane = lax.broadcasted_iota(jnp.int32, (8, 128), 1)
+    sub = lax.broadcasted_iota(jnp.int32, (8, 128), 0)
+    lane_row = lax.broadcasted_iota(jnp.int32, (1, 128), 1)
+
+    @pl.when(step == 0)
+    def small():
+        for source, row, low, high in small_plan:
+            for entry in range(3):
+                old = outs[entry][pl.ds(row, 1), :]
+                new = small_ref[entry, pl.ds(source, 1), :]
+                outs[entry][pl.ds(row, 1), :] = jnp.where((lane_row >= low) & (lane_row < high), new, old)
+
+    for index, (rows, tiles, start, shifted) in enumerate(plan):
+        state, grad = refs[2 * index], refs[2 * index + 1]
+        for group in range(rows // 8):
+            place = pl.ds(group * 8, 8)
+            base = start + (step * (rows // 8) + group) * (8 * tiles)
+
+            def values(column, state=state, grad=grad, place=place):
+                lanes = pl.ds(pl.multiple_of(column * 128, 128), 128)
+                return adam_values(
+                    state[0, place, lanes], state[1, place, lanes], state[2, place, lanes], grad[place, lanes]
+                )
+
+            if not shifted:
+
+                def plain(column, carry, base=base, tiles=tiles, values=values):
+                    for out, value in zip(outs, values(column)):
+                        out[pl.ds(base + column, 8, stride=tiles), :] = value
+                    return carry
+
+                lax.fori_loop(0, tiles, plain, 0, unroll=4)
+                continue
+
+            def turned(column, values=values):
+                return tuple(pltpu.roll(value, 64, 1) for value in values(column))
+
+            last = turned(tiles - 1)
+            before = tuple(
+                jnp.where(sub == 0, out[pl.ds(base, 1), :], pltpu.roll(value, 1, 0))
+                for out, value in zip(outs, last)
+            )
+
+            def moved(column, carry, base=base, tiles=tiles, turned=turned):
+                now = turned(column)
+                for out, old, new in zip(outs, carry, now):
+                    out[pl.ds(base + column, 8, stride=tiles), :] = jnp.where(lane < 64, old, new)
+                return now
+
+            lax.fori_loop(0, tiles, moved, before, unroll=4)
+            for out, value in zip(outs, last):
+                row = pl.ds(base + 8 * tiles, 1)
+                out[row, :] = jnp.where(lane_row < 64, value[7:8], out[row, :])
+
+
+def owner_update(states, grads, small_states, small_grads):
+    steps = 8
+    sizes = [state.shape[1] * state.shape[2] for state in states]
+    small_sizes = [grad.size for grad in small_grads]
+    order = [("m", 0), ("s", 0), ("m", 1), ("m", 2), ("s", 1), ("m", 3), ("s", 2)]
+    offset = 0
+    plan = [None] * 4
+    small_plan = []
+    pads = []
+    small_row = 0
+    for kind, index in order:
+        if kind == "m":
+            state = states[index]
+            rows = state.shape[1] // steps
+            plan[index] = (rows, state.shape[2] // 128, offset // 128, offset % 128 == 64)
+            offset += sizes[index]
+        else:
+            size = small_sizes[index]
+            front = offset % 128
+            total = -(-(front + size) // 128)
+            pads.append((front, total * 128 - front - size))
+            for extra in range(total):
+                low = front if extra == 0 else 0
+                high = min(128, front + size - extra * 128)
+                small_plan.append((small_row + extra, offset // 128 + extra, low, high))
+            small_row += total
+            offset += size
+    entries = offset
+    out_rows = -(-entries // 1024) * 8
+    small_new = [
+        adam_values(state[0].reshape(-1), state[1].reshape(-1), state[2].reshape(-1), grad.reshape(-1))
+        for state, grad in zip(small_states, small_grads)
+    ]
+    small = jnp.stack(
+        [
+            jnp.concatenate([jnp.pad(new[entry], pad) for new, pad in zip(small_new, pads)])
+            for entry in range(3)
+        ]
+    ).reshape(3, small_row, 128)
+    in_specs = []
+    operands = []
+    for state, grad, (rows, tiles, start, shifted) in zip(states, grads, plan):
+        in_specs.append(pl.BlockSpec((3, rows, tiles * 128), lambda s: (0, s, 0)))
+        in_specs.append(pl.BlockSpec((rows, tiles * 128), lambda s: (s, 0)))
+        operands += [state, grad]
+    in_specs.append(pl.BlockSpec((3, small_row, 128), lambda s: (0, 0, 0)))
+    outs = pl.pallas_call(
+        partial(owner_update_kernel, plan, small_plan),
+        grid=(steps,),
+        in_specs=in_specs,
+        out_specs=[pl.BlockSpec((out_rows, 128), lambda s: (0, 0), pipeline_mode=pl.Buffered(1))] * 3,
+        out_shape=[jax.ShapeDtypeStruct((out_rows, 128), jnp.float32)] * 3,
+        compiler_params=pltpu.CompilerParams(vmem_limit_bytes=56 << 20),
+        cost_estimate=pl.CostEstimate(
+            flops=20 * entries, bytes_accessed=28 * entries, transcendentals=2 * entries
+        ),
+    )(*operands, small)
+    return tuple(out.reshape(1, 1, out_rows * 128)[:, :, :entries] for out in outs)
+
+
+class Wires:
+    def __init__(self, send_sems):
+        self.send_sems, self.count, self.pending = send_sems, 0, []
+        self.plane, self.core, self.shard = (
+            lax.axis_index("plane"),
+            lax.axis_index("core"),
+            lax.axis_index("shard"),
+        )
+        self.shards = lax.axis_size("shard")
+        self.group = lax.axis_size("core") * self.shards
+        self.mine = self.core * self.shards + self.shard
+        self.first = (self.plane ^ 1, self.core, self.shard)
+        self.second = (self.plane ^ 2, self.core, self.shard)
+
+    def member(self, index):
+        return (self.plane, index // self.shards, index % self.shards)
+
+    def barrier(self):
+        barrier = pltpu.get_barrier_semaphore()
+        partners = [self.member(self.mine ^ mask) for mask in range(1, self.group)]
+        partners += [self.first, self.second]
+        for partner in partners:
+            pl.semaphore_signal(barrier, inc=1, device_id=partner, device_id_type=pl.DeviceIdType.MESH)
+        pl.semaphore_wait(barrier, len(partners))
+
+    def send(self, source, target, recv_sem, device, when=None):
+        copy = pltpu.make_async_remote_copy(
+            src_ref=source,
+            dst_ref=target,
+            send_sem=self.send_sems.at[self.count],
+            recv_sem=recv_sem,
+            device_id=device,
+            device_id_type=pl.DeviceIdType.MESH,
+        )
+        self.count += 1
+        self.pending.append((copy, when))
+        if when is None:
+            copy.start()
+        else:
+            pl.when(when)(copy.start)
+
+    def arrived(self, place, recv_sem, when=None):
+        copy = pltpu.make_async_remote_copy(
+            src_ref=place,
+            dst_ref=place,
+            send_sem=self.send_sems.at[0],
+            recv_sem=recv_sem,
+            device_id=self.first,
+            device_id_type=pl.DeviceIdType.MESH,
+        )
+        if when is None:
+            copy.wait_recv()
+        else:
+            pl.when(when)(copy.wait_recv)
+
+    def drain(self):
+        for copy, when in self.pending:
+            if when is None:
+                copy.wait_send()
+            else:
+                pl.when(when)(copy.wait_send)
+
+
+def gather_kernel(
+    pieces, dense, down, tokens, cotangent, vectors,
+    cat_out, dense_out, down_out, x_out, dy_out, vec_out,
+    send_sems, group_sem, first_sem, second_sem, far_sem, up_sem, low_sem, core_sem, local_sem,
+):
+    net = Wires(send_sems)
+    plane, core, shard, shards, group, mine = net.plane, net.core, net.shard, net.shards, net.group, net.mine
+    order = sorted(range(group), key=lambda mask: (mask % shards, mask // shards))
+    partner = (plane, 1 - core, shard)
+
+    def cat_unit(mask):
+        return lambda p: cat_out.at[p, mine ^ mask]
+
+    def vec_unit(mask):
+        return lambda p: vec_out.at[p, mine ^ mask]
+
+    units = []
+    down_rows = down.shape[0] // 4
+    for part in range(4):
+        rows = pl.ds(part * down_rows, down_rows)
+        units.append((down.at[rows], lambda p, rows=rows: down_out.at[p, rows]))
+    dense_rows = dense.shape[0] // 2
+    for part in range(2):
+        rows = pl.ds(part * dense_rows, dense_rows)
+        units.append((dense.at[rows], lambda p, rows=rows: dense_out.at[p, rows]))
+    own_units = list(range(len(units)))
+    cat_units, vec_units = {}, {}
+    for mask in order:
+        cat_units[mask] = len(units)
+        units.append((pieces.at[mine] if mask == 0 else None, cat_unit(mask)))
+        vec_units[mask] = len(units)
+        units.append((vectors if mask == 0 else None, vec_unit(mask)))
+
+    def spread(index):
+        source, place = units[index]
+        source = place(plane) if source is None else source
+        net.send(source, place(plane), first_sem.at[index], net.first)
+        net.send(source, place(plane), second_sem.at[index], net.second)
+
+    def hand_on(index):
+        place = units[index][1]
+        if relay_first[index]:
+            net.arrived(place(plane ^ 1), first_sem.at[index])
+            net.send(place(plane ^ 1), place(plane ^ 1), far_sem.at[index], net.second)
+        else:
+            net.arrived(place(plane ^ 2), second_sem.at[index])
+            net.send(place(plane ^ 2), place(plane ^ 2), far_sem.at[index], net.first)
+
+    relay_first = {}
+    for position, index in enumerate(own_units):
+        relay_first[index] = position % 2 == 0
+    for position, mask in enumerate(order):
+        relay_first[cat_units[mask]] = position % 2 == 0
+        relay_first[vec_units[mask]] = position % 2 == 1
+
+    net.barrier()
+
+    locals_ = [
+        (pieces.at[mine], cat_out.at[plane, mine]),
+        (dense, dense_out.at[plane]),
+        (down, down_out.at[plane]),
+        (tokens, x_out.at[mine]),
+        (cotangent, dy_out.at[mine]),
+        (vectors, vec_out.at[plane, mine]),
+    ]
+    copies = [
+        pltpu.make_async_copy(source, target, local_sem.at[index])
+        for index, (source, target) in enumerate(locals_)
+    ]
+    for mask in order[1:]:
+        target = net.member(mine ^ mask)
+        net.send(vectors, vec_out.at[plane, mine], group_sem.at[1, mask], target)
+        net.send(pieces.at[mine ^ mask], cat_out.at[plane, mine], group_sem.at[0, mask], target)
+    for index in own_units:
+        spread(index)
+    spread(cat_units[0])
+    spread(vec_units[0])
+    streams = ((tokens, x_out), (cotangent, dy_out))
+
+    def block(stream, origin):
+        return streams[stream][1].at[core * shards + origin]
+
+    def to_core(stream, source, origin, slot, when=None):
+        net.send(source, block(stream, origin), core_sem.at[stream, slot], partner, when)
+
+    def hop(stream, distance):
+        own = distance == 1
+        for upward, sem in ((True, up_sem), (False, low_sem)):
+            origin = shard - (distance - 1) if upward else shard + (distance - 1)
+            there = shard + 1 if upward else shard - 1
+            held = (origin >= 0) if upward else (origin < shards)
+            inside = (there < shards) if upward else (there >= 0)
+            near = jnp.clip(origin, 0, shards - 1)
+            source = streams[stream][0] if own else block(stream, near)
+            net.send(
+                source,
+                block(stream, near),
+                sem.at[stream, distance],
+                (plane, core, jnp.clip(there, 0, shards - 1)),
+                inside & held,
+            )
+
+    def hop_arrived(stream, distance):
+        for upward, sem in ((True, up_sem), (False, low_sem)):
+            origin = shard - distance if upward else shard + distance
+            held = (origin >= 0) if upward else (origin < shards)
+            near = jnp.clip(origin, 0, shards - 1)
+            net.arrived(block(stream, near), sem.at[stream, distance], held)
+            slot = distance if upward else shards + distance
+            to_core(stream, block(stream, near), near, slot, held)
+
+    for stream in range(2):
+        hop(stream, 1)
+    for stream in range(2):
+        to_core(stream, streams[stream][0], shard, 0)
+    for copy in copies:
+        copy.start()
+
+    for position, mask in enumerate(order[1:]):
+        net.arrived(vec_out.at[plane, mine ^ mask], group_sem.at[1, mask])
+        spread(vec_units[mask])
+        net.arrived(cat_out.at[plane, mine ^ mask], group_sem.at[0, mask])
+        spread(cat_units[mask])
+        if position == 2:
+            for index in own_units:
+                hand_on(index)
+    hand_on(cat_units[0])
+    hand_on(vec_units[0])
+    for distance in range(1, shards):
+        for stream in range(2):
+            hop_arrived(stream, distance)
+            if distance + 1 < shards:
+                hop(stream, distance + 1)
+        for mask in order[1 + (distance - 1) * 3 : 1 + distance * 3]:
+            hand_on(vec_units[mask])
+            hand_on(cat_units[mask])
+
+    for index, (source, place) in enumerate(units):
+        if relay_first[index]:
+            net.arrived(place(plane ^ 2), second_sem.at[index])
+        else:
+            net.arrived(place(plane ^ 1), first_sem.at[index])
+        net.arrived(place(plane ^ 3), far_sem.at[index])
+    for stream in range(2):
+        other = streams[stream][1]
+        for slot in range(2 * shards):
+            if slot == shards:
+                continue
+            origin = shard - slot if slot < shards else shard + (slot - shards)
+            held = None if slot == 0 else ((origin >= 0) & (origin < shards))
+            near = jnp.clip(origin, 0, shards - 1)
+            net.arrived(other.at[(1 - core) * shards + near], core_sem.at[stream, slot], held)
+    for copy in copies:
+        copy.wait()
+    net.drain()
+
+
+def gather_wires(pieces, dense, down, tokens, cotangent, vectors):
+    group, shards = lax.axis_size("core") * lax.axis_size("shard"), lax.axis_size("shard")
+    planes = lax.axis_size("plane")
+    units = 6 + 2 * group
+    vmem = pl.BlockSpec(memory_space=pltpu.VMEM)
+    hbm = pl.BlockSpec(memory_space=pl.ANY)
+
+    def out(lead, value):
+        return jax.ShapeDtypeStruct(lead + value.shape, value.dtype)
+
+    dma = pltpu.SemaphoreType.DMA
+    return pl.pallas_call(
+        gather_kernel,
+        in_specs=[vmem] * 6,
+        out_specs=[hbm] * 6,
+        out_shape=[
+            out((planes,), pieces),
+            out((planes,), dense),
+            out((planes,), down),
+            out((group,), tokens),
+            out((group,), cotangent),
+            out((planes, group), vectors),
+        ],
+        scratch_shapes=[
+            dma((2 * (group - 1) + 3 * units + 2 * 2 * (shards - 1) + 2 * (2 * shards - 1),)),
+            dma((2, group)),
+            dma((units,)),
+            dma((units,)),
+            dma((units,)),
+            dma((2, shards)),
+            dma((2, shards)),
+            dma((2, 2 * shards)),
+            dma((6,)),
+        ],
+        compiler_params=pltpu.CompilerParams(
+            collective_id=0, has_side_effects=True, vmem_limit_bytes=24 << 20
+        ),
+    )(pieces, dense, down, tokens, cotangent, vectors)
+
+
+def add_rows(target, *sources):
+    step = 16
+    rows = target.shape[0]
+
+    def body(index, carry):
+        place = pl.ds(pl.multiple_of(index * step, step), step)
+        total = sources[0][place, :].astype(jnp.float32)
+        for source in sources[1:]:
+            total = total + source[place, :].astype(jnp.float32)
+        target[place, :] = total.astype(target.dtype)
+        return carry
+
+    lax.fori_loop(0, rows // step, body, 0)
+
+
+def reduce_kernel(
+    cat, dense, down, out_part, norm_part, sums,
+    cat_out, dense_out, down_out, mixed_out, norm_out, sums_out,
+    cat_buf, down_buf, dense_buf, token_buf, sum_buf,
+    send_sems, near_sem, pass_sem, group_sem, core_sem, line_sem, sum_sem, local_sem,
+):
+    PASS_IN, PASS_OWN, PASS_OUT, KEEP_IN, KEEP_OWN, LAST_IN = range(6)
+    net = Wires(send_sems)
+    plane, core, shard, shards, group, mine = net.plane, net.core, net.shard, net.shards, net.group, net.mine
+    partner = (plane, 1 - core, shard)
+    order = sorted(range(group), key=lambda mask: (mask % shards, mask // shards), reverse=True)
+
+    units = []
+    for mask in order:
+        units.append((lambda p, mask=mask: cat.at[p, mine ^ mask], cat_buf, mask))
+    down_rows = down.shape[1] // 4
+    for part in range(4):
+        rows = pl.ds(part * down_rows, down_rows)
+        units.append((lambda p, rows=rows: down.at[p, rows], down_buf, part))
+    dense_rows = dense.shape[1] // 2
+    for part in range(2):
+        rows = pl.ds(part * dense_rows, dense_rows)
+        units.append((lambda p, rows=rows: dense.at[p, rows], dense_buf, part))
+
+    def ways(index):
+        if index % 2 == 0:
+            return net.first, net.second, plane ^ 1, plane ^ 2
+        return net.second, net.first, plane ^ 2, plane ^ 1
+
+    loads = {}
+
+    def load(key, source, target):
+        loads[key] = pltpu.make_async_copy(source, target, local_sem.at[len(loads)])
+        loads[key].start()
+
+    streams = (out_part, norm_part)
+    finals = (mixed_out, norm_out)
+    TOKEN_IN, TOKEN_OWN, TOKEN_SUM, TOKEN_LINE = range(4)
+
+    for index, (part, buffers, slot) in enumerate(units):
+        near, far, near_plane, far_plane = ways(index)
+        load(("pass", index), part(far_plane), buffers.at[PASS_OWN, slot])
+    for stream in range(2):
+        for mask in range(shards):
+            load(
+                ("token", stream, mask),
+                streams[stream].at[core * shards + (shard ^ mask)],
+                token_buf.at[TOKEN_OWN, stream, mask],
+            )
+    for index, (part, buffers, slot) in enumerate(units):
+        load(("keep", index), part(plane), buffers.at[KEEP_OWN, slot])
+
+    net.barrier()
+
+    net.send(sums, sum_buf.at[0], sum_sem.at[0], net.first)
+    for stream in range(2):
+        for mask in reversed(range(shards)):
+            net.send(
+                streams[stream].at[(1 - core) * shards + (shard ^ mask)],
+                token_buf.at[TOKEN_IN, stream, mask],
+                core_sem.at[stream, mask],
+                partner,
+            )
+    for index, (part, buffers, slot) in enumerate(units):
+        near, far, near_plane, far_plane = ways(index)
+        net.send(part(plane ^ 3), buffers.at[PASS_IN, slot], pass_sem.at[0, index], near)
+        net.send(part(near_plane), buffers.at[KEEP_IN, slot], near_sem.at[index], near)
+
+    def token_sum(stream, mask):
+        net.arrived(token_buf.at[TOKEN_IN, stream, mask], core_sem.at[stream, mask])
+        loads["token", stream, mask].wait()
+        add_rows(
+            token_buf.at[TOKEN_SUM, stream, mask],
+            token_buf.at[TOKEN_IN, stream, mask],
+            token_buf.at[TOKEN_OWN, stream, mask],
+        )
+        if mask:
+            net.send(
+                token_buf.at[TOKEN_SUM, stream, mask],
+                token_buf.at[TOKEN_LINE, stream, mask],
+                line_sem.at[stream, mask],
+                (plane, core, shard ^ mask),
+            )
+
+    def pass_on(index):
+        part, buffers, slot = units[index]
+        near, far, near_plane, far_plane = ways(index)
+        net.arrived(buffers.at[PASS_IN, slot], pass_sem.at[0, index])
+        loads["pass", index].wait()
+        add_rows(buffers.at[PASS_OUT, slot], buffers.at[PASS_IN, slot], buffers.at[PASS_OWN, slot])
+        net.send(buffers.at[PASS_OUT, slot], buffers.at[LAST_IN, slot], pass_sem.at[1, index], far)
+
+    def finish(index):
+        part, buffers, slot = units[index]
+        net.arrived(buffers.at[KEEP_IN, slot], near_sem.at[index])
+        loads["keep", index].wait()
+        net.arrived(buffers.at[LAST_IN, slot], pass_sem.at[1, index])
+        values = (buffers.at[KEEP_IN, slot], buffers.at[KEEP_OWN, slot], buffers.at[LAST_IN, slot])
+        if index < group:
+            add_rows(buffers.at[KEEP_OWN, slot], *values)
+            if slot:
+                net.send(
+                    buffers.at[KEEP_OWN, slot],
+                    cat_out.at[mine],
+                    group_sem.at[0, slot],
+                    net.member(mine ^ slot),
+                )
+            else:
+                load("own", buffers.at[KEEP_OWN, slot], cat_out.at[mine])
+        elif index < group + 4:
+            add_rows(down_out.at[pl.ds(slot * down_rows, down_rows)], *values)
+        else:
+            add_rows(dense_out.at[pl.ds(slot * dense_rows, dense_rows)], *values)
+
+    net.arrived(sum_buf.at[0], sum_sem.at[0])
+    sum_buf[1] = sums[...] + sum_buf[0]
+    net.send(sum_buf.at[1], sum_buf.at[2], sum_sem.at[1], net.second)
+    for mask in reversed(range(shards)):
+        token_sum(0, mask)
+    net.arrived(sum_buf.at[2], sum_sem.at[1])
+    sum_buf[3] = sum_buf[1] + sum_buf[2]
+    for mask in range(1, group):
+        net.send(sum_buf.at[3], sums_out.at[mine], group_sem.at[1, mask], net.member(mine ^ mask))
+    load("sums", sum_buf.at[3], sums_out.at[mine])
+    lag = 4
+    for index in range(len(units) + lag):
+        if index < len(units):
+            pass_on(index)
+        if index >= lag:
+            finish(index - lag)
+        if index == 1:
+            for mask in reversed(range(shards)):
+                token_sum(1, mask)
+    for stream in range(2):
+        for mask in range(1, shards):
+            net.arrived(token_buf.at[TOKEN_LINE, stream, mask], line_sem.at[stream, mask])
+        add_rows(
+            finals[stream],
+            token_buf.at[TOKEN_SUM, stream, 0],
+            *[token_buf.at[TOKEN_LINE, stream, mask] for mask in range(1, shards)],
+        )
+    for mask in range(1, group):
+        net.arrived(cat_out.at[mine ^ mask], group_sem.at[0, mask])
+        net.arrived(sums_out.at[mine ^ mask], group_sem.at[1, mask])
+    loads["own"].wait()
+    loads["sums"].wait()
+    net.drain()
+
+
+def reduce_wires(cat, dense, down, out_part, norm_part, sums):
+    shards = lax.axis_size("shard")
+    group = lax.axis_size("core") * shards
+    units = group + 6
+    vmem = pl.BlockSpec(memory_space=pltpu.VMEM)
+    hbm = pl.BlockSpec(memory_space=pl.ANY)
+    dma = pltpu.SemaphoreType.DMA
+    tokens = out_part.shape[1:]
+    return pl.pallas_call(
+        reduce_kernel,
+        in_specs=[hbm] * 5 + [vmem],
+        out_specs=[hbm] + [vmem] * 4 + [hbm],
+        out_shape=[
+            jax.ShapeDtypeStruct(cat.shape[1:], cat.dtype),
+            jax.ShapeDtypeStruct(dense.shape[1:], jnp.float32),
+            jax.ShapeDtypeStruct(down.shape[1:], jnp.float32),
+            jax.ShapeDtypeStruct(tokens, jnp.float32),
+            jax.ShapeDtypeStruct(tokens, jnp.float32),
+            jax.ShapeDtypeStruct((group,) + sums.shape, sums.dtype),
+        ],
+        scratch_shapes=[
+            pltpu.VMEM((6, group) + cat.shape[2:], cat.dtype),
+            pltpu.VMEM((6, 4, down.shape[1] // 4, down.shape[2]), down.dtype),
+            pltpu.VMEM((6, 2, dense.shape[1] // 2, dense.shape[2]), dense.dtype),
+            pltpu.VMEM((4, 2, shards) + tokens, out_part.dtype),
+            pltpu.VMEM((4,) + sums.shape, sums.dtype),
+            dma((2 + 2 * shards + 2 * (shards - 1) + 3 * units + 2 * (group - 1),)),
+            dma((units,)),
+            dma((2, units)),
+            dma((2, group)),
+            dma((2, shards)),
+            dma((2, shards)),
+            dma((2,)),
+            dma((2 * units + 2 * shards + 2,)),
+        ],
+        compiler_params=pltpu.CompilerParams(
+            collective_id=1, has_side_effects=True, vmem_limit_bytes=58 << 20
+        ),
+    )(cat, dense, down, out_part, norm_part, sums)
+
+
+def fast_body(
+    hidden_in,
+    segment_ids,
+    out_grad,
+    qkv_weight_state,
+    qkv_bias_state,
+    dense_weight_state,
+    up_weight_state,
+    up_bias_state,
+    down_weight_state,
+    vector_state,
+):
+    planes, cores, shards = lax.axis_size("plane"), lax.axis_size("core"), lax.axis_size("shard")
+    plane, core, shard = lax.axis_index("plane"), lax.axis_index("core"), lax.axis_index("shard")
+    group = cores * shards
+    owner = (plane * cores + core) * shards + shard
+    owners = planes * group
+    model_rows = qkv_weight_state.shape[1]
+    unit_rows = down_weight_state.shape[1]
+    tokens_here = hidden_in.shape[1]
+    head_width = planes * HD
+    unit_width = planes * unit_rows
+    qkv_count, upb_count = qkv_bias_state.shape[1], up_bias_state.shape[1]
+
+    tokens, cotangent, q_seg = hidden_in[0], out_grad[0], segment_ids[0]
+    qkv_pieces = (
+        qkv_weight_state[0]
+        .astype(jnp.bfloat16)
+        .reshape(model_rows, 3, planes, cores, shards, HD)
+        .transpose(3, 4, 0, 1, 2, 5)
+        .reshape(group, model_rows, 3 * head_width)
+    )
+    up_pieces = (
+        up_weight_state[0]
+        .astype(jnp.bfloat16)
+        .reshape(model_rows, planes, cores, shards, unit_rows)
+        .transpose(2, 3, 0, 1, 4)
+        .reshape(group, model_rows, unit_width)
+    )
+    pieces = jnp.concatenate([qkv_pieces, up_pieces], axis=2)
+    dense_own = dense_weight_state[0].astype(jnp.bfloat16)
+    down_own = down_weight_state[0].astype(jnp.bfloat16)
+    vec_list = [
+        qkv_bias_state[0],
+        up_bias_state[0],
+        vector_state[0].T.reshape(-1),
+        q_seg.astype(jnp.float32),
+    ]
+    vec_sizes = [value.size for value in vec_list]
+    vec_rows = -(-sum(vec_sizes) // 1024) * 8
+    vec_own = jnp.pad(jnp.concatenate(vec_list), (0, vec_rows * 128 - sum(vec_sizes))).reshape(vec_rows, 128)
+
+    cat_w, dense_w, down_w, x_all, dy_all, vec_all = gather_wires(
+        pieces, dense_own, down_own, tokens, cotangent, vec_own
+    )
+
+    cat_w = cat_w.reshape(D, 3 * head_width + unit_width)
+    dense_w = dense_w.reshape(head_width, D)
+    down_w = down_w.reshape(unit_width, D)
+    rows = group * tokens_here
+    x_all = x_all.reshape(rows, D)
+    dy_all = dy_all.reshape(rows, D)
+    vec_flat = vec_all.reshape(planes, cores, shards, vec_rows * 128)
+    at = [0]
+    for size in vec_sizes:
+        at.append(at[-1] + size)
+
+    def rounded(value):
+        return value.astype(jnp.bfloat16).astype(jnp.float32)
+
+    qkv_bias = rounded(vec_flat[..., at[0] : at[1]]).reshape(3, planes, cores, shards, HD)
+    qkv_bias = lax.dynamic_index_in_dim(
+        qkv_bias.transpose(2, 3, 0, 1, 4).reshape(group, 3 * head_width), core * shards + shard, 0, False
+    )
+    up_bias = lax.dynamic_index_in_dim(
+        rounded(vec_flat[..., at[1] : at[2]]).transpose(1, 2, 0, 3).reshape(group, unit_width),
+        core * shards + shard,
+        0,
+        False,
+    )
+    vec_columns = (
+        rounded(vec_flat[..., at[2] : at[3]])
+        .reshape(owners, 4, model_rows)
+        .transpose(1, 0, 2)
+        .reshape(4, D)
+    )
+    norm_gain, norm_shift, dense_bias, down_bias = (vec_columns[index] for index in range(4))
+    segments = lax.dynamic_index_in_dim(vec_flat[..., at[3] : at[4]], plane, 0, False)
+    segments = segments.astype(jnp.int32).reshape(cores, shards * tokens_here)
+    cat_bias = jnp.concatenate([qkv_bias, up_bias])
+
+    x_float = x_all.astype(jnp.float32)
+    center = x_float - jnp.mean(x_float, axis=-1, keepdims=True)
+    inverse = lax.rsqrt(jnp.mean(center * center, axis=-1, keepdims=True) + norm_eps)
+    x_hat = center * inverse
+    norm_bf = (x_hat * norm_gain + norm_shift).astype(jnp.bfloat16)
+
+    fu = jnp.dot(norm_bf, cat_w, preferred_element_type=jnp.float32) + cat_bias
+    pre_act = fu[:, 3 * head_width :]
+    hidden = gelu_tanh(pre_act).astype(jnp.bfloat16)
+    grad_hidden = jnp.dot(dy_all, down_w.T, preferred_element_type=jnp.float32)
+    grad_pre = jax.vjp(gelu_tanh, pre_act)[1](grad_hidden)[0]
+    upb_part = jnp.sum(grad_pre, axis=0)
+    grad_heads = jnp.dot(dy_all, dense_w.T, preferred_element_type=jnp.float32).astype(jnp.bfloat16)
+    attn, dcat, qkvb_part = attention(fu, grad_heads, grad_pre.astype(jnp.bfloat16), segments)
+    out_part = (
+        jnp.dot(attn, dense_w, preferred_element_type=jnp.float32)
+        + jnp.dot(hidden, down_w, preferred_element_type=jnp.float32)
+    ).astype(jnp.bfloat16)
+    down_grad = jnp.dot(hidden.T, dy_all, preferred_element_type=jnp.float32).astype(jnp.bfloat16)
+    dense_grad = jnp.dot(attn.T, dy_all, preferred_element_type=jnp.float32).astype(jnp.bfloat16)
+    cat_grad = jnp.dot(norm_bf.T, dcat, preferred_element_type=jnp.float32).astype(jnp.bfloat16)
+    norm_part = jnp.dot(dcat, cat_w.T, preferred_element_type=jnp.float32)
+    gain_part = jnp.sum(norm_part * x_hat, axis=0)
+    shift_part = jnp.sum(norm_part, axis=0)
+    bias_part = jnp.sum(cotangent.astype(jnp.float32), axis=0)
+    sums = [qkvb_part, upb_part, gain_part, shift_part, bias_part]
+    sum_sizes = [value.size for value in sums]
+    sum_rows = -(-sum(sum_sizes) // 1024) * 8
+    sums = jnp.pad(jnp.concatenate(sums), (0, sum_rows * 128 - sum(sum_sizes))).reshape(sum_rows, 128)
+
+    cat_sum, dense_grad, down_grad, mixed, grad_norm, sums_all = reduce_wires(
+        cat_grad.reshape(planes, group, model_rows, 3 * head_width + unit_width),
+        dense_grad.reshape(planes, model_rows, D),
+        down_grad.reshape(planes, unit_rows, D),
+        out_part.reshape(group, tokens_here, D),
+        norm_part.astype(jnp.bfloat16).reshape(group, tokens_here, D),
+        sums,
+    )
+
+    cat_sum = cat_sum.astype(jnp.float32)
+    qkv_grad = (
+        cat_sum[:, :, : 3 * head_width]
+        .reshape(cores, shards, model_rows, 3, planes, HD)
+        .transpose(2, 3, 4, 0, 1, 5)
+        .reshape(model_rows, 3 * D)
+    )
+    up_grad = (
+        cat_sum[:, :, 3 * head_width :]
+        .reshape(cores, shards, model_rows, planes, unit_rows)
+        .transpose(2, 3, 0, 1, 4)
+        .reshape(model_rows, FF)
+    )
+    sums_flat = sums_all.reshape(cores, shards, sum_rows * 128)
+    at = [0]
+    for size in sum_sizes:
+        at.append(at[-1] + size)
+    qkvb_grad = (
+        sums_flat[..., : at[1]]
+        .reshape(cores, shards, 3, planes, HD)
+        .transpose(2, 3, 0, 1, 4)
+        .reshape(owners, qkv_count)
+    )
+    qkvb_grad = lax.dynamic_index_in_dim(qkvb_grad, owner, 0, False)
+    upb_grad = sums_flat[..., at[1] : at[2]].reshape(group, planes, upb_count)
+    upb_grad = lax.dynamic_index_in_dim(
+        lax.dynamic_index_in_dim(upb_grad, core * shards + shard, 0, False), plane, 0, False
+    )
+    vec_grad = jnp.sum(sums_flat[..., at[2] : at[5]], axis=(0, 1)).reshape(3, owners, model_rows)
+    vec_grad = lax.dynamic_index_in_dim(vec_grad, owner, 1, False)
+    vec_grad = jnp.stack([vec_grad[0], vec_grad[1], vec_grad[2], vec_grad[2]], axis=1)
+
+    x_own = tokens.astype(jnp.float32)
+    output = (x_own + (mixed.astype(jnp.float32) + dense_bias + down_bias)).astype(jnp.bfloat16)
+    own_center = x_own - jnp.mean(x_own, axis=-1, keepdims=True)
+    own_inverse = lax.rsqrt(jnp.mean(own_center * own_center, axis=-1, keepdims=True) + norm_eps)
+    own_hat = own_center * own_inverse
+    hat_grad = grad_norm.astype(jnp.float32) * norm_gain
+    x_grad = own_inverse * (
+        hat_grad
+        - jnp.mean(hat_grad, axis=-1, keepdims=True)
+        - own_hat * jnp.mean(hat_grad * own_hat, axis=-1, keepdims=True)
+    )
+    input_grad = cotangent.astype(jnp.float32) + x_grad
+
+    new = owner_update(
+        (qkv_weight_state, dense_weight_state, up_weight_state, down_weight_state),
+        (qkv_grad, dense_grad, up_grad, down_grad),
+        (qkv_bias_state, up_bias_state, vector_state),
+        (qkvb_grad, upb_grad, vec_grad),
+    )
+    return (
+        output[None],
+        input_grad[None],
+        qkv_grad,
+        qkvb_grad,
+        dense_grad,
+        up_grad,
+        upb_grad,
+        down_grad,
+        vec_grad,
+        *new,
+    )
+
+
+def fast_solution(mesh):
+    rep, shard = mesh.shape["rep"], mesh.shape["shard"]
+    inner = Mesh(mesh.devices.reshape(rep // 2, 2, shard), ("plane", "core", "shard"))
+    both = ("plane", "core")
+    every = ("plane", "core", "shard")
+    in_specs = (
+        P(both, "shard", None),
+        P(both, "shard"),
+        P(both, "shard", None),
+        P(None, every, None),
+        P(None, every),
+        P(None, every, None),
+        P(None, every, None),
+        P(None, every),
+        P(None, every, None),
+        P(None, every, None),
+    )
+    out_specs = (
+        P(both, "shard", None),
+        P(both, "shard", None),
+        P(every, None),
+        P(every),
+        P(every, None),
+        P(every, None),
+        P(every),
+        P(every, None),
+        P(every, None),
+        P(both, "shard", None),
+        P(both, "shard", None),
+        P(both, "shard", None),
+    )
+    return jax.shard_map(fast_body, mesh=inner, in_specs=in_specs, out_specs=out_specs, check_vma=False)
+
+
 def solution(mesh):
     in_specs = (
         P("rep", "shard", None),
@@ -433,4 +1385,6 @@
         P("rep", "shard", None),
         P("rep", "shard", None),
     )
+    if whole_heads(mesh):
+        return fast_solution(mesh)
     return jax.shard_map(body, mesh=mesh, in_specs=in_specs, out_specs=out_specs, check_vma=False)

time: 1800 us -> 509 us (0.28)
  waiting for transfers between devices: 667 us -> 0 us
  blocking collectives: 575 us -> 0 us
  Pallas kernels: 0 us -> 340 us
  local copies, waits for them, and re-layouts: 366 us -> 74.1 us
  matrix products: 102 us -> 67.4 us
  starting transfers between devices: 27.1 us -> 0 us
    all_to_all x5 -> x0, waiting for transfers between devices: 543 us -> none  [the longest x1 411 us: sliced_pass(): lax.all_to_all(down_grid_grad, 'shard', split_axis=2, concat_axis=0, tile...]
    pallas_call x0 -> x4, Pallas kernels: none -> 340 us  [the longest x1 169 us: reduce_wires(): pl.pallas_call(reduce_kernel, in_specs=[hbm] * 5 + [vmem], out_specs=[hbm...]
    unnamed x2 -> x0, blocking collectives: 307 us -> none
    concatenate x3 -> x1, local copies, waits for them, and re-layouts: 160 us -> 0.01 us  [fast_body(): jnp.concatenate(sums)]
    all_gather x3 -> x0, blocking collectives: 140 us -> none  [the longest x1 66.2 us: gather_vectors(): lax.all_gather(own_upb, ('rep', 'shard'), axis=0, tiled=True)]
    all_to_all x3 -> x0, blocking collectives: 128 us -> none  [the longest x1 51.2 us: sliced_pass(): lax.all_to_all(up_split, 'shard', split_axis=2, concat_axis=0, tiled=True)]
    reduce_scatter x5 -> x0, waiting for transfers between devices: 110 us -> none  [the longest x1 110 us: sliced_pass(): lax.psum_scatter(down_back.reshape(outer_count, down_rows, D), 'rep', sca...]
    reshape x7 -> x21, local copies, waits for them, and re-layouts: 114 us -> 27.8 us  [the longest x3 14.1 us: fast_body(): qkv_grad = cat_sum[:, :, :3 * head_width].reshape(cores, shards, model_ro...]
  transfers between devices with their start and end apart: 18 -> 0, of which waited for: 5 -> 0; matrix products, arithmetic and copies ran while one was open for 12% -> 0% of each run, Pallas kernels for 0% -> 0%
where the time goes in v1:
time: 509 us; the launch traced here: 500 us
  Pallas kernels  340 us (67%)
  local copies, waits for them, and re-layouts  74.1 us (15%)
  matrix products  67.4 us (13%)
  other arithmetic  16.7 us (3%)
    pallas_call x1, Pallas kernels, reduce_wires(): pl.pallas_call(reduce_kernel, in_specs=[hbm] * 5 + [vmem], out_specs=[hbm...  169 us
    pallas_call x1, Pallas kernels, gather_wires(): pl.pallas_call(gather_kernel, in_specs=[vmem] * 6, out_specs=[hbm] * 6, o...  113 us
    pallas_call x1, Pallas kernels, owner_update(): pl.pallas_call(partial(owner_update_kernel, plan, small_plan), grid=(step...  43.9 us
    unnamed x79, local copies, waits for them, and re-layouts  15.6 us
    dot_general x1, matrix products, fast_body(): norm_part = jnp.dot(dcat, cat_w.T, preferred_element_type=jnp.float32)  15 us
    pallas_call x1, Pallas kernels, attention(): pl.pallas_call(attention_kernel, grid=(count,), in_specs=[pl.BlockSpec((r...  14.9 us
    reshape x3, local copies, waits for them, and re-layouts, fast_body(): qkv_grad = cat_sum[:, :, :3 * head_width].reshape(cores, shards, model_ro...  14.1 us
    slice x3, local copies, waits for them, and re-layouts, owner_update(): out.reshape(1, 1, out_rows * 128)[:, :, :entries]  13.9 us

profile of v1, /device:TPU:0, one launch (start us, length us, event | category | flops | bytes accessed | tf_op | source)
XLA Modules:
  0.0 500.3 jit_solution(7695466501413092388)
XLA Ops:
  0.6 1.7 slice.203
  2.3 0.8 convert_element_type.146
  3.6 1.5 reshape.314
  5.1 1.5 slice.204
  6.6 1.6 convert_element_type.145
  8.2 1.7 copy.57
  10.0 3.7 reshape.313
  13.7 1.6 pad_maximum_fusion.pieces
  15.3 1.1 fusion.22.dense
  16.4 2.7 fusion.16.down
  19.3 1.2 copy-done.4
  20.5 112.6 %shard_map.193 = (bf16[4,8,64,1792]{3,2,1,0:T(8,128)(2,1)S(1)}, bf16[4,64,2048]{2,1,0:T(8,128)(2,1)S(1)}, bf16[4,256,2048]{2,1,0:T(8,128)(2,1)S(1)}, bf16[8,128,...) custom-call(bf16[8,64,1792]{2,1,0:T(8,128)(2,1)S(1)} %pad_maximum_fusion.pieces, ...), custom_call_target="tpu_custom_call" | custom-call | tf_op jit(solution)/shard_map/pallas_call | solution.py:898
  133.2 2.9 copy-done.7
  136.1 2.0 copy-done.8
  138.1 2.0 copy-done.11
  140.7 1.2 multiply_reduce_fusion.1
  143.1 4.6 add_convert_fusion.1
  148.0 12.3 %convolution_add_fusion.fu_ref = f32[1024,1792]{1,0:T(8,128)S(1)} fusion(bf16[1024,2048]{1,0:T(8,128)(2,1)} %bitcast.143, bf16[2048,1792]{1,0:T(8,128)(2,1)} %bitcast.119, f32[1792]{0:T(1024)S(1)} %pad_maximum_fusion.2), kind=kOutput, calls=%fused_computation.19 | convolution fusion | flops 7518027776 | bytes 18881536 | tf_op jit(solution)/shard_map/dot_general | solution.py:1229
  160.3 2.1 convolution_convert_fusion.3.do_ref
  162.4 1.8 copy-done.15
  164.3 1.1 copy-done.9
  165.3 8.8 %fusion.45 = (f32[1024]{0:T(1024)S(1)}, bf16[1024,1024]{1,0:T(8,128)(2,1)}) fusion(f32[1024,1792]{1,0:T(8,128)S(1)} %convolution_add_fusion.fu_ref, bf16[1024,2048]{1,0:T(8,128)(2,1)S(1)} %bitcast.124, bf16[1024,2048]{1,0:T(8,128)(2,1)S(1)} %bitcast.121), kind=kOutput, calls=%fused_computation.147 | convolution fusion | flops 4321180672 | bytes 14684160 | tf_op jit(solution)/shard_map/dot_general | solution.py:1232
  174.2 1.0 copy.41.seg_col_ref
  175.2 1.9 fusion.18
  177.1 14.9 %shard_map.194 = (bf16[1024,256]{1,0:T(8,128)(2,1)}, bf16[1024,1792]{1,0:T(8,128)(2,1)}, f32[2,1,768]{2,1,0:T(1,128)}) custom-call(f32[1024,1792]{1,0:T(8,128)} %copy-done.15, bf16[1024,256]{1,0:T(8,128)(2,1)} %convolution_convert_fusion.3.do_ref, bf16[1024,1024]{1,0:T(8,128)(2,1)} %get-tuple-element.66.du_ref, s32[1024,1]{1,0:T(8,128)} %copy.41.seg_col_ref, ...), custom_call_target="tpu_custom_call" | custom-call | flops 1342177280 | bytes 9437184 | tf_op jit(solution)/shard_map/pallas_call | solution.py:506
  192.1 15.0 %fusion.41 = (f32[2048]{0:T(1024)S(1)}, f32[2048]{0:T(1024)S(1)}, bf16[1024,2048]{1,0:T(8,128)(2,1)}, bf16[1024,2048]{1,0:T(8,128)(2,1)}) fusion(f32[1024]{0:T(1024)S(1)} %get-tuple-element.87, f32[1024]{0:T(1024)S(1)} %get-tuple-element.88, bf16[8,128,2048]{2,1,0:T(8,128)(2,1)S(1)} %copy-done.1, f32[2048]{0:T(1024)S(1)} %add.217, f32[2048]{0:T(1024)S(1)} %mul.297, ...), kind=kOutput, calls=%fused_computation.146 | convolution fusion | flops 7537160192 | bytes 23633920 | tf_op jit(solution)/shard_map/dot_general | solution.py:1244
  207.2 12.0 %convolution_convert_fusion = bf16[2048,1792]{1,0:T(8,128)(2,1)} fusion(bf16[1024,2048]{1,0:T(8,128)(2,1)} %get-tuple-element.68, bf16[1024,1792]{1,0:T(8,128)(2,1)S(1)} %copy-done.28), kind=kOutput, calls=%fused_computation.8 | convolution fusion | flops 7519862784 | bytes 15204352 | tf_op jit(solution)/shard_map/dot_general | solution.py:1243
  219.1 2.2 convolution_convert_fusion.2
  221.4 6.9 %convolution_convert_fusion.1 = bf16[1024,2048]{1,0:T(8,128)(2,1)} fusion(bf16[1024,2048]{1,0:T(8,128)(2,1)S(1)} %bitcast.126, f32[1024,1792]{1,0:T(8,128)S(1)} %bitcast.132), kind=kOutput, calls=%fused_computation.20 | convolution fusion | flops 4306501632 | bytes 12582912 | tf_op jit(solution)/shard_map/dot_general | solution.py:1241
  228.3 4.8 fusion.40
  233.1 3.3 add_convert_fusion
  237.2 169.0 %shard_map.195 = (bf16[8,64,1792]{2,1,0:T(8,128)(2,1)}, f32[64,2048]{1,0:T(8,128)}, f32[256,2048]{1,0:T(8,128)}, f32[128,2048]{1,0:T(8,128)}, f32[128,2048]{1,0:T(8,128)}, /*index=5*/f32[8,64,128]{2,1,0:T(8,128)}) custom-call(bf16[4,8,64,1792]{3,2,1,0:T(8,128)(2,1)} %bitcast.130, bf16[4,64,2048]{2,1,0:T(8,128)(2,1)} %bitcast.145, ...), custom_call_target="tpu_custom_call" | custom-call | tf_op jit(solution)/shard_map/pallas_call | solution.py:1099
  406.7 1.7 multiply_reduce_fusion.2
  408.6 3.3 fusion.14
  411.8 1.3 slice.163
  413.1 3.7 reshape.334
  416.8 5.6 %copy.55 = f32[2,4,64,3,4,64]{5,1,0,4,3,2:T(4,128)} copy(f32[2,4,64,3,4,64]{5,4,3,2,1,0:T(4,128)} %reshape.334) | data formatting | bytes 3145728 | tf_op jit(solution)/shard_map/reshape | solution.py:1265
  422.5 4.8 reshape.335.refs_1_
  427.6 1.5 slice.165
  429.1 2.0 reshape.339
  431.1 2.9 copy.56
  434.0 2.1 reshape.340.refs_5_
  438.1 43.9 %shard_map.196 = (f32[12296,128]{1,0:T(8,128)}, f32[12296,128]{1,0:T(8,128)}, f32[12296,128]{1,0:T(8,128)}) custom-call(f32[3,64,6144]{2,1,0:T(8,128)} %refs_0_.1, f32[64,6144]{1,0:T(8,128)} %reshape.335.refs_1_, f32[3,64,2048]{2,1,0:T(8,128)} %refs_2_.1, f32[64,2048]{1,0:T(8,128)} %get-tuple-element.114.refs_3_, f32[3,64,8192]{2,1,0:T(8,128)} %refs_4_.1, ...), custom_call_target="tpu_custom_call" | custom-call | flops 31471360 | bytes 44059904 | tf_op jit(solution)/shard_map/pallas_call | solution.py:653
  482.0 7.7 %slice.168 = f32[1,1,1573568]{2,1,0:T(1,128)} slice(f32[1,1,1573888]{2,1,0:T(1,128)} %bitcast.139), slice={[0:1], [0:1], [0:1573568]} | slice | bytes 12588544 | tf_op jit(solution)/shard_map/slice | solution.py:664
  489.7 3.3 slice.169
  493.0 1.1 slice-done.2
  494.8 2.9 slice.170
  498.5 1.3 copy.68
  (146 shorter events, 7.9 us)
Async XLA Ops:
  10.0 9.1 %copy-start.29 = (s32[1,128]{1,0:T(1,128)S(1)}, s32[1,128]{1,0:T(1,128)}, u32[]{:S(2)}) copy-start(s32[1,128]{1,0:T(1,128)} %param.11) | copy-start | bytes 1540
  10.0 9.1 %copy-start.22 = (f32[3,64,4]{1,2,0:T(4,128)S(1)}, f32[3,64,4]{1,2,0:T(4,128)}, u32[]{:S(2)}) copy-start(f32[3,64,4]{1,2,0:T(4,128)} %param.19) | copy-start | bytes 9220
  10.0 9.2 %copy-start.26 = (f32[3,256]{1,0:T(4,128)S(1)}, f32[3,256]{1,0:T(4,128)}, u32[]{:S(2)}) copy-start(f32[3,256]{1,0:T(4,128)} %param.17) | copy-start | bytes 9220
  10.0 9.2 %copy-start.27 = (f32[3,192]{1,0:T(4,128)S(1)}, f32[3,192]{1,0:T(4,128)}, u32[]{:S(2)}) copy-start(f32[3,192]{1,0:T(4,128)} %param.14) | copy-start | bytes 6916
  10.0 9.3 %copy-start.2 = (bf16[1,128,2048]{2,1,0:T(8,128)(2,1)S(1)}, bf16[1,128,2048]{2,1,0:T(8,128)(2,1)}, u32[]{:S(2)}) copy-start(bf16[1,128,2048]{2,1,0:T(8,128)(2,1)} %param.10) | copy-start | bytes 1572868
  10.0 9.3 %copy-start.3 = (bf16[1,128,2048]{2,1,0:T(8,128)(2,1)S(1)}, bf16[1,128,2048]{2,1,0:T(8,128)(2,1)}, u32[]{:S(2)}) copy-start(bf16[1,128,2048]{2,1,0:T(8,128)(2,1)} %param.12) | copy-start | bytes 1572868
  19.3 1.2 copy-start.4
  133.2 2.9 copy-start.7
  136.1 2.0 copy-start.8
  138.1 2.0 copy-start.11
  140.1 2.0 copy-start
  140.1 2.3 copy-start.5
  148.0 12.3 %copy-start.6 = (bf16[4,64,2048]{2,1,0:T(8,128)(2,1)S(1)}, bf16[4,64,2048]{2,1,0:T(8,128)(2,1)}, u32[]{:S(2)}) copy-start(bf16[4,64,2048]{2,1,0:T(8,128)(2,1)} %copy-done.5) | copy-start | bytes 3145732
  148.0 12.3 %copy-start.12 = (bf16[8,128,2048]{2,1,0:T(8,128)(2,1)S(1)}, bf16[8,128,2048]{2,1,0:T(8,128)(2,1)}, u32[]{:S(2)}) copy-start(bf16[8,128,2048]{2,1,0:T(8,128)(2,1)} %copy-done.11) | copy-start | bytes 12582916
  160.3 4.0 copy-start.15
  160.3 5.0 %copy-start.9 = (bf16[4,256,2048]{2,1,0:T(8,128)(2,1)S(1)}, bf16[4,256,2048]{2,1,0:T(8,128)(2,1)}, u32[]{:S(2)}) copy-start(bf16[4,256,2048]{2,1,0:T(8,128)(2,1)} %copy-done.8) | copy-start | bytes 12582916
  174.2 3.0 copy-start.20
  177.1 14.9 %copy-start.1 = (bf16[8,128,2048]{2,1,0:T(8,128)(2,1)S(1)}, bf16[8,128,2048]{2,1,0:T(8,128)(2,1)}, u32[]{:S(2)}) copy-start(bf16[8,128,2048]{2,1,0:T(8,128)(2,1)} %copy-done) | copy-start | bytes 12582916
  192.1 15.1 %copy-start.28 = (bf16[1024,1792]{1,0:T(8,128)(2,1)S(1)}, bf16[1024,1792]{1,0:T(8,128)(2,1)}, u32[]{:S(2)}) copy-start(bf16[1024,1792]{1,0:T(8,128)(2,1)} %get-tuple-element.36) | copy-start | bytes 11010052
  207.1 14.3 %slice-start = ((s8[7340032]{0:T(1024)(128)(4,1)}), s8[4194304]{0:T(1024)(128)(4,1)S(1)}, s32[]{:S(2)}) async-start(s8[7340032]{0:T(1024)(128)(4,1)} %bitcast.131), calls=%async_computation | async-start | bytes 8388608
  207.1 12.0 %copy-start.13 = (bf16[8,128,2048]{2,1,0:T(8,128)(2,1)S(1)}, bf16[8,128,2048]{2,1,0:T(8,128)(2,1)}, u32[]{:S(2)}) copy-start(bf16[8,128,2048]{2,1,0:T(8,128)(2,1)} %copy-done.11) | copy-start | bytes 12582916
  207.1 12.0 %copy-start.18 = (bf16[1024,256]{1,0:T(8,128)(2,1)S(1)}, bf16[1024,256]{1,0:T(8,128)(2,1)}, u32[]{:S(2)}) copy-start(bf16[1024,256]{1,0:T(8,128)(2,1)} %get-tuple-element.37) | copy-start | bytes 1572868
  207.2 14.2 %slice-start.1 = ((s8[7340032]{0:T(1024)(128)(4,1)}), s8[3145728]{0:T(1024)(128)(4,1)S(1)}, s32[]{:S(2)}) async-start(s8[7340032]{0:T(1024)(128)(4,1)} %bitcast.131), calls=%async_computation.1 | async-start | bytes 6291456
  221.4 6.9 %copy-start.10 = (bf16[4,256,2048]{2,1,0:T(8,128)(2,1)S(1)}, bf16[4,256,2048]{2,1,0:T(8,128)(2,1)}, u32[]{:S(2)}) copy-start(bf16[4,256,2048]{2,1,0:T(8,128)(2,1)} %copy-done.8) | copy-start | bytes 12582916
  233.1 3.3 copy-start.23
  406.3 5.6 %copy-start.16 = (bf16[8,64,1792]{2,1,0:T(8,128)(2,1)S(1)}, bf16[8,64,1792]{2,1,0:T(8,128)(2,1)}, u32[]{:S(2)}) copy-start(bf16[8,64,1792]{2,1,0:T(8,128)(2,1)} %get-tuple-element.41) | copy-start | bytes 5505028
  416.8 10.4 %copy-start.19 = (f32[8,64,128]{2,1,0:T(8,128)S(1)}, f32[8,64,128]{2,1,0:T(8,128)}, u32[]{:S(2)}) copy-start(f32[8,64,128]{2,1,0:T(8,128)} %get-tuple-element.42) | copy-start | bytes 786436
  427.6 9.6 %copy-start.25 = (f32[1,192]{1,0:T(1,128)}, f32[1,192]{1,0:T(1,128)S(1)}, u32[]{:S(2)}) copy-start(f32[1,192]{1,0:T(1,128)S(1)} %constant_dynamic-slice_fusion.4) | copy-start | bytes 2308
  436.2 45.8 %copy-start.24 = (f32[1,1,256]{2,1,0:T(1,128)}, f32[1,1,256]{2,1,0:T(1,128)S(1)}, u32[]{:S(2)}) copy-start(f32[1,1,256]{2,1,0:T(1,128)S(1)} %constant_dynamic-slice_fusion.3) | copy-start | bytes 3076
  436.3 45.6 %copy-start.21 = (f32[64,4]{0,1:T(4,128)}, f32[64,4]{0,1:T(4,128)S(1)}, u32[]{:S(2)}) copy-start(f32[64,4]{0,1:T(4,128)S(1)} %pad_maximum_fusion.3) | copy-start | bytes 3076
  482.0 7.7 %slice-start.4 = ((s8[6295552]{0:T(1024)(128)(4,1)}), s8[4194304]{0:T(1024)(128)(4,1)S(1)}, s32[]{:S(2)}) async-start(s8[6295552]{0:T(1024)(128)(4,1)} %bitcast.136), calls=%async_computation.4 | async-start | bytes 8388608
  482.0 7.7 %slice-start.5 = ((s8[6295552]{0:T(1024)(128)(4,1)}), s8[2101248]{0:T(1024)(128)(4,1)S(1)}, s32[]{:S(2)}) async-start(s8[6295552]{0:T(1024)(128)(4,1)} %bitcast.136), calls=%async_computation.5 | async-start | bytes 4202496
  489.7 4.4 slice-start.2
  489.7 5.1 %slice-start.3 = ((s8[6295552]{0:T(1024)(128)(4,1)}), s8[2101248]{0:T(1024)(128)(4,1)S(1)}, s32[]{:S(2)}) async-start(s8[6295552]{0:T(1024)(128)(4,1)} %bitcast.133), calls=%async_computation.3 | async-start | bytes 4202496
  494.8 2.9 copy-start.17
  494.8 3.7 copy-start.14

commit v2 on v1

--- a/solution.py
+++ b/solution.py
@@ -544,14 +544,16 @@
     return weight - learn_rate * (corrected / divisor + weight_decay * weight), first, second
 
 
-def owner_update_kernel(plan, small_plan, *refs):
-    count = len(plan)
-    small_ref = refs[2 * count]
-    outs = refs[2 * count + 1 :]
+def owner_update_kernel(plan, small_plan, groups, *refs):
+    planes, cores, shards = groups
+    qkv_state, dense_state, up_state, down_state, cat_ref, dense_grad, down_grad, small_ref = refs[:8]
+    outs = refs[8:11]
+    qkv_out, up_out, cat_buf = refs[11:]
     step = pl.program_id(0)
     lane = lax.broadcasted_iota(jnp.int32, (8, 128), 1)
     sub = lax.broadcasted_iota(jnp.int32, (8, 128), 0)
     lane_row = lax.broadcasted_iota(jnp.int32, (1, 128), 1)
+    wide = 1024
 
     @pl.when(step == 0)
     def small():
@@ -561,51 +563,89 @@
                 new = small_ref[entry, pl.ds(source, 1), :]
                 outs[entry][pl.ds(row, 1), :] = jnp.where((lane_row >= low) & (lane_row < high), new, old)
 
-    for index, (rows, tiles, start, shifted) in enumerate(plan):
-        state, grad = refs[2 * index], refs[2 * index + 1]
-        for group in range(rows // 8):
-            place = pl.ds(group * 8, 8)
+    def widen(piece, carry):
+        cat_buf[piece] = cat_ref[piece].astype(jnp.float32)
+        return carry
+
+    lax.fori_loop(0, cat_ref.shape[0], widen, 0)
+
+    def place_rows(state, grad_of, rows, tiles, start, shifted, keep=None):
+        chunk = min(wide, tiles * 128)
+
+        def one_group(group, carry):
+            place = pl.ds(pl.multiple_of(group * 8, 8), 8)
             base = start + (step * (rows // 8) + group) * (8 * tiles)
 
-            def values(column, state=state, grad=grad, place=place):
-                lanes = pl.ds(pl.multiple_of(column * 128, 128), 128)
+            def values(column, size):
+                lanes = pl.ds(column, size)
+                grad = grad_of(place, column, size)
+                if keep is not None and size > 128:
+                    keep[place, lanes] = grad
                 return adam_values(
-                    state[0, place, lanes], state[1, place, lanes], state[2, place, lanes], grad[place, lanes]
+                    state[0, place, lanes], state[1, place, lanes], state[2, place, lanes], grad
                 )
 
-            if not shifted:
-
-                def plain(column, carry, base=base, tiles=tiles, values=values):
-                    for out, value in zip(outs, values(column)):
-                        out[pl.ds(base + column, 8, stride=tiles), :] = value
-                    return carry
-
-                lax.fori_loop(0, tiles, plain, 0, unroll=4)
-                continue
-
-            def turned(column, values=values):
-                return tuple(pltpu.roll(value, 64, 1) for value in values(column))
-
-            last = turned(tiles - 1)
-            before = tuple(
-                jnp.where(sub == 0, out[pl.ds(base, 1), :], pltpu.roll(value, 1, 0))
-                for out, value in zip(outs, last)
-            )
-
-            def moved(column, carry, base=base, tiles=tiles, turned=turned):
-                now = turned(column)
-                for out, old, new in zip(outs, carry, now):
-                    out[pl.ds(base + column, 8, stride=tiles), :] = jnp.where(lane < 64, old, new)
-                return now
-
-            lax.fori_loop(0, tiles, moved, before, unroll=4)
-            for out, value in zip(outs, last):
-                row = pl.ds(base + 8 * tiles, 1)
-                out[row, :] = jnp.where(lane_row < 64, value[7:8], out[row, :])
-
-
-def owner_update(states, grads, small_states, small_grads):
-    steps = 8
+            if shifted:
+                last = tuple(pltpu.roll(value, 64, 1) for value in values((tiles - 1) * 128, 128))
+                before = tuple(
+                    jnp.where(sub == 0, out[pl.ds(base, 1), :], pltpu.roll(value, 1, 0))
+                    for out, value in zip(outs, last)
+                )
+            for column in range(0, tiles * 128, chunk):
+                done = values(column, chunk)
+                for entry, out in enumerate(outs):
+                    for tile in range(chunk // 128):
+                        value = done[entry][:, tile * 128 : (tile + 1) * 128]
+                        if shifted:
+                            value = pltpu.roll(value, 64, 1)
+                            old = before[entry] if tile == 0 else now
+                            now = value
+                            value = jnp.where(lane < 64, old, value)
+                        out[pl.ds(base + column // 128 + tile, 8, stride=tiles), :] = value
+                    if shifted:
+                        before = before[:entry] + (now,) + before[entry + 1 :]
+            if shifted:
+                for out, value in zip(outs, before):
+                    row = pl.ds(base + 8 * tiles, 1)
+                    out[row, :] = jnp.where(lane_row < 64, value[7:8], out[row, :])
+            return carry
+
+        lax.fori_loop(0, rows // 8, one_group, 0)
+
+    def qkv_grad(place, column, size):
+        tiles = []
+        for start in range(column, column + size, 128):
+            part, head = divmod(start // HD, planes * cores * shards)
+            halves = []
+            for side in range(2):
+                plane, member = divmod(head + side, cores * shards)
+                spot = (part * planes + plane) * HD
+                half = cat_buf[member, place, pl.ds(spot // 128 * 128, 128)]
+                halves.append(half if spot % 128 == side * HD else pltpu.roll(half, HD, 1))
+            tiles.append(jnp.where(lane < HD, halves[0], halves[1]))
+        return tiles[0] if len(tiles) == 1 else jnp.concatenate(tiles, axis=1)
+
+    units = up_state.shape[2] // (planes * cores * shards)
+
+    def up_grad(place, column, size):
+        parts = []
+        for start in range(column, column + size, min(units, size)):
+            plane, member = divmod(start // units, cores * shards)
+            spot = 3 * planes * HD + plane * units + start % units
+            parts.append(cat_buf[member, place, pl.ds(spot, min(units, size))])
+        return parts[0] if len(parts) == 1 else jnp.concatenate(parts, axis=1)
+
+    def plain(grad):
+        return lambda place, column, size: grad[place, pl.ds(column, size)]
+
+    place_rows(qkv_state, qkv_grad, *plan[0], keep=qkv_out)
+    place_rows(dense_state, plain(dense_grad), *plan[1])
+    place_rows(up_state, up_grad, *plan[2], keep=up_out)
+    place_rows(down_state, plain(down_grad), *plan[3])
+
+
+def owner_update(states, cat_sum, grads, small_states, small_grads, groups):
+    steps = 4
     sizes = [state.shape[1] * state.shape[2] for state in states]
     small_sizes = [grad.size for grad in small_grads]
     order = [("m", 0), ("s", 0), ("m", 1), ("m", 2), ("s", 1), ("m", 3), ("s", 2)]
@@ -643,25 +683,36 @@
             for entry in range(3)
         ]
     ).reshape(3, small_row, 128)
-    in_specs = []
-    operands = []
-    for state, grad, (rows, tiles, start, shifted) in zip(states, grads, plan):
-        in_specs.append(pl.BlockSpec((3, rows, tiles * 128), lambda s: (0, s, 0)))
-        in_specs.append(pl.BlockSpec((rows, tiles * 128), lambda s: (s, 0)))
-        operands += [state, grad]
+    in_specs = [
+        pl.BlockSpec((3, rows, tiles * 128), lambda s: (0, s, 0)) for rows, tiles, start, shifted in plan
+    ]
+    qkv_rows, up_rows = plan[0][0], plan[2][0]
+    in_specs.append(pl.BlockSpec((cat_sum.shape[0], qkv_rows, cat_sum.shape[2]), lambda s: (0, s, 0)))
+    in_specs.append(pl.BlockSpec((plan[1][0], plan[1][1] * 128), lambda s: (s, 0)))
+    in_specs.append(pl.BlockSpec((plan[3][0], plan[3][1] * 128), lambda s: (s, 0)))
     in_specs.append(pl.BlockSpec((3, small_row, 128), lambda s: (0, 0, 0)))
-    outs = pl.pallas_call(
-        partial(owner_update_kernel, plan, small_plan),
+    flat = [pl.BlockSpec((out_rows, 128), lambda s: (0, 0), pipeline_mode=pl.Buffered(1))] * 3
+    *outs, qkv_grad, up_grad = pl.pallas_call(
+        partial(owner_update_kernel, plan, small_plan, groups),
         grid=(steps,),
         in_specs=in_specs,
-        out_specs=[pl.BlockSpec((out_rows, 128), lambda s: (0, 0), pipeline_mode=pl.Buffered(1))] * 3,
-        out_shape=[jax.ShapeDtypeStruct((out_rows, 128), jnp.float32)] * 3,
+        out_specs=flat
+        + [
+            pl.BlockSpec((qkv_rows, plan[0][1] * 128), lambda s: (s, 0)),
+            pl.BlockSpec((up_rows, plan[2][1] * 128), lambda s: (s, 0)),
+        ],
+        out_shape=[jax.ShapeDtypeStruct((out_rows, 128), jnp.float32)] * 3
+        + [
+            jax.ShapeDtypeStruct(states[0].shape[1:], jnp.float32),
+            jax.ShapeDtypeStruct(states[2].shape[1:], jnp.float32),
+        ],
+        scratch_shapes=[pltpu.VMEM((cat_sum.shape[0], qkv_rows, cat_sum.shape[2]), jnp.float32)],
         compiler_params=pltpu.CompilerParams(vmem_limit_bytes=56 << 20),
         cost_estimate=pl.CostEstimate(
             flops=20 * entries, bytes_accessed=28 * entries, transcendentals=2 * entries
         ),
-    )(*operands, small)
-    return tuple(out.reshape(1, 1, out_rows * 128)[:, :, :entries] for out in outs)
+    )(*states, cat_sum, *grads, small)
+    return tuple(out.reshape(1, 1, out_rows * 128)[:, :, :entries] for out in outs), qkv_grad, up_grad
 
 
 class Wires:
@@ -727,10 +778,36 @@
                 pl.when(when)(copy.wait_send)
 
 
+def pack_pieces(qkv, up, pieces, planes, cores, shards):
+    rows = qkv.shape[0]
+    lane = lax.broadcasted_iota(jnp.int32, (rows, 128), 1)
+    units = up.shape[1] // (planes * cores * shards)
+    for core in range(cores):
+        for shard in range(shards):
+            piece = core * shards + shard
+            for tile in range(3 * planes // 2):
+                halves = []
+                for side in range(2):
+                    part, plane = divmod(2 * tile + side, planes)
+                    head = (plane * cores + core) * shards + shard
+                    start = part * planes * cores * shards * HD + head * HD
+                    half = qkv[:, pl.ds(start // 128 * 128, 128)]
+                    halves.append(half if start % 128 == side * HD else pltpu.roll(half, HD, 1))
+                pieces[piece, :, pl.ds(tile * 128, 128)] = jnp.where(lane < HD, halves[0], halves[1]).astype(
+                    jnp.bfloat16
+                )
+            for plane in range(planes):
+                block = (plane * cores + core) * shards + shard
+                pieces[piece, :, pl.ds(3 * planes * HD + plane * units, units)] = up[
+                    :, pl.ds(block * units, units)
+                ].astype(jnp.bfloat16)
+
+
 def gather_kernel(
-    pieces, dense, down, tokens, cotangent, vectors,
+    qkv_state, up_state, dense_state, down_state, tokens, cotangent, vectors,
     cat_out, dense_out, down_out, x_out, dy_out, vec_out,
-    send_sems, group_sem, first_sem, second_sem, far_sem, up_sem, low_sem, core_sem, local_sem,
+    qkv_buf, up_buf, dense_buf, down_buf, pieces, dense, down,
+    load_sem, send_sems, group_sem, first_sem, second_sem, far_sem, up_sem, low_sem, core_sem, local_sem,
 ):
     net = Wires(send_sems)
     plane, core, shard, shards, group, mine = net.plane, net.core, net.shard, net.shards, net.group, net.mine
@@ -782,7 +859,18 @@
         relay_first[cat_units[mask]] = position % 2 == 0
         relay_first[vec_units[mask]] = position % 2 == 1
 
+    loads = [
+        pltpu.make_async_copy(state.at[0], buffer, load_sem.at[index])
+        for index, (state, buffer) in enumerate(
+            ((qkv_state, qkv_buf), (up_state, up_buf), (down_state, down_buf), (dense_state, dense_buf))
+        )
+    ]
+    for load in loads:
+        load.start()
     net.barrier()
+    loads[0].wait()
+    loads[1].wait()
+    pack_pieces(qkv_buf, up_buf, pieces, cat_out.shape[0], group // shards, shards)
 
     locals_ = [
         (pieces.at[mine], cat_out.at[plane, mine]),
@@ -800,6 +888,10 @@
         target = net.member(mine ^ mask)
         net.send(vectors, vec_out.at[plane, mine], group_sem.at[1, mask], target)
         net.send(pieces.at[mine ^ mask], cat_out.at[plane, mine], group_sem.at[0, mask], target)
+    loads[2].wait()
+    down[...] = down_buf[...].astype(jnp.bfloat16)
+    loads[3].wait()
+    dense[...] = dense_buf[...].astype(jnp.bfloat16)
     for index in own_units:
         spread(index)
     spread(cat_units[0])
@@ -884,30 +976,39 @@
     net.drain()
 
 
-def gather_wires(pieces, dense, down, tokens, cotangent, vectors):
+def gather_wires(qkv, up, dense, down, tokens, cotangent, vectors):
     group, shards = lax.axis_size("core") * lax.axis_size("shard"), lax.axis_size("shard")
     planes = lax.axis_size("plane")
+    width = (qkv.shape[2] + up.shape[2]) // group
     units = 6 + 2 * group
     vmem = pl.BlockSpec(memory_space=pltpu.VMEM)
     hbm = pl.BlockSpec(memory_space=pl.ANY)
 
-    def out(lead, value):
-        return jax.ShapeDtypeStruct(lead + value.shape, value.dtype)
+    def out(*shape, dtype=jnp.bfloat16):
+        return jax.ShapeDtypeStruct(shape, dtype)
 
     dma = pltpu.SemaphoreType.DMA
     return pl.pallas_call(
         gather_kernel,
-        in_specs=[vmem] * 6,
+        in_specs=[hbm] * 4 + [vmem] * 3,
         out_specs=[hbm] * 6,
         out_shape=[
-            out((planes,), pieces),
-            out((planes,), dense),
-            out((planes,), down),
-            out((group,), tokens),
-            out((group,), cotangent),
-            out((planes, group), vectors),
+            out(planes, group, qkv.shape[1], width),
+            out(planes, *dense.shape[1:]),
+            out(planes, *down.shape[1:]),
+            out(group, *tokens.shape),
+            out(group, *cotangent.shape),
+            out(planes, group, *vectors.shape, dtype=vectors.dtype),
         ],
         scratch_shapes=[
+            pltpu.VMEM(qkv.shape[1:], qkv.dtype),
+            pltpu.VMEM(up.shape[1:], up.dtype),
+            pltpu.VMEM(dense.shape[1:], dense.dtype),
+            pltpu.VMEM(down.shape[1:], down.dtype),
+            pltpu.VMEM((group, qkv.shape[1], width), jnp.bfloat16),
+            pltpu.VMEM(dense.shape[1:], jnp.bfloat16),
+            pltpu.VMEM(down.shape[1:], jnp.bfloat16),
+            dma((4,)),
             dma((2 * (group - 1) + 3 * units + 2 * 2 * (shards - 1) + 2 * (2 * shards - 1),)),
             dma((2, group)),
             dma((units,)),
@@ -921,7 +1022,7 @@
         compiler_params=pltpu.CompilerParams(
             collective_id=0, has_side_effects=True, vmem_limit_bytes=24 << 20
         ),
-    )(pieces, dense, down, tokens, cotangent, vectors)
+    )(qkv, up, dense, down, tokens, cotangent, vectors)
 
 
 def add_rows(target, *sources):
@@ -976,52 +1077,76 @@
 
     streams = (out_part, norm_part)
     finals = (mixed_out, norm_out)
-    TOKEN_IN, TOKEN_OWN, TOKEN_SUM, TOKEN_LINE = range(4)
-
+    TOKEN_IN, TOKEN_OWN, TOKEN_UP, TOKEN_LOW, TOKEN_SUM = range(5)
+
+    for stream in range(2):
+        for place in range(shards):
+            load(
+                ("token", stream, place),
+                streams[stream].at[core * shards + place],
+                token_buf.at[TOKEN_OWN, stream, place],
+            )
     for index, (part, buffers, slot) in enumerate(units):
         near, far, near_plane, far_plane = ways(index)
         load(("pass", index), part(far_plane), buffers.at[PASS_OWN, slot])
-    for stream in range(2):
-        for mask in range(shards):
-            load(
-                ("token", stream, mask),
-                streams[stream].at[core * shards + (shard ^ mask)],
-                token_buf.at[TOKEN_OWN, stream, mask],
-            )
     for index, (part, buffers, slot) in enumerate(units):
         load(("keep", index), part(plane), buffers.at[KEEP_OWN, slot])
 
     net.barrier()
 
-    net.send(sums, sum_buf.at[0], sum_sem.at[0], net.first)
-    for stream in range(2):
-        for mask in reversed(range(shards)):
-            net.send(
-                streams[stream].at[(1 - core) * shards + (shard ^ mask)],
-                token_buf.at[TOKEN_IN, stream, mask],
-                core_sem.at[stream, mask],
-                partner,
-            )
-    for index, (part, buffers, slot) in enumerate(units):
+    def start_unit(index):
+        part, buffers, slot = units[index]
         near, far, near_plane, far_plane = ways(index)
         net.send(part(plane ^ 3), buffers.at[PASS_IN, slot], pass_sem.at[0, index], near)
         net.send(part(near_plane), buffers.at[KEEP_IN, slot], near_sem.at[index], near)
 
-    def token_sum(stream, mask):
-        net.arrived(token_buf.at[TOKEN_IN, stream, mask], core_sem.at[stream, mask])
-        loads["token", stream, mask].wait()
-        add_rows(
-            token_buf.at[TOKEN_SUM, stream, mask],
-            token_buf.at[TOKEN_IN, stream, mask],
-            token_buf.at[TOKEN_OWN, stream, mask],
-        )
-        if mask:
+    net.send(sums, sum_buf.at[0], sum_sem.at[0], net.first)
+    places = [place for rank in range(shards // 2) for place in (shards - 1 - rank, rank)]
+    for place in places:
+        for stream in range(2):
             net.send(
-                token_buf.at[TOKEN_SUM, stream, mask],
-                token_buf.at[TOKEN_LINE, stream, mask],
-                line_sem.at[stream, mask],
-                (plane, core, shard ^ mask),
+                streams[stream].at[(1 - core) * shards + place],
+                token_buf.at[TOKEN_IN, stream, place],
+                core_sem.at[stream, place],
+                partner,
             )
+    for index in range(group):
+        start_unit(index)
+
+    def chain(stream, hop, rank):
+        for upward in (True, False):
+            target = shards - 1 - rank if upward else rank
+            here = hop if upward else shards - 1 - hop
+            slot, sems = (TOKEN_UP, line_sem.at[0]) if upward else (TOKEN_LOW, line_sem.at[1])
+            values = [token_buf.at[TOKEN_IN, stream, target], token_buf.at[TOKEN_OWN, stream, target]]
+            came = token_buf.at[slot, stream, target]
+            total = token_buf.at[TOKEN_SUM, stream, target]
+            holds = shard == here
+            if hop:
+                net.arrived(came, sems.at[stream, target], holds)
+
+            @pl.when(holds)
+            def add(values=values, came=came, total=total):
+                add_rows(total, *(values + ([came] if hop else [])))
+
+            there = jnp.clip(shard + (1 if upward else -1), 0, shards - 1)
+            net.send(total, came, sems.at[stream, target], (plane, core, there), holds)
+
+    def final(stream):
+        for place in range(shards):
+            holds = shard == place
+            values = [token_buf.at[TOKEN_IN, stream, place], token_buf.at[TOKEN_OWN, stream, place]]
+            for slot, side, present in (
+                (TOKEN_UP, line_sem.at[0], place > 0),
+                (TOKEN_LOW, line_sem.at[1], place < shards - 1),
+            ):
+                if present:
+                    values.append(token_buf.at[slot, stream, place])
+                    net.arrived(token_buf.at[slot, stream, place], side.at[stream, place], holds)
+
+            @pl.when(holds)
+            def add(values=values):
+                add_rows(finals[stream], *values)
 
     def pass_on(index):
         part, buffers, slot = units[index]
@@ -1053,33 +1178,51 @@
         else:
             add_rows(dense_out.at[pl.ds(slot * dense_rows, dense_rows)], *values)
 
+    for place in places:
+        for stream in range(2):
+            net.arrived(token_buf.at[TOKEN_IN, stream, place], core_sem.at[stream, place])
+            loads["token", stream, place].wait()
+    for rank in range(shards - 1):
+        for stream in range(2):
+            chain(stream, 0, rank)
     net.arrived(sum_buf.at[0], sum_sem.at[0])
     sum_buf[1] = sums[...] + sum_buf[0]
     net.send(sum_buf.at[1], sum_buf.at[2], sum_sem.at[1], net.second)
-    for mask in reversed(range(shards)):
-        token_sum(0, mask)
+    later = [
+        (stream, hop, rank)
+        for hop, rank in sorted(
+            ((hop, rank) for hop in range(1, shards - 1) for rank in range(shards - 1 - hop)),
+            key=lambda pair: (pair[0] + 2 * pair[1], pair[0]),
+        )
+        for stream in range(2)
+    ]
+    cats, every = range(group), range(len(units))
+    for index in cats:
+        if index == group - 2:
+            for other in every[group:]:
+                start_unit(other)
+        pass_on(index)
+        if index % 2 and later:
+            chain(*later.pop(0))
+            if later and index > 1:
+                chain(*later.pop(0))
     net.arrived(sum_buf.at[2], sum_sem.at[1])
     sum_buf[3] = sum_buf[1] + sum_buf[2]
     for mask in range(1, group):
         net.send(sum_buf.at[3], sums_out.at[mine], group_sem.at[1, mask], net.member(mine ^ mask))
     load("sums", sum_buf.at[3], sums_out.at[mine])
-    lag = 4
-    for index in range(len(units) + lag):
-        if index < len(units):
-            pass_on(index)
-        if index >= lag:
-            finish(index - lag)
-        if index == 1:
-            for mask in reversed(range(shards)):
-                token_sum(1, mask)
+    for index in cats[: group - 2]:
+        finish(index)
+        if later:
+            chain(*later.pop(0))
+    for index in every[group:]:
+        pass_on(index)
+    for index in cats[group - 2 :]:
+        finish(index)
     for stream in range(2):
-        for mask in range(1, shards):
-            net.arrived(token_buf.at[TOKEN_LINE, stream, mask], line_sem.at[stream, mask])
-        add_rows(
-            finals[stream],
-            token_buf.at[TOKEN_SUM, stream, 0],
-            *[token_buf.at[TOKEN_LINE, stream, mask] for mask in range(1, shards)],
-        )
+        final(stream)
+    for index in every[group:]:
+        finish(index)
     for mask in range(1, group):
         net.arrived(cat_out.at[mine ^ mask], group_sem.at[0, mask])
         net.arrived(sums_out.at[mine ^ mask], group_sem.at[1, mask])
@@ -1112,14 +1255,14 @@
             pltpu.VMEM((6, group) + cat.shape[2:], cat.dtype),
             pltpu.VMEM((6, 4, down.shape[1] // 4, down.shape[2]), down.dtype),
             pltpu.VMEM((6, 2, dense.shape[1] // 2, dense.shape[2]), dense.dtype),
-            pltpu.VMEM((4, 2, shards) + tokens, out_part.dtype),
+            pltpu.VMEM((5, 2, shards) + tokens, out_part.dtype),
             pltpu.VMEM((4,) + sums.shape, sums.dtype),
-            dma((2 + 2 * shards + 2 * (shards - 1) + 3 * units + 2 * (group - 1),)),
+            dma((2 + 2 * shards + 2 * shards * (shards - 1) + 3 * units + 2 * (group - 1),)),
             dma((units,)),
             dma((2, units)),
             dma((2, group)),
             dma((2, shards)),
-            dma((2, shards)),
+            dma((2, 2, shards)),
             dma((2,)),
             dma((2 * units + 2 * shards + 2,)),
         ],
@@ -1154,23 +1297,6 @@
     qkv_count, upb_count = qkv_bias_state.shape[1], up_bias_state.shape[1]
 
     tokens, cotangent, q_seg = hidden_in[0], out_grad[0], segment_ids[0]
-    qkv_pieces = (
-        qkv_weight_state[0]
-        .astype(jnp.bfloat16)
-        .reshape(model_rows, 3, planes, cores, shards, HD)
-        .transpose(3, 4, 0, 1, 2, 5)
-        .reshape(group, model_rows, 3 * head_width)
-    )
-    up_pieces = (
-        up_weight_state[0]
-        .astype(jnp.bfloat16)
-        .reshape(model_rows, planes, cores, shards, unit_rows)
-        .transpose(2, 3, 0, 1, 4)
-        .reshape(group, model_rows, unit_width)
-    )
-    pieces = jnp.concatenate([qkv_pieces, up_pieces], axis=2)
-    dense_own = dense_weight_state[0].astype(jnp.bfloat16)
-    down_own = down_weight_state[0].astype(jnp.bfloat16)
     vec_list = [
         qkv_bias_state[0],
         up_bias_state[0],
@@ -1182,7 +1308,13 @@
     vec_own = jnp.pad(jnp.concatenate(vec_list), (0, vec_rows * 128 - sum(vec_sizes))).reshape(vec_rows, 128)
 
     cat_w, dense_w, down_w, x_all, dy_all, vec_all = gather_wires(
-        pieces, dense_own, down_own, tokens, cotangent, vec_own
+        qkv_weight_state,
+        up_weight_state,
+        dense_weight_state,
+        down_weight_state,
+        tokens,
+        cotangent,
+        vec_own,
     )
 
     cat_w = cat_w.reshape(D, 3 * head_width + unit_width)
@@ -1259,19 +1391,6 @@
         sums,
     )
 
-    cat_sum = cat_sum.astype(jnp.float32)
-    qkv_grad = (
-        cat_sum[:, :, : 3 * head_width]
-        .reshape(cores, shards, model_rows, 3, planes, HD)
-        .transpose(2, 3, 4, 0, 1, 5)
-        .reshape(model_rows, 3 * D)
-    )
-    up_grad = (
-        cat_sum[:, :, 3 * head_width :]
-        .reshape(cores, shards, model_rows, planes, unit_rows)
-        .transpose(2, 3, 0, 1, 4)
-        .reshape(model_rows, FF)
-    )
     sums_flat = sums_all.reshape(cores, shards, sum_rows * 128)
     at = [0]
     for size in sum_sizes:
@@ -1304,11 +1423,13 @@
     )
     input_grad = cotangent.astype(jnp.float32) + x_grad
 
-    new = owner_update(
+    new, qkv_grad, up_grad = owner_update(
         (qkv_weight_state, dense_weight_state, up_weight_state, down_weight_state),
-        (qkv_grad, dense_grad, up_grad, down_grad),
+        cat_sum,
+        (dense_grad, down_grad),
         (qkv_bias_state, up_bias_state, vector_state),
         (qkvb_grad, upb_grad, vec_grad),
+        (planes, cores, shards),
     )
     return (
         output[None],

time: 509 us -> 403 us (0.79)
  Pallas kernels: 340 us -> 274 us
  local copies, waits for them, and re-layouts: 74.1 us -> 36.8 us
    pallas_call x1, Pallas kernels: 169 us -> 121 us  [reduce_wires(): pl.pallas_call(reduce_kernel, in_specs=[hbm] * 5 + [vmem], out_specs=[hbm...]
    reshape x8 -> x0, local copies, waits for them, and re-layouts: 26.4 us -> none  [the longest x3 14.1 us: fast_body(): qkv_grad = cat_sum[:, :, :3 * head_width].reshape(cores, shards, model_ro...]
    pallas_call x2, Pallas kernels: 157 us -> 138 us  [the longest x1 114 us: gather_wires(): pl.pallas_call(gather_kernel, in_specs=[hbm] * 4 + [vmem] * 3, out_specs=...]
    convert_element_type x6 -> x0, local copies, waits for them, and re-layouts: 8.38 us -> none  [the longest x2 3.39 us: fast_body(): qkv_pieces = qkv_weight_state[0].astype(jnp.bfloat16).reshape(model_rows,...]
    slice x4 -> x0, local copies, waits for them, and re-layouts: 5.92 us -> none  [the longest x1 1.7 us: fast_body(): up_weight_state[0].astype(jnp.bfloat16)]
    unnamed x79 -> x71, local copies, waits for them, and re-layouts: 15.6 us -> 19 us
where the time goes in v2:
time: 403 us; the launch traced here: 396 us
  Pallas kernels  274 us (68%)
  matrix products  64.8 us (16%)
  local copies, waits for them, and re-layouts  36.8 us (9%)
  other arithmetic  18 us (4%)
    pallas_call x1, Pallas kernels, reduce_wires(): pl.pallas_call(reduce_kernel, in_specs=[hbm] * 5 + [vmem], out_specs=[hbm...  121 us
    pallas_call x1, Pallas kernels, gather_wires(): pl.pallas_call(gather_kernel, in_specs=[hbm] * 4 + [vmem] * 3, out_specs=...  114 us
    pallas_call x1, Pallas kernels, owner_update(): pl.pallas_call(partial(owner_update_kernel, plan, small_plan, groups), gr...  24.1 us
    unnamed x71, local copies, waits for them, and re-layouts  19 us
    pallas_call x1, Pallas kernels, attention(): pl.pallas_call(attention_kernel, grid=(count,), in_specs=[pl.BlockSpec((r...  14.9 us
    dot_general x1, matrix products, fast_body(): norm_part = jnp.dot(dcat, cat_w.T, preferred_element_type=jnp.float32)  14.4 us
    slice x3, local copies, waits for them, and re-layouts, owner_update(): out.reshape(1, 1, out_rows * 128)[:, :, :entries]  13.9 us
    dot_general x1, matrix products, fast_body(): fu = jnp.dot(norm_bf, cat_w, preferred_element_type=jnp.float32) + cat_bias  11.8 us

profile of v2, /device:TPU:0, one launch (start us, length us, event | category | flops | bytes accessed | tf_op | source)
XLA Modules:
  0.0 395.6 jit_solution(16320089283343310768)
XLA Ops:
  0.6 0.7 convert_bitcast_fusion.1
  1.3 0.7 slice_multiply_fusion
  2.1 0.8 slice_multiply_fusion.2
  2.9 0.8 slice_multiply_fusion.4
  3.8 2.8 copy-done.2
  6.6 2.3 copy-done.3
  8.9 1.0 copy-done.4
  10.0 1.4 copy-done.6
  11.4 1.0 copy-done.7
  12.4 113.8 %shard_map.193 = (bf16[4,8,64,1792]{3,2,1,0:T(8,128)(2,1)}, bf16[4,64,2048]{2,1,0:T(8,128)(2,1)S(1)}, bf16[4,256,2048]{2,1,0:T(8,128)(2,1)S(1)}, bf16[8,128,2048...) custom-call(f32[3,64,6144]{2,1,0:T(8,128)S(1)} %copy-done.3, ...), custom_call_target="tpu_custom_call" | custom-call | tf_op jit(solution)/shard_map/pallas_call | solution.py:991
  126.2 2.0 copy-done.12
  128.3 0.6 convert_reduce_fusion
  128.9 1.2 multiply_reduce_fusion.1
  130.1 0.2 copy-done
  130.3 1.3 copy-done.9
  131.9 0.2 slice_reduce_fusion.2
  132.2 4.6 %add_convert_fusion.1 = bf16[8,128,2048]{2,1,0:T(8,128)(2,1)} fusion(bf16[8,128,2048]{2,1,0:T(8,128)(2,1)} %copy-done, f32[2048]{0:T(1024)S(1)} %add.217, f32[2048]{0:T(1024)S(1)} %mul.297, f32[8,128]{1,0:T(8,128)S(1)} %get-tuple-element.90, f32[8,128]{1,0:T(8,128)S(1)} %get-tuple-element.93), kind=kLoop, calls=%fused_computation.4 | loop fusion | flops 12582912 | bytes 8413184 | tf_op jit(solution)/shard_map/convert_element_type | solution.py:1359
  137.2 11.8 %convolution_add_fusion.fu_ref = f32[1024,1792]{1,0:T(8,128)S(1)} fusion(bf16[1024,2048]{1,0:T(8,128)(2,1)} %bitcast.122, bf16[2048,1792]{1,0:T(8,128)(2,1)} %bitcast.144, f32[1792]{0:T(1024)S(1)} %pad_maximum_fusion.1), kind=kOutput, calls=%fused_computation.19 | convolution fusion | flops 7518027776 | bytes 18881536 | tf_op jit(solution)/shard_map/dot_general | solution.py:1361
  149.0 2.2 convolution_convert_fusion.3.do_ref
  151.2 1.8 copy-done.16
  153.0 1.1 copy-done.10
  154.0 8.9 %fusion.43 = (f32[1024]{0:T(1024)S(1)}, bf16[1024,1024]{1,0:T(8,128)(2,1)}) fusion(f32[1024,1792]{1,0:T(8,128)S(1)} %convolution_add_fusion.fu_ref, bf16[1024,2048]{1,0:T(8,128)(2,1)S(1)} %bitcast.106, bf16[1024,2048]{1,0:T(8,128)(2,1)S(1)} %bitcast.103), kind=kOutput, calls=%fused_computation.136 | convolution fusion | flops 4321180672 | bytes 14684160 | tf_op jit(solution)/shard_map/dot_general | solution.py:1364
  163.0 1.0 copy.31.seg_col_ref
  164.1 1.9 fusion.17
  166.0 14.9 %shard_map.194 = (bf16[1024,256]{1,0:T(8,128)(2,1)}, bf16[1024,1792]{1,0:T(8,128)(2,1)}, f32[2,1,768]{2,1,0:T(1,128)}) custom-call(f32[1024,1792]{1,0:T(8,128)} %copy-done.16, bf16[1024,256]{1,0:T(8,128)(2,1)} %convolution_convert_fusion.3.do_ref, bf16[1024,1024]{1,0:T(8,128)(2,1)} %get-tuple-element.70.du_ref, s32[1024,1]{1,0:T(8,128)} %copy.31.seg_col_ref, ...), custom_call_target="tpu_custom_call" | custom-call | flops 1342177280 | bytes 9437184 | tf_op jit(solution)/shard_map/pallas_call | solution.py:506
  180.9 14.4 %fusion.39 = (f32[2048]{0:T(1024)S(1)}, f32[2048]{0:T(1024)S(1)}, bf16[1024,2048]{1,0:T(8,128)(2,1)}, bf16[1024,2048]{1,0:T(8,128)(2,1)S(1)}) fusion(f32[1024]{0:T(1024)S(1)} %get-tuple-element.91, f32[1024]{0:T(1024)S(1)} %get-tuple-element.92, bf16[8,128,2048]{2,1,0:T(8,128)(2,1)S(1)} %copy-done.1, f32[2048]{0:T(1024)S(1)} %add.217, f32[2048]{0:T(1024)S(1)} %mul.297, ...), kind=kOutput, calls=%fused_computation.135 | convolution fusion | flops 7537160192 | bytes 23633920 | tf_op jit(solution)/shard_map/dot_general | solution.py:1376
  195.4 10.2 %convolution_convert_fusion = bf16[2048,1792]{1,0:T(8,128)(2,1)} fusion(bf16[1024,2048]{1,0:T(8,128)(2,1)S(1)} %get-tuple-element.72, bf16[1024,1792]{1,0:T(8,128)(2,1)S(1)} %copy-done.25), kind=kOutput, calls=%fused_computation.8 | convolution fusion | flops 7519862784 | bytes 15204352 | tf_op jit(solution)/shard_map/dot_general | solution.py:1375
  205.6 2.2 convolution_convert_fusion.2
  207.8 7.0 %convolution_convert_fusion.1 = bf16[1024,2048]{1,0:T(8,128)(2,1)} fusion(bf16[1024,2048]{1,0:T(8,128)(2,1)S(1)} %bitcast.108, f32[1024,1792]{1,0:T(8,128)S(1)} %bitcast.112), kind=kOutput, calls=%fused_computation.20 | convolution fusion | flops 4306501632 | bytes 12582912 | tf_op jit(solution)/shard_map/dot_general | solution.py:1373
  214.8 4.8 %fusion.38 = f32[1024,2048]{1,0:T(8,128)S(1)} fusion(bf16[1024,2048]{1,0:T(8,128)(2,1)S(1)} %bitcast.104, f32[1024,1792]{1,0:T(8,128)S(1)} %bitcast.112), kind=kOutput, calls=%fused_computation.134 | convolution fusion | flops 4304404480 | bytes 16777216 | tf_op jit(solution)/shard_map/dot_general | solution.py:1371
  219.7 3.3 add_convert_fusion
  223.1 0.6 pad_bitcast_fusion.sums
  223.8 121.5 %shard_map.195 = (bf16[8,64,1792]{2,1,0:T(8,128)(2,1)}, f32[64,2048]{1,0:T(8,128)}, f32[256,2048]{1,0:T(8,128)}, f32[128,2048]{1,0:T(8,128)}, f32[128,2048]{1,0:T(8,128)}, /*index=5*/f32[8,64,128]{2,1,0:T(8,128)}) custom-call(bf16[4,8,64,1792]{3,2,1,0:T(8,128)(2,1)} %bitcast.110, bf16[4,64,2048]{2,1,0:T(8,128)(2,1)} %bitcast.123, ...), custom_call_target="tpu_custom_call" | custom-call | tf_op jit(solution)/shard_map/pallas_call | solution.py:1242
  345.3 0.2 convert_reduce_fusion.1
  345.4 0.3 fusion.13
  345.7 1.6 multiply_reduce_fusion.2
  347.5 3.3 fusion.14
  351.1 0.1 mul.368
  351.8 0.1 mul.372
  352.6 0.6 pad_maximum_fusion.refs_7_
  353.2 24.1 %shard_map.196 = (f32[12296,128]{1,0:T(8,128)}, f32[12296,128]{1,0:T(8,128)}, f32[12296,128]{1,0:T(8,128)}, f32[64,6144]{1,0:T(8,128)}, f32[64,8192]{1,0:T(8,128)}) custom-call(f32[3,64,6144]{2,1,0:T(8,128)} %refs_0_.1, f32[3,64,2048]{2,1,0:T(8,128)} %refs_1_.1, f32[3,64,8192]{2,1,0:T(8,128)} %refs_2_.1, f32[3,256,2048]{2,1,0:T(8,128)} %refs_3_.1, ...), custom_call_target="tpu_custom_call" | custom-call | flops 31471360 | bytes 44059904 | tf_op jit(solution)/shard_map/pallas_call | solution.py:695
  377.3 7.7 %slice.134 = f32[1,1,1573568]{2,1,0:T(1,128)} slice(f32[1,1,1573888]{2,1,0:T(1,128)} %bitcast.119), slice={[0:1], [0:1], [0:1573568]} | slice | bytes 12588544 | tf_op jit(solution)/shard_map/slice | solution.py:715
  385.0 3.3 slice.135
  388.3 1.1 slice-done.2
  389.4 0.7 slice-done.3
  390.1 2.9 slice.136
  393.0 0.8 copy.47
  393.8 1.3 copy.48
  (119 shorter events, 2.8 us)
Async XLA Ops:
  3.8 2.8 copy-start.2
  6.6 2.3 copy-start.3
  8.9 1.0 copy-start.4
  10.0 1.4 copy-start.6
  11.4 1.0 copy-start.7
  126.2 2.0 copy-start.12
  128.2 2.0 copy-start
  128.3 3.4 copy-start.9
  137.2 11.8 %copy-start.13 = (bf16[8,128,2048]{2,1,0:T(8,128)(2,1)S(1)}, bf16[8,128,2048]{2,1,0:T(8,128)(2,1)}, u32[]{:S(2)}) copy-start(bf16[8,128,2048]{2,1,0:T(8,128)(2,1)} %copy-done.12) | copy-start | bytes 12582916
  149.0 4.0 %copy-start.16 = (f32[1024,1792]{1,0:T(8,128)}, f32[1024,1792]{1,0:T(8,128)S(1)}, u32[]{:S(2)}) copy-start(f32[1024,1792]{1,0:T(8,128)S(1)} %convolution_add_fusion.fu_ref) | copy-start | bytes 22020100
  149.0 5.0 %copy-start.10 = (bf16[4,256,2048]{2,1,0:T(8,128)(2,1)S(1)}, bf16[4,256,2048]{2,1,0:T(8,128)(2,1)}, u32[]{:S(2)}) copy-start(bf16[4,256,2048]{2,1,0:T(8,128)(2,1)} %copy-done.9) | copy-start | bytes 12582916
  163.0 3.0 copy-start.20
  166.0 14.9 %copy-start.1 = (bf16[8,128,2048]{2,1,0:T(8,128)(2,1)S(1)}, bf16[8,128,2048]{2,1,0:T(8,128)(2,1)}, u32[]{:S(2)}) copy-start(bf16[8,128,2048]{2,1,0:T(8,128)(2,1)} %copy-done) | copy-start | bytes 12582916
  180.9 14.5 %copy-start.25 = (bf16[1024,1792]{1,0:T(8,128)(2,1)S(1)}, bf16[1024,1792]{1,0:T(8,128)(2,1)}, u32[]{:S(2)}) copy-start(bf16[1024,1792]{1,0:T(8,128)(2,1)} %get-tuple-element.38) | copy-start | bytes 11010052
  195.4 12.5 %slice-start = ((s8[7340032]{0:T(1024)(128)(4,1)}), s8[4194304]{0:T(1024)(128)(4,1)S(1)}, s32[]{:S(2)}) async-start(s8[7340032]{0:T(1024)(128)(4,1)} %bitcast.111), calls=%async_computation | async-start | bytes 8388608
  195.4 10.2 %copy-start.14 = (bf16[8,128,2048]{2,1,0:T(8,128)(2,1)S(1)}, bf16[8,128,2048]{2,1,0:T(8,128)(2,1)}, u32[]{:S(2)}) copy-start(bf16[8,128,2048]{2,1,0:T(8,128)(2,1)} %copy-done.12) | copy-start | bytes 12582916
  195.4 10.2 %copy-start.18 = (bf16[1024,256]{1,0:T(8,128)(2,1)S(1)}, bf16[1024,256]{1,0:T(8,128)(2,1)}, u32[]{:S(2)}) copy-start(bf16[1024,256]{1,0:T(8,128)(2,1)} %get-tuple-element.39) | copy-start | bytes 1572868
  195.4 12.5 %slice-start.1 = ((s8[7340032]{0:T(1024)(128)(4,1)}), s8[3145728]{0:T(1024)(128)(4,1)S(1)}, s32[]{:S(2)}) async-start(s8[7340032]{0:T(1024)(128)(4,1)} %bitcast.111), calls=%async_computation.1 | async-start | bytes 6291456
  207.8 7.0 %copy-start.11 = (bf16[4,256,2048]{2,1,0:T(8,128)(2,1)S(1)}, bf16[4,256,2048]{2,1,0:T(8,128)(2,1)}, u32[]{:S(2)}) copy-start(bf16[4,256,2048]{2,1,0:T(8,128)(2,1)} %copy-done.9) | copy-start | bytes 12582916
  219.7 3.3 copy-start.22
  219.7 3.4 copy-start.8
  223.8 121.5 %copy-start.5 = (bf16[1,128,2048]{2,1,0:T(8,128)(2,1)S(1)}, bf16[1,128,2048]{2,1,0:T(8,128)(2,1)}, u32[]{:S(2)}) copy-start(bf16[1,128,2048]{2,1,0:T(8,128)(2,1)} %param.10) | copy-start | bytes 1572868
  345.3 6.0 %copy-start.19 = (f32[8,64,128]{2,1,0:T(8,128)S(1)}, f32[8,64,128]{2,1,0:T(8,128)}, u32[]{:S(2)}) copy-start(f32[8,64,128]{2,1,0:T(8,128)} %get-tuple-element.46) | copy-start | bytes 786436
  351.5 25.7 %copy-start.21 = (f32[64,4]{0,1:T(4,128)}, f32[64,4]{0,1:T(4,128)S(1)}, u32[]{:S(2)}) copy-start(f32[64,4]{0,1:T(4,128)S(1)} %pad_maximum_fusion.2) | copy-start | bytes 3076
  352.0 25.2 %copy-start.23 = (f32[1,1,256]{2,1,0:T(1,128)}, f32[1,1,256]{2,1,0:T(1,128)S(1)}, u32[]{:S(2)}) copy-start(f32[1,1,256]{2,1,0:T(1,128)S(1)} %constant_dynamic-slice_fusion.3) | copy-start | bytes 3076
  352.3 24.9 %copy-start.24 = (f32[1,192]{1,0:T(1,128)}, f32[1,192]{1,0:T(1,128)S(1)}, u32[]{:S(2)}) copy-start(f32[1,192]{1,0:T(1,128)S(1)} %constant_dynamic-slice_fusion.4) | copy-start | bytes 2308
  377.3 7.7 %slice-start.4 = ((s8[6295552]{0:T(1024)(128)(4,1)}), s8[4194304]{0:T(1024)(128)(4,1)S(1)}, s32[]{:S(2)}) async-start(s8[6295552]{0:T(1024)(128)(4,1)} %bitcast.116), calls=%async_computation.4 | async-start | bytes 8388608
  377.3 7.7 %slice-start.5 = ((s8[6295552]{0:T(1024)(128)(4,1)}), s8[2101248]{0:T(1024)(128)(4,1)S(1)}, s32[]{:S(2)}) async-start(s8[6295552]{0:T(1024)(128)(4,1)} %bitcast.116), calls=%async_computation.5 | async-start | bytes 4202496
  385.0 4.4 %slice-start.2 = ((s8[6295552]{0:T(1024)(128)(4,1)}), s8[4194304]{0:T(1024)(128)(4,1)S(1)}, s32[]{:S(2)}) async-start(s8[6295552]{0:T(1024)(128)(4,1)} %bitcast.113), calls=%async_computation.2 | async-start | bytes 8388608
  385.0 5.1 %slice-start.3 = ((s8[6295552]{0:T(1024)(128)(4,1)}), s8[2101248]{0:T(1024)(128)(4,1)S(1)}, s32[]{:S(2)}) async-start(s8[6295552]{0:T(1024)(128)(4,1)} %bitcast.113), calls=%async_computation.3 | async-start | bytes 4202496
  390.1 2.9 copy-start.17
  390.1 3.7 copy-start.15

commit v3 on v2

--- a/solution.py
+++ b/solution.py
@@ -1020,7 +1020,7 @@
             dma((6,)),
         ],
         compiler_params=pltpu.CompilerParams(
-            collective_id=0, has_side_effects=True, vmem_limit_bytes=24 << 20
+            collective_id=0, has_side_effects=True, vmem_limit_bytes=67043328
         ),
     )(qkv, up, dense, down, tokens, cotangent, vectors)
 
@@ -1040,223 +1040,357 @@
     lax.fori_loop(0, rows // step, body, 0)
 
 
+def chunked(first, last, copies_of, body):
+    for copy in copies_of(first, first % 2):
+        copy.start()
+
+    def step(n, carry):
+        slot = lax.rem(n, 2)
+
+        @pl.when(n + 1 < last)
+        def ahead():
+            for copy in copies_of(n + 1, 1 - slot):
+                copy.start()
+
+        for copy in copies_of(n, slot):
+            copy.wait()
+        body(n, slot)
+        return carry
+
+    lax.fori_loop(first, last, step, 0)
+
+
 def reduce_kernel(
-    cat, dense, down, out_part, norm_part, sums,
+    norm, dcat, x_all, mean, inverse, attn, hidden, dy, cat_w, dense_w, down_w, sums,
     cat_out, dense_out, down_out, mixed_out, norm_out, sums_out,
-    cat_buf, down_buf, dense_buf, token_buf, sum_buf,
-    send_sems, near_sem, pass_sem, group_sem, core_sem, line_sem, sum_sem, local_sem,
+    cat_part, down_part, dense_part, cat_in, down_in, dense_in,
+    tokens, token_in, token_line, token_last, sum_buf,
+    wide, attn_turned, norm_chunk, norm_turned, cat_chunk, x_chunk, down_chunk, dense_chunk, dy_chunk,
+    send_sems, near_sem, pass_sem, group_sem, core_sem, line_sem, sum_sem, local_sem, chunk_sem,
 ):
-    PASS_IN, PASS_OWN, PASS_OUT, KEEP_IN, KEEP_OWN, LAST_IN = range(6)
+    PASS, KEEP, LAST = range(3)
     net = Wires(send_sems)
     plane, core, shard, shards, group, mine = net.plane, net.core, net.shard, net.shards, net.group, net.mine
+    planes = cat_part.shape[0]
     partner = (plane, 1 - core, shard)
     order = sorted(range(group), key=lambda mask: (mask % shards, mask // shards), reverse=True)
-
-    units = []
-    for mask in order:
-        units.append((lambda p, mask=mask: cat.at[p, mine ^ mask], cat_buf, mask))
-    down_rows = down.shape[1] // 4
-    for part in range(4):
-        rows = pl.ds(part * down_rows, down_rows)
-        units.append((lambda p, rows=rows: down.at[p, rows], down_buf, part))
-    dense_rows = dense.shape[1] // 2
-    for part in range(2):
-        rows = pl.ds(part * dense_rows, dense_rows)
-        units.append((lambda p, rows=rows: dense.at[p, rows], dense_buf, part))
+    rows, width = dcat.shape
+    model = norm.shape[1]
+    block = cat_part.shape[2]
+    token_rows = tokens.shape[2]
+    units_here = hidden.shape[1]
+    heads_here = attn.shape[1]
+    lane = 256
+
+    def dot(a, b, a_dim=1, b_dim=0):
+        return lax.dot_general(a, b, (((a_dim,), (b_dim,)), ((), ())), preferred_element_type=jnp.float32)
+
+    def columns(n):
+        return pl.ds(pl.multiple_of(n * lane, lane), lane)
+
+    units = [(cat_part, cat_in, mask) for mask in order]
+    units += [(down_part, down_in, part) for part in range(down_part.shape[1])]
+    units += [(dense_part, dense_in, part) for part in range(dense_part.shape[1])]
+    down_rows, dense_rows = down_part.shape[2], dense_part.shape[2]
 
     def ways(index):
-        if index % 2 == 0:
-            return net.first, net.second, plane ^ 1, plane ^ 2
-        return net.second, net.first, plane ^ 2, plane ^ 1
-
-    loads = {}
-
-    def load(key, source, target):
-        loads[key] = pltpu.make_async_copy(source, target, local_sem.at[len(loads)])
-        loads[key].start()
-
-    streams = (out_part, norm_part)
-    finals = (mixed_out, norm_out)
-    TOKEN_IN, TOKEN_OWN, TOKEN_UP, TOKEN_LOW, TOKEN_SUM = range(5)
-
-    for stream in range(2):
-        for place in range(shards):
-            load(
-                ("token", stream, place),
-                streams[stream].at[core * shards + place],
-                token_buf.at[TOKEN_OWN, stream, place],
+        return (net.first, net.second, 1, 2) if index % 2 == 0 else (net.second, net.first, 2, 1)
+
+    def send_pass(index):
+        parts, came, slot = units[index]
+        net.send(parts.at[3, slot], came.at[PASS, slot], pass_sem.at[0, index], ways(index)[0])
+
+    def send_keep(index):
+        parts, came, slot = units[index]
+        near, far, near_mask, far_mask = ways(index)
+        net.send(parts.at[near_mask, slot], came.at[KEEP, slot], near_sem.at[index], near)
+
+    locals_ = {}
+
+    def local(key, source, target):
+        locals_[key] = pltpu.make_async_copy(source, target, local_sem.at[len(locals_)])
+        locals_[key].start()
+
+    local("dcat", dcat, wide.at[:, pl.ds(0, width)])
+    net.barrier()
+
+    plane_rows = group * block
+
+    def norm_copy(turn, distance):
+        place = pl.ds(pl.multiple_of((plane ^ distance) * plane_rows, plane_rows), plane_rows)
+        return pltpu.make_async_copy(
+            norm.at[:, place], norm_chunk.at[turn % 2], chunk_sem.at[0, turn % 2]
+        )
+
+    cats, every = range(group), range(len(units))
+    turns = (3, 1, 2, 0)
+    norm_copy(0, turns[0]).start()
+    locals_["dcat"].wait()
+    for turn, distance in enumerate(turns):
+        if turn + 1 < planes:
+            norm_copy(turn + 1, turns[turn + 1]).start()
+        norm_copy(turn, distance).wait()
+        norm_turned[...] = norm_chunk[turn % 2].T
+
+        def cat_step(n, carry, distance=distance):
+            total = dot(norm_turned[...], wide[:, columns(n)]).astype(jnp.bfloat16)
+            for member in range(group):
+                cat_part[distance, mine ^ member, :, columns(n)] = total[member * block : (member + 1) * block]
+            return carry
+
+        lax.fori_loop(0, width // lane, cat_step, 0)
+        for index in cats:
+            if distance == 3:
+                send_pass(index)
+            elif distance == ways(index)[2]:
+                send_keep(index)
+
+    sum_buf[4] = sums[...]
+    gain_row = width // 128
+
+    def norm_copies(n, slot):
+        return [
+            pltpu.make_async_copy(cat_w.at[columns(n), :], cat_chunk.at[slot], chunk_sem.at[1, slot]),
+            pltpu.make_async_copy(x_all.at[:, columns(n)], x_chunk.at[slot], chunk_sem.at[2, slot]),
+        ]
+
+    def norm_step(n, slot):
+        total = dot(wide[:, pl.ds(0, width)], cat_chunk[slot], 1, 1)
+        x_hat = (x_chunk[slot].astype(jnp.float32) - mean[...]) * inverse[...]
+        gain = jnp.sum(total * x_hat, axis=0, keepdims=True)
+        shift = jnp.sum(total, axis=0, keepdims=True)
+        for half in range(lane // 128):
+            row = gain_row + n * (lane // 128) + half
+            sum_buf[4, pl.ds(row, 1), :] = gain[:, half * 128 : (half + 1) * 128]
+            sum_buf[4, pl.ds(row + model // 128, 1), :] = shift[:, half * 128 : (half + 1) * 128]
+        for member in range(group):
+            tokens[1, member, :, columns(n)] = total[member * token_rows : (member + 1) * token_rows].astype(
+                jnp.bfloat16
             )
-    for index, (part, buffers, slot) in enumerate(units):
-        near, far, near_plane, far_plane = ways(index)
-        load(("pass", index), part(far_plane), buffers.at[PASS_OWN, slot])
-    for index, (part, buffers, slot) in enumerate(units):
-        load(("keep", index), part(plane), buffers.at[KEEP_OWN, slot])
-
-    net.barrier()
-
-    def start_unit(index):
-        part, buffers, slot = units[index]
-        near, far, near_plane, far_plane = ways(index)
-        net.send(part(plane ^ 3), buffers.at[PASS_IN, slot], pass_sem.at[0, index], near)
-        net.send(part(near_plane), buffers.at[KEEP_IN, slot], near_sem.at[index], near)
-
-    net.send(sums, sum_buf.at[0], sum_sem.at[0], net.first)
+
+    chunked(0, model // lane, norm_copies, norm_step)
+
     places = [place for rank in range(shards // 2) for place in (shards - 1 - rank, rank)]
-    for place in places:
-        for stream in range(2):
+
+    def to_partner(stream):
+        for place in places:
             net.send(
-                streams[stream].at[(1 - core) * shards + place],
-                token_buf.at[TOKEN_IN, stream, place],
+                tokens.at[stream, (1 - core) * shards + place],
+                token_in.at[stream, place],
                 core_sem.at[stream, place],
                 partner,
             )
-    for index in range(group):
-        start_unit(index)
+
+    net.send(sum_buf.at[4], sum_buf.at[0], sum_sem.at[0], net.first)
+    to_partner(1)
+
+    local("hidden", hidden, wide.at[:, pl.ds(0, units_here)])
+    local("attn", attn, wide.at[:, pl.ds(2 * units_here, heads_here)])
+
+    def own(stream, place):
+        return tokens.at[stream, core * shards + place]
 
     def chain(stream, hop, rank):
         for upward in (True, False):
             target = shards - 1 - rank if upward else rank
             here = hop if upward else shards - 1 - hop
-            slot, sems = (TOKEN_UP, line_sem.at[0]) if upward else (TOKEN_LOW, line_sem.at[1])
-            values = [token_buf.at[TOKEN_IN, stream, target], token_buf.at[TOKEN_OWN, stream, target]]
-            came = token_buf.at[slot, stream, target]
-            total = token_buf.at[TOKEN_SUM, stream, target]
+            sems = line_sem.at[0 if upward else 1]
+            came = token_line.at[stream, target]
+            total = own(stream, target)
             holds = shard == here
             if hop:
                 net.arrived(came, sems.at[stream, target], holds)
 
             @pl.when(holds)
-            def add(values=values, came=came, total=total):
-                add_rows(total, *(values + ([came] if hop else [])))
+            def add(target=target, came=came, total=total):
+                add_rows(total, total, token_in.at[stream, target], *([came] if hop else []))
 
             there = jnp.clip(shard + (1 if upward else -1), 0, shards - 1)
-            net.send(total, came, sems.at[stream, target], (plane, core, there), holds)
+            ends = (not upward) and rank == shards - 2 - hop
+            landing = token_last.at[stream] if ends else came
+            net.send(total, landing, sems.at[stream, target], (plane, core, there), holds)
 
     def final(stream):
         for place in range(shards):
             holds = shard == place
-            values = [token_buf.at[TOKEN_IN, stream, place], token_buf.at[TOKEN_OWN, stream, place]]
-            for slot, side, present in (
-                (TOKEN_UP, line_sem.at[0], place > 0),
-                (TOKEN_LOW, line_sem.at[1], place < shards - 1),
+            values = [own(stream, place), token_in.at[stream, place]]
+            for landing, side, present in (
+                (token_line.at[stream, place], line_sem.at[0], place > 0),
+                (token_last.at[stream], line_sem.at[1], place < shards - 1),
             ):
                 if present:
-                    values.append(token_buf.at[slot, stream, place])
-                    net.arrived(token_buf.at[slot, stream, place], side.at[stream, place], holds)
+                    values.append(landing)
+                    net.arrived(landing, side.at[stream, place], holds)
 
             @pl.when(holds)
             def add(values=values):
-                add_rows(finals[stream], *values)
+                add_rows((mixed_out, norm_out)[stream], *values)
+
+    locals_["hidden"].wait()
+    locals_["attn"].wait()
+    turned = pl.ds(units_here, rows)
+    wide[:, turned] = wide[:, pl.ds(0, units_here)].T
+    attn_turned[...] = wide[:, pl.ds(2 * units_here, heads_here)].T
+
+    def out_copies(n, slot):
+        return [
+            pltpu.make_async_copy(down_w.at[:, columns(n)], down_chunk.at[slot], chunk_sem.at[3, slot]),
+            pltpu.make_async_copy(dense_w.at[:, columns(n)], dense_chunk.at[slot], chunk_sem.at[4, slot]),
+            pltpu.make_async_copy(dy.at[:, columns(n)], dy_chunk.at[slot], chunk_sem.at[5, slot]),
+        ]
+
+    def out_step(n, slot):
+        total = dot(wide[:, pl.ds(0, units_here)], down_chunk[slot]) + dot(
+            wide[:, pl.ds(2 * units_here, heads_here)], dense_chunk[slot]
+        )
+        for member in range(group):
+            tokens[0, member, :, columns(n)] = total[member * token_rows : (member + 1) * token_rows].astype(
+                jnp.bfloat16
+            )
+        for parts, left in ((down_part, wide[:, turned]), (dense_part, attn_turned[...])):
+            grad = dot(left, dy_chunk[slot]).astype(jnp.bfloat16)
+            pieces, size = parts.shape[1], parts.shape[2]
+            for q in range(planes):
+                for piece in range(pieces):
+                    start = (q * pieces + piece) * size
+                    parts[plane ^ q, piece, :, columns(n)] = grad[start : start + size]
+
+    half = model // lane // 2
+    chunked(0, half, out_copies, out_step)
+    for place in places:
+        net.arrived(token_in.at[1, place], core_sem.at[1, place])
+    for rank in range(shards - 1):
+        chain(1, 0, rank)
+    chunked(half, 2 * half, out_copies, out_step)
+    to_partner(0)
 
     def pass_on(index):
-        part, buffers, slot = units[index]
-        near, far, near_plane, far_plane = ways(index)
-        net.arrived(buffers.at[PASS_IN, slot], pass_sem.at[0, index])
-        loads["pass", index].wait()
-        add_rows(buffers.at[PASS_OUT, slot], buffers.at[PASS_IN, slot], buffers.at[PASS_OWN, slot])
-        net.send(buffers.at[PASS_OUT, slot], buffers.at[LAST_IN, slot], pass_sem.at[1, index], far)
+        parts, came, slot = units[index]
+        near, far, near_mask, far_mask = ways(index)
+        total = parts.at[far_mask, slot]
+        net.arrived(came.at[PASS, slot], pass_sem.at[0, index])
+        add_rows(total, total, came.at[PASS, slot])
+        net.send(total, came.at[LAST, slot], pass_sem.at[1, index], far)
 
     def finish(index):
-        part, buffers, slot = units[index]
-        net.arrived(buffers.at[KEEP_IN, slot], near_sem.at[index])
-        loads["keep", index].wait()
-        net.arrived(buffers.at[LAST_IN, slot], pass_sem.at[1, index])
-        values = (buffers.at[KEEP_IN, slot], buffers.at[KEEP_OWN, slot], buffers.at[LAST_IN, slot])
+        parts, came, slot = units[index]
+        total = parts.at[0, slot]
+        net.arrived(came.at[KEEP, slot], near_sem.at[index])
+        net.arrived(came.at[LAST, slot], pass_sem.at[1, index])
+        values = (total, came.at[KEEP, slot], came.at[LAST, slot])
         if index < group:
-            add_rows(buffers.at[KEEP_OWN, slot], *values)
+            add_rows(total, *values)
             if slot:
-                net.send(
-                    buffers.at[KEEP_OWN, slot],
-                    cat_out.at[mine],
-                    group_sem.at[0, slot],
-                    net.member(mine ^ slot),
-                )
+                net.send(total, cat_out.at[mine], group_sem.at[0, slot], net.member(mine ^ slot))
             else:
-                load("own", buffers.at[KEEP_OWN, slot], cat_out.at[mine])
-        elif index < group + 4:
+                local("own", total, cat_out.at[mine])
+        elif parts is down_part:
             add_rows(down_out.at[pl.ds(slot * down_rows, down_rows)], *values)
         else:
             add_rows(dense_out.at[pl.ds(slot * dense_rows, dense_rows)], *values)
 
+    for index in every[group:]:
+        send_pass(index)
+        send_keep(index)
+    net.arrived(sum_buf.at[0], sum_sem.at[0])
+    sum_buf[1] = sum_buf[4] + sum_buf[0]
+    net.send(sum_buf.at[1], sum_buf.at[2], sum_sem.at[1], net.second)
+    for index in cats[:2]:
+        pass_on(index)
     for place in places:
-        for stream in range(2):
-            net.arrived(token_buf.at[TOKEN_IN, stream, place], core_sem.at[stream, place])
-            loads["token", stream, place].wait()
+        net.arrived(token_in.at[0, place], core_sem.at[0, place])
     for rank in range(shards - 1):
-        for stream in range(2):
-            chain(stream, 0, rank)
-    net.arrived(sum_buf.at[0], sum_sem.at[0])
-    sum_buf[1] = sums[...] + sum_buf[0]
-    net.send(sum_buf.at[1], sum_buf.at[2], sum_sem.at[1], net.second)
+        chain(0, 0, rank)
     later = [
         (stream, hop, rank)
         for hop, rank in sorted(
             ((hop, rank) for hop in range(1, shards - 1) for rank in range(shards - 1 - hop)),
             key=lambda pair: (pair[0] + 2 * pair[1], pair[0]),
         )
-        for stream in range(2)
+        for stream in (1, 0)
     ]
-    cats, every = range(group), range(len(units))
-    for index in cats:
-        if index == group - 2:
-            for other in every[group:]:
-                start_unit(other)
+    later.sort(key=lambda item: -item[0])
+    for index in cats[2:]:
         pass_on(index)
         if index % 2 and later:
             chain(*later.pop(0))
-            if later and index > 1:
-                chain(*later.pop(0))
     net.arrived(sum_buf.at[2], sum_sem.at[1])
     sum_buf[3] = sum_buf[1] + sum_buf[2]
     for mask in range(1, group):
         net.send(sum_buf.at[3], sums_out.at[mine], group_sem.at[1, mask], net.member(mine ^ mask))
-    load("sums", sum_buf.at[3], sums_out.at[mine])
+    local("sums", sum_buf.at[3], sums_out.at[mine])
     for index in cats[: group - 2]:
         finish(index)
         if later:
             chain(*later.pop(0))
+    while later:
+        chain(*later.pop(0))
     for index in every[group:]:
         pass_on(index)
     for index in cats[group - 2 :]:
         finish(index)
-    for stream in range(2):
+    for stream in (1, 0):
         final(stream)
     for index in every[group:]:
         finish(index)
     for mask in range(1, group):
         net.arrived(cat_out.at[mine ^ mask], group_sem.at[0, mask])
         net.arrived(sums_out.at[mine ^ mask], group_sem.at[1, mask])
-    loads["own"].wait()
-    loads["sums"].wait()
+    locals_["own"].wait()
+    locals_["sums"].wait()
     net.drain()
 
 
-def reduce_wires(cat, dense, down, out_part, norm_part, sums):
-    shards = lax.axis_size("shard")
+def reduce_wires(norm, dcat, x_all, mean, inverse, attn, hidden, dy, cat_w, dense_w, down_w, sums):
+    planes, shards = lax.axis_size("plane"), lax.axis_size("shard")
     group = lax.axis_size("core") * shards
     units = group + 6
+    rows, width = dcat.shape
+    model = norm.shape[1]
+    block = model // (planes * group)
+    unit_rows, head_rows = down_w.shape[0] // planes, dense_w.shape[0] // planes
+    token_rows = rows // group
     vmem = pl.BlockSpec(memory_space=pltpu.VMEM)
     hbm = pl.BlockSpec(memory_space=pl.ANY)
     dma = pltpu.SemaphoreType.DMA
-    tokens = out_part.shape[1:]
+    lane = 256
+
+    def scratch(*shape, dtype=jnp.bfloat16):
+        return pltpu.VMEM(shape, dtype)
+
     return pl.pallas_call(
         reduce_kernel,
-        in_specs=[hbm] * 5 + [vmem],
+        in_specs=[hbm] * 3 + [vmem] * 2 + [hbm] * 6 + [vmem],
         out_specs=[hbm] + [vmem] * 4 + [hbm],
         out_shape=[
-            jax.ShapeDtypeStruct(cat.shape[1:], cat.dtype),
-            jax.ShapeDtypeStruct(dense.shape[1:], jnp.float32),
-            jax.ShapeDtypeStruct(down.shape[1:], jnp.float32),
-            jax.ShapeDtypeStruct(tokens, jnp.float32),
-            jax.ShapeDtypeStruct(tokens, jnp.float32),
+            jax.ShapeDtypeStruct((group, block, width), jnp.bfloat16),
+            jax.ShapeDtypeStruct((head_rows, model), jnp.float32),
+            jax.ShapeDtypeStruct((unit_rows, model), jnp.float32),
+            jax.ShapeDtypeStruct((token_rows, model), jnp.float32),
+            jax.ShapeDtypeStruct((token_rows, model), jnp.float32),
             jax.ShapeDtypeStruct((group,) + sums.shape, sums.dtype),
         ],
         scratch_shapes=[
-            pltpu.VMEM((6, group) + cat.shape[2:], cat.dtype),
-            pltpu.VMEM((6, 4, down.shape[1] // 4, down.shape[2]), down.dtype),
-            pltpu.VMEM((6, 2, dense.shape[1] // 2, dense.shape[2]), dense.dtype),
-            pltpu.VMEM((5, 2, shards) + tokens, out_part.dtype),
-            pltpu.VMEM((4,) + sums.shape, sums.dtype),
+            scratch(planes, group, block, width),
+            scratch(planes, 4, unit_rows // 4, model),
+            scratch(planes, 2, head_rows // 2, model),
+            scratch(3, group, block, width),
+            scratch(3, 4, unit_rows // 4, model),
+            scratch(3, 2, head_rows // 2, model),
+            scratch(2, group, token_rows, model),
+            scratch(2, shards, token_rows, model),
+            scratch(2, shards, token_rows, model),
+            scratch(2, token_rows, model),
+            scratch(5, *sums.shape, dtype=jnp.float32),
+            scratch(rows, hidden.shape[1] + rows + attn.shape[1]),
+            scratch(attn.shape[1], rows),
+            scratch(2, rows, group * block),
+            scratch(group * block, rows),
+            scratch(2, lane, width),
+            scratch(2, rows, lane),
+            scratch(2, hidden.shape[1], lane),
+            scratch(2, attn.shape[1], lane),
+            scratch(2, rows, lane),
             dma((2 + 2 * shards + 2 * shards * (shards - 1) + 3 * units + 2 * (group - 1),)),
             dma((units,)),
             dma((2, units)),
@@ -1264,12 +1398,13 @@
             dma((2, shards)),
             dma((2, 2, shards)),
             dma((2,)),
-            dma((2 * units + 2 * shards + 2,)),
+            dma((5,)),
+            dma((6, 2)),
         ],
         compiler_params=pltpu.CompilerParams(
-            collective_id=1, has_side_effects=True, vmem_limit_bytes=58 << 20
+            collective_id=1, has_side_effects=True, vmem_limit_bytes=67043328
         ),
-    )(cat, dense, down, out_part, norm_part, sums)
+    )(norm, dcat, x_all, mean, inverse, attn, hidden, dy, cat_w, dense_w, down_w, sums)
 
 
 def fast_body(
@@ -1353,7 +1488,8 @@
     cat_bias = jnp.concatenate([qkv_bias, up_bias])
 
     x_float = x_all.astype(jnp.float32)
-    center = x_float - jnp.mean(x_float, axis=-1, keepdims=True)
+    x_mean = jnp.mean(x_float, axis=-1, keepdims=True)
+    center = x_float - x_mean
     inverse = lax.rsqrt(jnp.mean(center * center, axis=-1, keepdims=True) + norm_eps)
     x_hat = center * inverse
     norm_bf = (x_hat * norm_gain + norm_shift).astype(jnp.bfloat16)
@@ -1366,28 +1502,25 @@
     upb_part = jnp.sum(grad_pre, axis=0)
     grad_heads = jnp.dot(dy_all, dense_w.T, preferred_element_type=jnp.float32).astype(jnp.bfloat16)
     attn, dcat, qkvb_part = attention(fu, grad_heads, grad_pre.astype(jnp.bfloat16), segments)
-    out_part = (
-        jnp.dot(attn, dense_w, preferred_element_type=jnp.float32)
-        + jnp.dot(hidden, down_w, preferred_element_type=jnp.float32)
-    ).astype(jnp.bfloat16)
-    down_grad = jnp.dot(hidden.T, dy_all, preferred_element_type=jnp.float32).astype(jnp.bfloat16)
-    dense_grad = jnp.dot(attn.T, dy_all, preferred_element_type=jnp.float32).astype(jnp.bfloat16)
-    cat_grad = jnp.dot(norm_bf.T, dcat, preferred_element_type=jnp.float32).astype(jnp.bfloat16)
-    norm_part = jnp.dot(dcat, cat_w.T, preferred_element_type=jnp.float32)
-    gain_part = jnp.sum(norm_part * x_hat, axis=0)
-    shift_part = jnp.sum(norm_part, axis=0)
     bias_part = jnp.sum(cotangent.astype(jnp.float32), axis=0)
-    sums = [qkvb_part, upb_part, gain_part, shift_part, bias_part]
+    nothing = jnp.zeros((D,), jnp.float32)
+    sums = [qkvb_part, upb_part, nothing, nothing, bias_part]
     sum_sizes = [value.size for value in sums]
     sum_rows = -(-sum(sum_sizes) // 1024) * 8
     sums = jnp.pad(jnp.concatenate(sums), (0, sum_rows * 128 - sum(sum_sizes))).reshape(sum_rows, 128)
 
     cat_sum, dense_grad, down_grad, mixed, grad_norm, sums_all = reduce_wires(
-        cat_grad.reshape(planes, group, model_rows, 3 * head_width + unit_width),
-        dense_grad.reshape(planes, model_rows, D),
-        down_grad.reshape(planes, unit_rows, D),
-        out_part.reshape(group, tokens_here, D),
-        norm_part.astype(jnp.bfloat16).reshape(group, tokens_here, D),
+        norm_bf,
+        dcat,
+        x_all,
+        x_mean,
+        inverse,
+        attn,
+        hidden,
+        dy_all,
+        cat_w,
+        dense_w,
+        down_w,
         sums,
     )
 

time: 403 us -> 391 us (0.970); the launches traced: 396 us -> 390 us
  matrix products: 64.8 us -> 25.5 us
  Pallas kernels: 274 us -> 307 us
  other arithmetic: 18 us -> 28.9 us
  local copies, waits for them, and re-layouts: 36.8 us -> 27 us
    dot_general x6 -> x0, matrix products: 41.9 us -> none  [the longest x1 14.4 us: fast_body(): norm_part = jnp.dot(dcat, cat_w.T, preferred_element_type=jnp.float32)]
    pallas_call x1, Pallas kernels: 121 us -> 154 us  [reduce_wires(): pl.pallas_call(reduce_kernel, in_specs=[hbm] * 3 + [vmem] * 2 + [hbm] * 6...]
    unnamed x71 -> x55, local copies, waits for them, and re-layouts: 19 us -> 4.45 us
    convert_element_type x1 -> x2, other arithmetic: 4.62 us -> 9.34 us  [fast_body(): norm_bf = (x_hat * norm_gain + norm_shift).astype(jnp.bfloat16)]
where the time goes in v3:
time: 391 us; the launch traced here: 390 us
  Pallas kernels  307 us (79%)
  other arithmetic  28.9 us (7%)
  local copies, waits for them, and re-layouts  27 us (7%)
  matrix products  25.5 us (7%)
    pallas_call x1, Pallas kernels, reduce_wires(): pl.pallas_call(reduce_kernel, in_specs=[hbm] * 3 + [vmem] * 2 + [hbm] * 6...  154 us
    pallas_call x1, Pallas kernels, gather_wires(): pl.pallas_call(gather_kernel, in_specs=[hbm] * 4 + [vmem] * 3, out_specs=...  114 us
    pallas_call x1, Pallas kernels, owner_update(): pl.pallas_call(partial(owner_update_kernel, plan, small_plan, groups), gr...  24 us
    pallas_call x1, Pallas kernels, attention(): pl.pallas_call(attention_kernel, grid=(count,), in_specs=[pl.BlockSpec((r...  15 us
    slice x3, local copies, waits for them, and re-layouts, owner_update(): out.reshape(1, 1, out_rows * 128)[:, :, :entries]  13.8 us
    dot_general x1, matrix products, fast_body(): fu = jnp.dot(norm_bf, cat_w, preferred_element_type=jnp.float32) + cat_bias  11.8 us
    dot_general x1, matrix products, fast_body(): grad_hidden = jnp.dot(dy_all, down_w.T, preferred_element_type=jnp.float32)  9.37 us
    convert_element_type x2, other arithmetic, fast_body(): norm_bf = (x_hat * norm_gain + norm_shift).astype(jnp.bfloat16)  9.34 us

profile of v3, /device:TPU:0, one launch (start us, length us, event | category | flops | bytes accessed | tf_op | source)
XLA Modules:
  0.0 389.8 jit_solution(4274993413847501036)
XLA Ops:
  0.6 1.3 slice_multiply_fusion
  2.1 1.4 slice_multiply_fusion.4
  3.4 1.4 slice_multiply_fusion.2
  4.8 0.7 convert_bitcast_fusion.1
  5.5 0.7 fusion.30.vectors
  6.2 114.3 %shard_map.193 = (bf16[4,8,64,1792]{3,2,1,0:T(8,128)(2,1)}, bf16[4,64,2048]{2,1,0:T(8,128)(2,1)}, bf16[4,256,2048]{2,1,0:T(8,128)(2,1)}, bf16[8,128,2048]{2,1,0:...) custom-call(f32[3,64,6144]{2,1,0:T(8,128)} %refs_0_.1, f32[3,64,8192]{2,1,0:T(8,128)} %refs_2_.1, ...), custom_call_target="tpu_custom_call" | custom-call | tf_op jit(solution)/shard_map/pallas_call | solution.py:991
  120.5 3.0 convert_reduce_fusion
  123.4 0.5 copy-done
  123.9 1.2 fusion.2
  125.3 0.1 reshape.323
  125.4 0.7 slice_reduce_fusion.2
  126.3 4.7 %fusion.5 = bf16[8,128,2048]{2,1,0:T(8,128)(2,1)} fusion(bf16[8,128,2048]{2,1,0:T(8,128)(2,1)} %get-tuple-element.32, f32[2048]{0:T(1024)S(1)} %add.219, f32[2048]{0:T(1024)S(1)} %mul.294, f32[8,128]{1,0:T(8,128)S(1)} %get-tuple-element.87, f32[8,128]{1,0:T(8,128)S(1)} %get-tuple-element.90), kind=kLoop, calls=%fused_computation.7 | loop fusion | flops 12582912 | bytes 8413184 | tf_op jit(solution)/shard_map/convert_element_type | solution.py:1495
  131.3 11.8 %convolution_add_fusion.fu_ref = f32[1024,1792]{1,0:T(8,128)S(1)} fusion(bf16[1024,2048]{1,0:T(8,128)(2,1)} %bitcast.97, bf16[2048,1792]{1,0:T(8,128)(2,1)} %bitcast.82, f32[1792]{0:T(1024)S(1)} %pad_maximum_fusion.1), kind=kOutput, calls=%fused_computation.19 | convolution fusion | flops 7518027776 | bytes 18881536 | tf_op jit(solution)/shard_map/dot_general | solution.py:1497
  143.2 9.4 %fusion.47 = (f32[1024]{0:T(1024)S(1)}, bf16[1024,1024]{1,0:T(8,128)(2,1)}, bf16[1024,1024]{1,0:T(8,128)(2,1)}) fusion(f32[1024,1792]{1,0:T(8,128)S(1)} %convolution_add_fusion.fu_ref, bf16[1024,2048]{1,0:T(8,128)(2,1)S(1)} %bitcast.96, bf16[1024,2048]{1,0:T(8,128)(2,1)S(1)} %bitcast.93), kind=kOutput, calls=%fused_computation.131 | convolution fusion | flops 4323277824 | bytes 16781312 | tf_op jit(solution)/shard_map/dot_general | solution.py:1500
  152.7 1.0 copy.33.seg_col_ref
  153.7 4.3 %convolution_convert_fusion.do_ref = bf16[1024,256]{1,0:T(8,128)(2,1)} fusion(bf16[1024,2048]{1,0:T(8,128)(2,1)} %bitcast.94, bf16[256,2048]{1,0:T(8,128)(2,1)S(1)} %bitcast.99), kind=kOutput, calls=%fused_computation.25 | convolution fusion | flops 1074003968 | bytes 5767168 | tf_op jit(solution)/shard_map/dot_general | solution.py:1503
  158.0 1.9 fusion.22
  159.9 15.0 %shard_map.194 = (bf16[1024,256]{1,0:T(8,128)(2,1)}, bf16[1024,1792]{1,0:T(8,128)(2,1)}, f32[2,1,768]{2,1,0:T(1,128)}) custom-call(f32[1024,1792]{1,0:T(8,128)} %copy-done.3, bf16[1024,256]{1,0:T(8,128)(2,1)} %convolution_convert_fusion.do_ref, bf16[1024,1024]{1,0:T(8,128)(2,1)} %get-tuple-element.68.du_ref, s32[1024,1]{1,0:T(8,128)} %copy.33.seg_col_ref, ...), custom_call_target="tpu_custom_call" | custom-call | flops 1342177280 | bytes 9437184 | tf_op jit(solution)/shard_map/pallas_call | solution.py:506
  174.9 0.7 reduce_sum.92
  175.7 0.6 fusion.26.sums
  176.4 4.6 %add_convert_fusion.norm = bf16[1024,2048]{1,0:T(8,128)(2,1)} fusion(f32[2048]{0:T(1024)S(1)} %add.219, f32[2048]{0:T(1024)S(1)} %mul.294, f32[1024]{0:T(1024)S(1)} %get-tuple-element.88, f32[1024]{0:T(1024)S(1)} %get-tuple-element.89, bf16[8,128,2048]{2,1,0:T(8,128)(2,1)} %get-tuple-element.32), kind=kLoop, calls=%fused_computation.8 | loop fusion | flops 12582912 | bytes 8413184 | tf_op jit(solution)/shard_map/convert_element_type | solution.py:1495
  181.0 1.0 copy.35.inverse
  182.0 1.0 copy.34.mean
  183.0 153.9 %shard_map.195 = (bf16[8,64,1792]{2,1,0:T(8,128)(2,1)}, f32[64,2048]{1,0:T(8,128)}, f32[256,2048]{1,0:T(8,128)}, f32[128,2048]{1,0:T(8,128)}, f32[128,2048]{1,0:T(8,128)}, /*index=5*/f32[8,64,128]{2,1,0:T(8,128)}) custom-call(bf16[1024,2048]{1,0:T(8,128)(2,1)} %add_convert_fusion.norm, bf16[1024,1792]{1,0:T(8,128)(2,1)} %get-tuple-element.38.dcat, ...), custom_call_target="tpu_custom_call" | custom-call | tf_op jit(solution)/shard_map/pallas_call | solution.py:1361
  336.9 1.1 reshape.310
  338.3 0.1 reshape.315
  338.4 0.7 copy.38
  339.1 0.1 mul.364
  339.2 0.8 copy.40
  340.0 0.1 mul.368
  340.1 0.8 copy.37
  340.9 0.1 reshape_squeeze.2
  341.1 0.1 reshape.312
  341.2 0.7 multiply_subtract_fusion.2
  342.0 0.7 multiply_subtract_fusion.1
  343.0 0.6 pad_maximum_fusion.refs_7_
  343.6 24.0 %shard_map.196 = (f32[12296,128]{1,0:T(8,128)}, f32[12296,128]{1,0:T(8,128)}, f32[12296,128]{1,0:T(8,128)}, f32[64,6144]{1,0:T(8,128)}, f32[64,8192]{1,0:T(8,128)}) custom-call(f32[3,64,6144]{2,1,0:T(8,128)} %refs_0_.1, f32[3,64,2048]{2,1,0:T(8,128)} %refs_1_.1, f32[3,64,8192]{2,1,0:T(8,128)} %refs_2_.1, f32[3,256,2048]{2,1,0:T(8,128)} %refs_3_.1, ...), custom_call_target="tpu_custom_call" | custom-call | flops 31471360 | bytes 44059904 | tf_op jit(solution)/shard_map/pallas_call | solution.py:695
  367.7 7.7 %slice.134 = f32[1,1,1573568]{2,1,0:T(1,128)} slice(f32[1,1,1573888]{2,1,0:T(1,128)} %bitcast.90), slice={[0:1], [0:1], [0:1573568]} | slice | bytes 12588544 | tf_op jit(solution)/shard_map/slice | solution.py:715
  375.4 3.3 slice.135
  378.7 1.1 slice-done
  379.8 0.7 slice-done.1
  380.5 2.8 slice.136
  383.3 0.2 convert_reduce_fusion.1
  383.4 0.3 fusion.18
  383.8 0.4 multiply_reduce_fusion
  384.3 3.3 fusion.19
  387.6 0.8 copy.46
  388.4 1.3 copy.47
  (98 shorter events, 1.8 us)
Async XLA Ops:
  3.4 2.7 copy-start.18
  4.8 0.7 copy-start.17
  120.4 3.5 copy-start
  120.4 4.7 %copy-start.13 = (f32[4,8,8,128]{3,2,1,0:T(8,128)S(1)}, f32[4,8,8,128]{3,2,1,0:T(8,128)}, u32[]{:S(2)}) copy-start(f32[4,8,8,128]{3,2,1,0:T(8,128)} %get-tuple-element.33) | copy-start | bytes 393220
  126.2 50.2 %copy-start.11 = (f32[2048]{0:T(1024)}, f32[2048]{0:T(1024)S(1)}, u32[]{:S(2)}) copy-start(f32[2048]{0:T(1024)S(1)} %mul.294) | copy-start | bytes 24580
  131.3 11.9 %copy-start.6 = (bf16[4,256,2048]{2,1,0:T(8,128)(2,1)S(1)}, bf16[4,256,2048]{2,1,0:T(8,128)(2,1)}, u32[]{:S(2)}) copy-start(bf16[4,256,2048]{2,1,0:T(8,128)(2,1)} %get-tuple-element.37) | copy-start | bytes 12582916
  131.3 11.9 %copy-start.7 = (bf16[8,128,2048]{2,1,0:T(8,128)(2,1)S(1)}, bf16[8,128,2048]{2,1,0:T(8,128)(2,1)}, u32[]{:S(2)}) copy-start(bf16[8,128,2048]{2,1,0:T(8,128)(2,1)} %get-tuple-element.35) | copy-start | bytes 12582916
  143.2 9.4 %copy-start.3 = (f32[1024,1792]{1,0:T(8,128)}, f32[1024,1792]{1,0:T(8,128)S(1)}, u32[]{:S(2)}) copy-start(f32[1024,1792]{1,0:T(8,128)S(1)} %convolution_add_fusion.fu_ref) | copy-start | bytes 22020100
  143.2 10.5 %copy-start.10 = (bf16[4,64,2048]{2,1,0:T(8,128)(2,1)S(1)}, bf16[4,64,2048]{2,1,0:T(8,128)(2,1)}, u32[]{:S(2)}) copy-start(bf16[4,64,2048]{2,1,0:T(8,128)(2,1)} %get-tuple-element.36) | copy-start | bytes 3145732
  152.7 5.3 %copy-start.16 = (s32[1,2,4,128]{3,2,1,0:T(4,128)}, s32[1,2,4,128]{3,2,1,0:T(4,128)S(1)}, u32[]{:S(2)}) copy-start(s32[1,2,4,128]{3,2,1,0:T(4,128)S(1)} %dynamic-slice_convert_fusion) | copy-start | bytes 12292
  159.9 15.7 %copy-start.4 = (bf16[1,128,2048]{2,1,0:T(8,128)(2,1)S(1)}, bf16[1,128,2048]{2,1,0:T(8,128)(2,1)}, u32[]{:S(2)}) copy-start(bf16[1,128,2048]{2,1,0:T(8,128)(2,1)} %param.12) | copy-start | bytes 1572868
  338.2 29.4 %copy-start.19 = (f32[64,4]{0,1:T(4,128)}, f32[64,4]{0,1:T(4,128)S(1)}, u32[]{:S(2)}) copy-start(f32[64,4]{0,1:T(4,128)S(1)} %pad_maximum_fusion.2) | copy-start | bytes 3076
  341.2 26.4 %copy-start.21 = (f32[1,192]{1,0:T(1,128)}, f32[1,192]{1,0:T(1,128)S(1)}, u32[]{:S(2)}) copy-start(f32[1,192]{1,0:T(1,128)S(1)} %constant_dynamic-slice_fusion.4) | copy-start | bytes 2308
  342.0 25.6 %copy-start.20 = (f32[1,1,256]{2,1,0:T(1,128)}, f32[1,1,256]{2,1,0:T(1,128)S(1)}, u32[]{:S(2)}) copy-start(f32[1,1,256]{2,1,0:T(1,128)S(1)} %constant_dynamic-slice_fusion.3) | copy-start | bytes 3076
  367.6 7.7 %slice-start.2 = ((s8[6295552]{0:T(1024)(128)(4,1)}), s8[4194304]{0:T(1024)(128)(4,1)S(1)}, s32[]{:S(2)}) async-start(s8[6295552]{0:T(1024)(128)(4,1)} %bitcast.87), calls=%async_computation.2 | async-start | bytes 8388608
  367.7 7.7 %slice-start.3 = ((s8[6295552]{0:T(1024)(128)(4,1)}), s8[2101248]{0:T(1024)(128)(4,1)S(1)}, s32[]{:S(2)}) async-start(s8[6295552]{0:T(1024)(128)(4,1)} %bitcast.87), calls=%async_computation.3 | async-start | bytes 4202496
  375.4 4.4 %slice-start = ((s8[6295552]{0:T(1024)(128)(4,1)}), s8[4194304]{0:T(1024)(128)(4,1)S(1)}, s32[]{:S(2)}) async-start(s8[6295552]{0:T(1024)(128)(4,1)} %bitcast.84), calls=%async_computation | async-start | bytes 8388608
  375.4 5.1 %slice-start.1 = ((s8[6295552]{0:T(1024)(128)(4,1)}), s8[2101248]{0:T(1024)(128)(4,1)S(1)}, s32[]{:S(2)}) async-start(s8[6295552]{0:T(1024)(128)(4,1)} %bitcast.84), calls=%async_computation.1 | async-start | bytes 4202496
  380.5 2.8 copy-start.1
  380.5 3.3 copy-start.8
  380.5 3.3 copy-start.12
  380.5 3.7 copy-start.15
  380.5 3.8 copy-start.14
  380.5 3.8 copy-start.5
  383.3 5.2 %copy-start.2 = (f32[256,2048]{1,0:T(8,128)S(1)}, f32[256,2048]{1,0:T(8,128)}, u32[]{:S(2)}) copy-start(f32[256,2048]{1,0:T(8,128)} %get-tuple-element.118.refs_6_) | copy-start | bytes 6291460
  384.3 3.4 copy-start.9

commit v4 on v3

--- a/solution.py
+++ b/solution.py
@@ -544,11 +544,13 @@
     return weight - learn_rate * (corrected / divisor + weight_decay * weight), first, second
 
 
-def owner_update_kernel(plan, small_plan, groups, *refs):
+def owner_update_kernel(plan, small_plan, groups, steps, whole_rows, *refs):
     planes, cores, shards = groups
     qkv_state, dense_state, up_state, down_state, cat_ref, dense_grad, down_grad, small_ref = refs[:8]
-    outs = refs[8:11]
-    qkv_out, up_out, cat_buf = refs[11:]
+    flat = refs[8:11]
+    qkv_out, up_out, cat_buf = refs[11:14]
+    outs = refs[14:17]
+    step_sem, rest_sem = refs[17:]
     step = pl.program_id(0)
     lane = lax.broadcasted_iota(jnp.int32, (8, 128), 1)
     sub = lax.broadcasted_iota(jnp.int32, (8, 128), 0)
@@ -642,6 +644,46 @@
     place_rows(dense_state, plain(dense_grad), *plan[1])
     place_rows(up_state, up_grad, *plan[2], keep=up_out)
     place_rows(down_state, plain(down_grad), *plan[3])
+
+    def flush(entry, row, count, sem):
+        place = pl.ds(pl.multiple_of(row * 128, 128), count * 128)
+        source = outs[entry].reshape(1, 1, outs[entry].shape[0] * 128)
+        return pltpu.make_async_copy(source.at[:, :, place], flat[entry].at[:, :, place], sem)
+
+    def step_copies(at):
+        copies = []
+        for index, (rows, tiles, start, shifted) in enumerate(plan):
+            count = rows * tiles
+            skip = 1 if shifted and at == 0 else 0
+            for entry in range(3):
+                copies.append(
+                    flush(entry, start + at * count + skip, count - skip, step_sem.at[entry, index, at])
+                )
+        return copies
+
+    for at in range(steps):
+
+        @pl.when(step == at)
+        def begin(at=at):
+            for copy in step_copies(at):
+                copy.start()
+
+    @pl.when(step == steps - 1)
+    def end():
+        covered = set()
+        for rows, tiles, start, shifted in plan:
+            covered |= set(range(start + (1 if shifted else 0), start + steps * rows * tiles))
+        left = [row for row in range(whole_rows) if row not in covered]
+        rest = [
+            flush(entry, row, 1, rest_sem.at[entry, index]) for index, row in enumerate(left) for entry in range(3)
+        ]
+        for copy in rest:
+            copy.start()
+        for at in range(steps):
+            for copy in step_copies(at):
+                copy.wait()
+        for copy in rest:
+            copy.wait()
 
 
 def owner_update(states, cat_sum, grads, small_states, small_grads, groups):
@@ -691,28 +733,36 @@
     in_specs.append(pl.BlockSpec((plan[1][0], plan[1][1] * 128), lambda s: (s, 0)))
     in_specs.append(pl.BlockSpec((plan[3][0], plan[3][1] * 128), lambda s: (s, 0)))
     in_specs.append(pl.BlockSpec((3, small_row, 128), lambda s: (0, 0, 0)))
-    flat = [pl.BlockSpec((out_rows, 128), lambda s: (0, 0), pipeline_mode=pl.Buffered(1))] * 3
+    whole_rows = entries // 128
     *outs, qkv_grad, up_grad = pl.pallas_call(
-        partial(owner_update_kernel, plan, small_plan, groups),
+        partial(owner_update_kernel, plan, small_plan, groups, steps, whole_rows),
         grid=(steps,),
         in_specs=in_specs,
-        out_specs=flat
+        out_specs=[pl.BlockSpec(memory_space=pl.ANY)] * 3
         + [
             pl.BlockSpec((qkv_rows, plan[0][1] * 128), lambda s: (s, 0)),
             pl.BlockSpec((up_rows, plan[2][1] * 128), lambda s: (s, 0)),
         ],
-        out_shape=[jax.ShapeDtypeStruct((out_rows, 128), jnp.float32)] * 3
+        out_shape=[jax.ShapeDtypeStruct((1, 1, entries), jnp.float32)] * 3
         + [
             jax.ShapeDtypeStruct(states[0].shape[1:], jnp.float32),
             jax.ShapeDtypeStruct(states[2].shape[1:], jnp.float32),
         ],
-        scratch_shapes=[pltpu.VMEM((cat_sum.shape[0], qkv_rows, cat_sum.shape[2]), jnp.float32)],
+        scratch_shapes=[pltpu.VMEM((cat_sum.shape[0], qkv_rows, cat_sum.shape[2]), jnp.float32)]
+        + [pltpu.VMEM((out_rows, 128), jnp.float32)] * 3
+        + [pltpu.SemaphoreType.DMA((3, 4, steps)), pltpu.SemaphoreType.DMA((3, 16))],
         compiler_params=pltpu.CompilerParams(vmem_limit_bytes=56 << 20),
         cost_estimate=pl.CostEstimate(
             flops=20 * entries, bytes_accessed=28 * entries, transcendentals=2 * entries
         ),
     )(*states, cat_sum, *grads, small)
-    return tuple(out.reshape(1, 1, out_rows * 128)[:, :, :entries] for out in outs), qkv_grad, up_grad
+    tail = entries - whole_rows * 128
+    if tail:
+        outs = [
+            lax.dynamic_update_slice(out, new[entries_of][-tail:].reshape(1, 1, tail), (0, 0, whole_rows * 128))
+            for out, (new, entries_of) in zip(outs, ((small_new[-1], entry) for entry in range(3)))
+        ]
+    return tuple(outs), qkv_grad, up_grad
 
 
 class Wires:
@@ -865,9 +915,15 @@
             ((qkv_state, qkv_buf), (up_state, up_buf), (down_state, down_buf), (dense_state, dense_buf))
         )
     ]
-    for load in loads:
-        load.start()
+    for index in (2, 3, 0, 1):
+        loads[index].start()
     net.barrier()
+    loads[2].wait()
+    down[...] = down_buf[...].astype(jnp.bfloat16)
+    loads[3].wait()
+    dense[...] = dense_buf[...].astype(jnp.bfloat16)
+    for index in own_units:
+        spread(index)
     loads[0].wait()
     loads[1].wait()
     pack_pieces(qkv_buf, up_buf, pieces, cat_out.shape[0], group // shards, shards)
@@ -888,12 +944,6 @@
         target = net.member(mine ^ mask)
         net.send(vectors, vec_out.at[plane, mine], group_sem.at[1, mask], target)
         net.send(pieces.at[mine ^ mask], cat_out.at[plane, mine], group_sem.at[0, mask], target)
-    loads[2].wait()
-    down[...] = down_buf[...].astype(jnp.bfloat16)
-    loads[3].wait()
-    dense[...] = dense_buf[...].astype(jnp.bfloat16)
-    for index in own_units:
-        spread(index)
     spread(cat_units[0])
     spread(vec_units[0])
     streams = ((tokens, x_out), (cotangent, dy_out))
@@ -1126,13 +1176,15 @@
     turns = (3, 1, 2, 0)
     norm_copy(0, turns[0]).start()
     locals_["dcat"].wait()
-    for turn, distance in enumerate(turns):
+
+    def cat_turn(turn):
+        distance = turns[turn]
         if turn + 1 < planes:
             norm_copy(turn + 1, turns[turn + 1]).start()
         norm_copy(turn, distance).wait()
         norm_turned[...] = norm_chunk[turn % 2].T
 
-        def cat_step(n, carry, distance=distance):
+        def cat_step(n, carry):
             total = dot(norm_turned[...], wide[:, columns(n)]).astype(jnp.bfloat16)
             for member in range(group):
                 cat_part[distance, mine ^ member, :, columns(n)] = total[member * block : (member + 1) * block]
@@ -1144,6 +1196,8 @@
                 send_pass(index)
             elif distance == ways(index)[2]:
                 send_keep(index)
+
+    cat_turn(0)
 
     sum_buf[4] = sums[...]
     gain_row = width // 128
@@ -1183,9 +1237,7 @@
 
     net.send(sum_buf.at[4], sum_buf.at[0], sum_sem.at[0], net.first)
     to_partner(1)
-
-    local("hidden", hidden, wide.at[:, pl.ds(0, units_here)])
-    local("attn", attn, wide.at[:, pl.ds(2 * units_here, heads_here)])
+    cat_turn(1)
 
     def own(stream, place):
         return tokens.at[stream, core * shards + place]
@@ -1226,6 +1278,39 @@
             def add(values=values):
                 add_rows((mixed_out, norm_out)[stream], *values)
 
+    def first_sums(stream):
+        for place in places:
+            net.arrived(token_in.at[stream, place], core_sem.at[stream, place])
+        for rank in range(shards - 1):
+            chain(stream, 0, rank)
+
+    def pass_on(index):
+        parts, came, slot = units[index]
+        near, far, near_mask, far_mask = ways(index)
+        total = parts.at[far_mask, slot]
+        net.arrived(came.at[PASS, slot], pass_sem.at[0, index])
+        add_rows(total, total, came.at[PASS, slot])
+        net.send(total, came.at[LAST, slot], pass_sem.at[1, index], far)
+
+    first_sums(1)
+    cat_turn(2)
+    net.arrived(sum_buf.at[0], sum_sem.at[0])
+    sum_buf[1] = sum_buf[4] + sum_buf[0]
+    net.send(sum_buf.at[1], sum_buf.at[2], sum_sem.at[1], net.second)
+    for index in cats:
+        pass_on(index)
+    cat_turn(3)
+    local("hidden", hidden, wide.at[:, pl.ds(0, units_here)])
+    local("attn", attn, wide.at[:, pl.ds(2 * units_here, heads_here)])
+    steps = [
+        (hop, rank)
+        for hop, rank in sorted(
+            ((hop, rank) for hop in range(1, shards - 1) for rank in range(shards - 1 - hop)),
+            key=lambda pair: (pair[0] + 2 * pair[1], pair[0]),
+        )
+    ]
+    later = [(stream, hop, rank) for stream in (1, 0) for hop, rank in steps]
+
     locals_["hidden"].wait()
     locals_["attn"].wait()
     turned = pl.ds(units_here, rows)
@@ -1257,20 +1342,14 @@
 
     half = model // lane // 2
     chunked(0, half, out_copies, out_step)
-    for place in places:
-        net.arrived(token_in.at[1, place], core_sem.at[1, place])
-    for rank in range(shards - 1):
-        chain(1, 0, rank)
+    chain(*later.pop(0))
     chunked(half, 2 * half, out_copies, out_step)
     to_partner(0)
-
-    def pass_on(index):
-        parts, came, slot = units[index]
-        near, far, near_mask, far_mask = ways(index)
-        total = parts.at[far_mask, slot]
-        net.arrived(came.at[PASS, slot], pass_sem.at[0, index])
-        add_rows(total, total, came.at[PASS, slot])
-        net.send(total, came.at[LAST, slot], pass_sem.at[1, index], far)
+    for index in every[group:]:
+        send_pass(index)
+        send_keep(index)
+    chain(*later.pop(0))
+    first_sums(0)
 
     def finish(index):
         parts, came, slot = units[index]
@@ -1289,31 +1368,6 @@
         else:
             add_rows(dense_out.at[pl.ds(slot * dense_rows, dense_rows)], *values)
 
-    for index in every[group:]:
-        send_pass(index)
-        send_keep(index)
-    net.arrived(sum_buf.at[0], sum_sem.at[0])
-    sum_buf[1] = sum_buf[4] + sum_buf[0]
-    net.send(sum_buf.at[1], sum_buf.at[2], sum_sem.at[1], net.second)
-    for index in cats[:2]:
-        pass_on(index)
-    for place in places:
-        net.arrived(token_in.at[0, place], core_sem.at[0, place])
-    for rank in range(shards - 1):
-        chain(0, 0, rank)
-    later = [
-        (stream, hop, rank)
-        for hop, rank in sorted(
-            ((hop, rank) for hop in range(1, shards - 1) for rank in range(shards - 1 - hop)),
-            key=lambda pair: (pair[0] + 2 * pair[1], pair[0]),
-        )
-        for stream in (1, 0)
-    ]
-    later.sort(key=lambda item: -item[0])
-    for index in cats[2:]:
-        pass_on(index)
-        if index % 2 and later:
-            chain(*later.pop(0))
     net.arrived(sum_buf.at[2], sum_sem.at[1])
     sum_buf[3] = sum_buf[1] + sum_buf[2]
     for mask in range(1, group):
@@ -1492,7 +1546,7 @@
     center = x_float - x_mean
     inverse = lax.rsqrt(jnp.mean(center * center, axis=-1, keepdims=True) + norm_eps)
     x_hat = center * inverse
-    norm_bf = (x_hat * norm_gain + norm_shift).astype(jnp.bfloat16)
+    norm_bf = lax.optimization_barrier((x_hat * norm_gain + norm_shift).astype(jnp.bfloat16))
 
     fu = jnp.dot(norm_bf, cat_w, preferred_element_type=jnp.float32) + cat_bias
     pre_act = fu[:, 3 * head_width :]

time: 391 us -> 355 us (0.908)
  Pallas kernels: 307 us -> 290 us
  local copies, waits for them, and re-layouts: 27 us -> 13.2 us
  other arithmetic: 28.9 us -> 24.3 us
    pallas_call x1, Pallas kernels: 154 us -> 138 us  [reduce_wires(): pl.pallas_call(reduce_kernel, in_specs=[hbm] * 3 + [vmem] * 2 + [hbm] * 6...]
    slice x3 -> x0, local copies, waits for them, and re-layouts: 13.8 us -> none  [owner_update(): out.reshape(1, 1, out_rows * 128)[:, :, :entries]]
    convert_element_type x2 -> x1, other arithmetic: 9.34 us -> 4.74 us  [fast_body(): (x_hat * norm_gain + norm_shift).astype(jnp.bfloat16)]
where the time goes in v4:
time: 355 us; the launch traced here: 354 us
  Pallas kernels  290 us (82%)
  matrix products  25.4 us (7%)
  other arithmetic  24.3 us (7%)
  local copies, waits for them, and re-layouts  13.2 us (4%)
    pallas_call x1, Pallas kernels, reduce_wires(): pl.pallas_call(reduce_kernel, in_specs=[hbm] * 3 + [vmem] * 2 + [hbm] * 6...  138 us
    pallas_call x1, Pallas kernels, gather_wires(): pl.pallas_call(gather_kernel, in_specs=[hbm] * 4 + [vmem] * 3, out_specs=...  115 us
    pallas_call x1, Pallas kernels, owner_update(): pl.pallas_call(partial(owner_update_kernel, plan, small_plan, groups, ste...  22.6 us
    pallas_call x1, Pallas kernels, attention(): pl.pallas_call(attention_kernel, grid=(count,), in_specs=[pl.BlockSpec((r...  15 us
    dot_general x1, matrix products, fast_body(): fu = jnp.dot(norm_bf, cat_w, preferred_element_type=jnp.float32) + cat_bias  11.8 us
    dot_general x1, matrix products, fast_body(): grad_hidden = jnp.dot(dy_all, down_w.T, preferred_element_type=jnp.float32)  9.37 us

profile of v4, /device:TPU:0, one launch (start us, length us, event | category | flops | bytes accessed | tf_op | source)
XLA Modules:
  0.0 354.2 jit_solution(15313162052971864199)
XLA Ops:
  0.6 1.3 slice_multiply_fusion
  2.0 1.4 slice_multiply_fusion.4
  3.4 1.4 slice_multiply_fusion.2
  4.8 0.7 convert_bitcast_fusion.1
  5.5 0.7 fusion.26.vectors
  6.2 115.0 %shard_map.193 = (bf16[4,8,64,1792]{3,2,1,0:T(8,128)(2,1)}, bf16[4,64,2048]{2,1,0:T(8,128)(2,1)}, bf16[4,256,2048]{2,1,0:T(8,128)(2,1)}, bf16[8,128,2048]{2,1,0:...) custom-call(f32[3,64,6144]{2,1,0:T(8,128)} %refs_0_.1, f32[3,64,8192]{2,1,0:T(8,128)} %refs_2_.1, ...), custom_call_target="tpu_custom_call" | custom-call | tf_op jit(solution)/shard_map/pallas_call | solution.py:1041
  121.2 3.0 convert_reduce_fusion
  124.2 0.5 copy-done
  124.7 1.2 fusion.1
  126.1 0.1 reshape.302
  126.2 0.7 slice_reduce_fusion.2
  127.1 4.7 %add_convert_fusion.norm = bf16[1024,2048]{1,0:T(8,128)(2,1)} fusion(f32[2048]{0:T(1024)S(1)} %add.213, f32[2048]{0:T(1024)S(1)} %mul.284, f32[1024]{0:T(1024)S(1)} %get-tuple-element.88, f32[1024]{0:T(1024)S(1)} %get-tuple-element.89, bf16[8,128,2048]{2,1,0:T(8,128)(2,1)} %get-tuple-element.32), kind=kLoop, calls=%fused_computation.4 | loop fusion | flops 12582912 | bytes 8413184 | tf_op jit(solution)/shard_map/convert_element_type | solution.py:1549
  131.9 0.1 reshape.306
  132.0 0.1 reshape.299
  132.1 11.8 %convolution_add_fusion.fu_ref = f32[1024,1792]{1,0:T(8,128)S(1)} fusion(bf16[1024,2048]{1,0:T(8,128)(2,1)} %add_convert_fusion.norm, bf16[2048,1792]{1,0:T(8,128)(2,1)} %bitcast.84, f32[1792]{0:T(1024)S(1)} %pad_maximum_fusion.1), kind=kOutput, calls=%fused_computation.15 | convolution fusion | flops 7518027776 | bytes 18881536 | tf_op jit(solution)/shard_map/dot_general | solution.py:1551
  144.0 9.4 %fusion.43 = (f32[1024]{0:T(1024)S(1)}, bf16[1024,1024]{1,0:T(8,128)(2,1)}, bf16[1024,1024]{1,0:T(8,128)(2,1)}) fusion(f32[1024,1792]{1,0:T(8,128)S(1)} %convolution_add_fusion.fu_ref, bf16[1024,2048]{1,0:T(8,128)(2,1)S(1)} %bitcast.91, bf16[1024,2048]{1,0:T(8,128)(2,1)S(1)} %bitcast.88), kind=kOutput, calls=%fused_computation.130 | convolution fusion | flops 4323277824 | bytes 16781312 | tf_op jit(solution)/shard_map/dot_general | solution.py:1554
  153.4 1.0 copy.33.seg_col_ref
  154.5 4.3 %convolution_convert_fusion.do_ref = bf16[1024,256]{1,0:T(8,128)(2,1)} fusion(bf16[1024,2048]{1,0:T(8,128)(2,1)} %bitcast.89, bf16[256,2048]{1,0:T(8,128)(2,1)S(1)} %bitcast.93), kind=kOutput, calls=%fused_computation.21 | convolution fusion | flops 1074003968 | bytes 5767168 | tf_op jit(solution)/shard_map/dot_general | solution.py:1557
  158.8 1.9 fusion.18
  160.7 15.0 %shard_map.194 = (bf16[1024,256]{1,0:T(8,128)(2,1)}, bf16[1024,1792]{1,0:T(8,128)(2,1)}, f32[2,1,768]{2,1,0:T(1,128)}) custom-call(f32[1024,1792]{1,0:T(8,128)} %copy-done.3, bf16[1024,256]{1,0:T(8,128)(2,1)} %convolution_convert_fusion.do_ref, bf16[1024,1024]{1,0:T(8,128)(2,1)} %get-tuple-element.68.du_ref, s32[1024,1]{1,0:T(8,128)} %copy.33.seg_col_ref, ...), custom_call_target="tpu_custom_call" | custom-call | flops 1342177280 | bytes 9437184 | tf_op jit(solution)/shard_map/pallas_call | solution.py:506
  175.7 0.7 reduce_sum.92
  176.5 0.6 fusion.22.sums
  177.1 1.0 copy.35.inverse
  178.2 1.0 copy.34.mean
  179.2 137.5 %shard_map.195 = (bf16[8,64,1792]{2,1,0:T(8,128)(2,1)}, f32[64,2048]{1,0:T(8,128)}, f32[256,2048]{1,0:T(8,128)}, f32[128,2048]{1,0:T(8,128)}, f32[128,2048]{1,0:T(8,128)}, /*index=5*/f32[8,64,128]{2,1,0:T(8,128)}) custom-call(bf16[1024,2048]{1,0:T(8,128)(2,1)} %add_convert_fusion.norm, bf16[1024,1792]{1,0:T(8,128)(2,1)} %get-tuple-element.38.dcat, ...), custom_call_target="tpu_custom_call" | custom-call | tf_op jit(solution)/shard_map/pallas_call | solution.py:1415
  316.7 1.1 reshape.289
  318.0 0.1 copy.39
  318.1 0.1 reshape.294
  318.2 0.8 copy.38
  318.9 0.1 mul.350
  319.0 0.7 copy.40
  319.8 0.1 mul.354
  319.9 0.7 copy.37
  320.6 0.1 reshape_squeeze.2
  320.9 0.1 reshape.291
  321.0 0.7 multiply_subtract_fusion.2
  321.8 0.7 multiply_subtract_fusion.1
  322.7 0.6 pad_maximum_fusion.refs_7_
  323.3 22.6 %shard_map.196 = (f32[1,1,1573568]{2,1,0:T(1,128)}, f32[1,1,1573568]{2,1,0:T(1,128)}, f32[1,1,1573568]{2,1,0:T(1,128)}, f32[64,6144]{1,0:T(8,128)}, f32[64,8192]{1,0:T(8,128)}) custom-call(f32[3,64,6144]{2,1,0:T(8,128)} %refs_0_.1, f32[3,64,2048]{2,1,0:T(8,128)} %refs_1_.1, f32[3,64,8192]{2,1,0:T(8,128)} %refs_2_.1, f32[3,256,2048]{2,1,0:T(8,128)} %refs_3_.1, ...), custom_call_target="tpu_custom_call" | custom-call | flops 31471360 | bytes 44059904 | tf_op jit(solution)/shard_map/pallas_call | solution.py:737
  346.0 0.6 constant_dynamic-update-slice_fusion
  346.5 0.6 constant_dynamic-update-slice_fusion.1
  347.1 0.6 constant_dynamic-update-slice_fusion.2
  347.7 0.2 convert_reduce_fusion.1
  347.9 0.3 fusion.14
  348.2 0.3 multiply_reduce_fusion
  348.7 3.3 fusion.15
  352.1 0.8 copy.49
  352.9 1.3 copy.50
  (87 shorter events, 1.5 us)
Async XLA Ops:
  3.4 2.7 copy-start.18
  4.8 0.7 copy-start.17
  121.2 3.5 copy-start
  121.2 4.7 %copy-start.13 = (f32[4,8,8,128]{3,2,1,0:T(8,128)S(1)}, f32[4,8,8,128]{3,2,1,0:T(8,128)}, u32[]{:S(2)}) copy-start(f32[4,8,8,128]{3,2,1,0:T(8,128)} %get-tuple-element.33) | copy-start | bytes 393220
  127.0 4.8 %copy-start.11 = (f32[2048]{0:T(1024)}, f32[2048]{0:T(1024)S(1)}, u32[]{:S(2)}) copy-start(f32[2048]{0:T(1024)S(1)} %mul.284) | copy-start | bytes 24580
  132.1 11.8 %copy-start.6 = (bf16[4,256,2048]{2,1,0:T(8,128)(2,1)S(1)}, bf16[4,256,2048]{2,1,0:T(8,128)(2,1)}, u32[]{:S(2)}) copy-start(bf16[4,256,2048]{2,1,0:T(8,128)(2,1)} %get-tuple-element.37) | copy-start | bytes 12582916
  132.1 11.8 %copy-start.7 = (bf16[8,128,2048]{2,1,0:T(8,128)(2,1)S(1)}, bf16[8,128,2048]{2,1,0:T(8,128)(2,1)}, u32[]{:S(2)}) copy-start(bf16[8,128,2048]{2,1,0:T(8,128)(2,1)} %get-tuple-element.35) | copy-start | bytes 12582916
  143.9 9.4 %copy-start.3 = (f32[1024,1792]{1,0:T(8,128)}, f32[1024,1792]{1,0:T(8,128)S(1)}, u32[]{:S(2)}) copy-start(f32[1024,1792]{1,0:T(8,128)S(1)} %convolution_add_fusion.fu_ref) | copy-start | bytes 22020100
  144.0 10.5 %copy-start.10 = (bf16[4,64,2048]{2,1,0:T(8,128)(2,1)S(1)}, bf16[4,64,2048]{2,1,0:T(8,128)(2,1)}, u32[]{:S(2)}) copy-start(bf16[4,64,2048]{2,1,0:T(8,128)(2,1)} %get-tuple-element.36) | copy-start | bytes 3145732
  153.4 5.3 %copy-start.16 = (s32[1,2,4,128]{3,2,1,0:T(4,128)}, s32[1,2,4,128]{3,2,1,0:T(4,128)S(1)}, u32[]{:S(2)}) copy-start(s32[1,2,4,128]{3,2,1,0:T(4,128)S(1)} %dynamic-slice_convert_fusion) | copy-start | bytes 12292
  160.7 15.7 %copy-start.4 = (bf16[1,128,2048]{2,1,0:T(8,128)(2,1)S(1)}, bf16[1,128,2048]{2,1,0:T(8,128)(2,1)}, u32[]{:S(2)}) copy-start(bf16[1,128,2048]{2,1,0:T(8,128)(2,1)} %param.12) | copy-start | bytes 1572868
  317.9 28.0 %copy-start.19 = (f32[64,4]{0,1:T(4,128)}, f32[64,4]{0,1:T(4,128)S(1)}, u32[]{:S(2)}) copy-start(f32[64,4]{0,1:T(4,128)S(1)} %pad_maximum_fusion.2) | copy-start | bytes 3076
  321.0 25.0 %copy-start.21 = (f32[1,192]{1,0:T(1,128)}, f32[1,192]{1,0:T(1,128)S(1)}, u32[]{:S(2)}) copy-start(f32[1,192]{1,0:T(1,128)S(1)} %constant_dynamic-slice_fusion.4) | copy-start | bytes 2308
  321.7 24.2 %copy-start.20 = (f32[1,1,256]{2,1,0:T(1,128)}, f32[1,1,256]{2,1,0:T(1,128)S(1)}, u32[]{:S(2)}) copy-start(f32[1,1,256]{2,1,0:T(1,128)S(1)} %constant_dynamic-slice_fusion.3) | copy-start | bytes 3076
  323.3 24.4 %copy-start.1 = (bf16[1,128,2048]{2,1,0:T(8,128)(2,1)S(1)}, bf16[1,128,2048]{2,1,0:T(8,128)(2,1)}, u32[]{:S(2)}) copy-start(bf16[1,128,2048]{2,1,0:T(8,128)(2,1)} %param.10) | copy-start | bytes 1572868
  323.3 24.9 %copy-start.8 = (f32[128,2048]{1,0:T(8,128)S(1)}, f32[128,2048]{1,0:T(8,128)}, u32[]{:S(2)}) copy-start(f32[128,2048]{1,0:T(8,128)} %get-tuple-element.42) | copy-start | bytes 3145732
  323.3 24.9 %copy-start.12 = (f32[2048]{0:T(1024)S(1)}, f32[2048]{0:T(1024)}, u32[]{:S(2)}) copy-start(f32[2048]{0:T(1024)} %copy-done.11) | copy-start | bytes 24580
  323.3 25.3 %copy-start.15 = (f32[32,64]{1,0:T(8,128)S(1)}, f32[32,64]{1,0:T(8,128)}, u32[]{:S(2)}) copy-start(f32[32,64]{1,0:T(8,128)} %get-tuple-element.54) | copy-start | bytes 24580
  323.3 25.3 %copy-start.14 = (f32[32,64]{1,0:T(8,128)S(1)}, f32[32,64]{1,0:T(8,128)}, u32[]{:S(2)}) copy-start(f32[32,64]{1,0:T(8,128)} %get-tuple-element.55) | copy-start | bytes 24580
  323.3 25.4 %copy-start.5 = (bf16[1,128,2048]{2,1,0:T(8,128)(2,1)S(1)}, bf16[1,128,2048]{2,1,0:T(8,128)(2,1)}, u32[]{:S(2)}) copy-start(bf16[1,128,2048]{2,1,0:T(8,128)(2,1)} %param.12) | copy-start | bytes 1572868
  347.7 5.2 %copy-start.2 = (f32[256,2048]{1,0:T(8,128)S(1)}, f32[256,2048]{1,0:T(8,128)}, u32[]{:S(2)}) copy-start(f32[256,2048]{1,0:T(8,128)} %get-tuple-element.118.refs_6_) | copy-start | bytes 6291460
  348.7 3.4 copy-start.9

commit v5 on v4

--- a/solution.py
+++ b/solution.py
@@ -1115,7 +1115,7 @@
     cat_out, dense_out, down_out, mixed_out, norm_out, sums_out,
     cat_part, down_part, dense_part, cat_in, down_in, dense_in,
     tokens, token_in, token_line, token_last, sum_buf,
-    wide, attn_turned, norm_chunk, norm_turned, cat_chunk, x_chunk, down_chunk, dense_chunk, dy_chunk,
+    wide, hidden_turned, attn_turned, norm_chunk, norm_turned, cat_chunk, x_chunk, down_chunk, dense_chunk, dy_chunk,
     send_sems, near_sem, pass_sem, group_sem, core_sem, line_sem, sum_sem, local_sem, chunk_sem,
 ):
     PASS, KEEP, LAST = range(3)
@@ -1161,8 +1161,43 @@
         locals_[key] = pltpu.make_async_copy(source, target, local_sem.at[len(locals_)])
         locals_[key].start()
 
+    local("hidden", hidden, wide.at[:, pl.ds(0, units_here)])
+    local("attn", attn, wide.at[:, pl.ds(units_here, heads_here)])
+    net.barrier()
+
+    places = [place for rank in range(shards // 2) for place in (shards - 1 - rank, rank)]
+
+    def to_partner(stream):
+        for place in places:
+            net.send(
+                tokens.at[stream, (1 - core) * shards + place],
+                token_in.at[stream, place],
+                core_sem.at[stream, place],
+                partner,
+            )
+
+    def out_copies(n, slot):
+        return [
+            pltpu.make_async_copy(down_w.at[:, columns(n)], down_chunk.at[slot], chunk_sem.at[3, slot]),
+            pltpu.make_async_copy(dense_w.at[:, columns(n)], dense_chunk.at[slot], chunk_sem.at[4, slot]),
+        ]
+
+    def out_step(n, slot):
+        total = dot(wide[:, pl.ds(0, units_here)], down_chunk[slot]) + dot(
+            wide[:, pl.ds(units_here, heads_here)], dense_chunk[slot]
+        )
+        for member in range(group):
+            tokens[0, member, :, columns(n)] = total[member * token_rows : (member + 1) * token_rows].astype(
+                jnp.bfloat16
+            )
+
+    locals_["hidden"].wait()
+    locals_["attn"].wait()
+    chunked(0, model // lane, out_copies, out_step)
+    to_partner(0)
+    hidden_turned[...] = wide[:, pl.ds(0, units_here)].T
+    attn_turned[...] = wide[:, pl.ds(units_here, heads_here)].T
     local("dcat", dcat, wide.at[:, pl.ds(0, width)])
-    net.barrier()
 
     plane_rows = group * block
 
@@ -1173,6 +1208,10 @@
         )
 
     cats, every = range(group), range(len(units))
+    chain_steps = sorted(
+        ((hop, rank) for hop in range(1, shards - 1) for rank in range(shards - 1 - hop)),
+        key=lambda pair: (pair[0] + 2 * pair[1], pair[0]),
+    )
     turns = (3, 1, 2, 0)
     norm_copy(0, turns[0]).start()
     locals_["dcat"].wait()
@@ -1197,7 +1236,61 @@
             elif distance == ways(index)[2]:
                 send_keep(index)
 
+    def own(stream, place):
+        return tokens.at[stream, core * shards + place]
+
+    def chain(stream, hop, rank):
+        for upward in (True, False):
+            target = shards - 1 - rank if upward else rank
+            here = hop if upward else shards - 1 - hop
+            sems = line_sem.at[0 if upward else 1]
+            came = token_line.at[stream, target]
+            total = own(stream, target)
+            holds = shard == here
+            if hop:
+                net.arrived(came, sems.at[stream, target], holds)
+
+            @pl.when(holds)
+            def add(target=target, came=came, total=total):
+                add_rows(total, total, token_in.at[stream, target], *([came] if hop else []))
+
+            there = jnp.clip(shard + (1 if upward else -1), 0, shards - 1)
+            ends = (not upward) and rank == shards - 2 - hop
+            landing = token_last.at[stream] if ends else came
+            net.send(total, landing, sems.at[stream, target], (plane, core, there), holds)
+
+    def final(stream):
+        for place in range(shards):
+            holds = shard == place
+            values = [own(stream, place), token_in.at[stream, place]]
+            for landing, side, present in (
+                (token_line.at[stream, place], line_sem.at[0], place > 0),
+                (token_last.at[stream], line_sem.at[1], place < shards - 1),
+            ):
+                if present:
+                    values.append(landing)
+                    net.arrived(landing, side.at[stream, place], holds)
+
+            @pl.when(holds)
+            def add(values=values):
+                add_rows((mixed_out, norm_out)[stream], *values)
+
+    def first_sums(stream):
+        for place in places:
+            net.arrived(token_in.at[stream, place], core_sem.at[stream, place])
+        for rank in range(shards - 1):
+            chain(stream, 0, rank)
+
+    def pass_on(index):
+        parts, came, slot = units[index]
+        near, far, near_mask, far_mask = ways(index)
+        total = parts.at[far_mask, slot]
+        net.arrived(came.at[PASS, slot], pass_sem.at[0, index])
+        add_rows(total, total, came.at[PASS, slot])
+        net.send(total, came.at[LAST, slot], pass_sem.at[1, index], far)
+
     cat_turn(0)
+    first_sums(0)
 
     sum_buf[4] = sums[...]
     gain_row = width // 128
@@ -1224,115 +1317,24 @@
 
     chunked(0, model // lane, norm_copies, norm_step)
 
-    places = [place for rank in range(shards // 2) for place in (shards - 1 - rank, rank)]
-
-    def to_partner(stream):
-        for place in places:
-            net.send(
-                tokens.at[stream, (1 - core) * shards + place],
-                token_in.at[stream, place],
-                core_sem.at[stream, place],
-                partner,
-            )
-
     net.send(sum_buf.at[4], sum_buf.at[0], sum_sem.at[0], net.first)
     to_partner(1)
     cat_turn(1)
-
-    def own(stream, place):
-        return tokens.at[stream, core * shards + place]
-
-    def chain(stream, hop, rank):
-        for upward in (True, False):
-            target = shards - 1 - rank if upward else rank
-            here = hop if upward else shards - 1 - hop
-            sems = line_sem.at[0 if upward else 1]
-            came = token_line.at[stream, target]
-            total = own(stream, target)
-            holds = shard == here
-            if hop:
-                net.arrived(came, sems.at[stream, target], holds)
-
-            @pl.when(holds)
-            def add(target=target, came=came, total=total):
-                add_rows(total, total, token_in.at[stream, target], *([came] if hop else []))
-
-            there = jnp.clip(shard + (1 if upward else -1), 0, shards - 1)
-            ends = (not upward) and rank == shards - 2 - hop
-            landing = token_last.at[stream] if ends else came
-            net.send(total, landing, sems.at[stream, target], (plane, core, there), holds)
-
-    def final(stream):
-        for place in range(shards):
-            holds = shard == place
-            values = [own(stream, place), token_in.at[stream, place]]
-            for landing, side, present in (
-                (token_line.at[stream, place], line_sem.at[0], place > 0),
-                (token_last.at[stream], line_sem.at[1], place < shards - 1),
-            ):
-                if present:
-                    values.append(landing)
-                    net.arrived(landing, side.at[stream, place], holds)
-
-            @pl.when(holds)
-            def add(values=values):
-                add_rows((mixed_out, norm_out)[stream], *values)
-
-    def first_sums(stream):
-        for place in places:
-            net.arrived(token_in.at[stream, place], core_sem.at[stream, place])
-        for rank in range(shards - 1):
-            chain(stream, 0, rank)
-
-    def pass_on(index):
-        parts, came, slot = units[index]
-        near, far, near_mask, far_mask = ways(index)
-        total = parts.at[far_mask, slot]
-        net.arrived(came.at[PASS, slot], pass_sem.at[0, index])
-        add_rows(total, total, came.at[PASS, slot])
-        net.send(total, came.at[LAST, slot], pass_sem.at[1, index], far)
-
+    chain(0, 1, 0)
     first_sums(1)
     cat_turn(2)
+    cat_turn(3)
     net.arrived(sum_buf.at[0], sum_sem.at[0])
     sum_buf[1] = sum_buf[4] + sum_buf[0]
     net.send(sum_buf.at[1], sum_buf.at[2], sum_sem.at[1], net.second)
     for index in cats:
         pass_on(index)
-    cat_turn(3)
-    local("hidden", hidden, wide.at[:, pl.ds(0, units_here)])
-    local("attn", attn, wide.at[:, pl.ds(2 * units_here, heads_here)])
-    steps = [
-        (hop, rank)
-        for hop, rank in sorted(
-            ((hop, rank) for hop in range(1, shards - 1) for rank in range(shards - 1 - hop)),
-            key=lambda pair: (pair[0] + 2 * pair[1], pair[0]),
-        )
-    ]
-    later = [(stream, hop, rank) for stream in (1, 0) for hop, rank in steps]
-
-    locals_["hidden"].wait()
-    locals_["attn"].wait()
-    turned = pl.ds(units_here, rows)
-    wide[:, turned] = wide[:, pl.ds(0, units_here)].T
-    attn_turned[...] = wide[:, pl.ds(2 * units_here, heads_here)].T
-
-    def out_copies(n, slot):
-        return [
-            pltpu.make_async_copy(down_w.at[:, columns(n)], down_chunk.at[slot], chunk_sem.at[3, slot]),
-            pltpu.make_async_copy(dense_w.at[:, columns(n)], dense_chunk.at[slot], chunk_sem.at[4, slot]),
-            pltpu.make_async_copy(dy.at[:, columns(n)], dy_chunk.at[slot], chunk_sem.at[5, slot]),
-        ]
-
-    def out_step(n, slot):
-        total = dot(wide[:, pl.ds(0, units_here)], down_chunk[slot]) + dot(
-            wide[:, pl.ds(2 * units_here, heads_here)], dense_chunk[slot]
-        )
-        for member in range(group):
-            tokens[0, member, :, columns(n)] = total[member * token_rows : (member + 1) * token_rows].astype(
-                jnp.bfloat16
-            )
-        for parts, left in ((down_part, wide[:, turned]), (dense_part, attn_turned[...])):
+
+    def grad_copies(n, slot):
+        return [pltpu.make_async_copy(dy.at[:, columns(n)], dy_chunk.at[slot], chunk_sem.at[5, slot])]
+
+    def grad_step(n, slot):
+        for parts, left in ((down_part, hidden_turned[...]), (dense_part, attn_turned[...])):
             grad = dot(left, dy_chunk[slot]).astype(jnp.bfloat16)
             pieces, size = parts.shape[1], parts.shape[2]
             for q in range(planes):
@@ -1340,16 +1342,12 @@
                     start = (q * pieces + piece) * size
                     parts[plane ^ q, piece, :, columns(n)] = grad[start : start + size]
 
-    half = model // lane // 2
-    chunked(0, half, out_copies, out_step)
-    chain(*later.pop(0))
-    chunked(half, 2 * half, out_copies, out_step)
-    to_partner(0)
+    chunked(0, model // lane, grad_copies, grad_step)
     for index in every[group:]:
         send_pass(index)
         send_keep(index)
-    chain(*later.pop(0))
-    first_sums(0)
+    for hop, rank in chain_steps[1:]:
+        chain(0, hop, rank)
 
     def finish(index):
         parts, came, slot = units[index]
@@ -1373,20 +1371,21 @@
     for mask in range(1, group):
         net.send(sum_buf.at[3], sums_out.at[mine], group_sem.at[1, mask], net.member(mine ^ mask))
     local("sums", sum_buf.at[3], sums_out.at[mine])
-    for index in cats[: group - 2]:
+    for index in cats[: group // 2]:
         finish(index)
-        if later:
-            chain(*later.pop(0))
-    while later:
-        chain(*later.pop(0))
+    chain(1, *chain_steps[0])
+    for index in cats[group // 2 : group - 2]:
+        finish(index)
+    for hop, rank in chain_steps[1:]:
+        chain(1, hop, rank)
+    for index in cats[group - 2 :]:
+        finish(index)
     for index in every[group:]:
         pass_on(index)
-    for index in cats[group - 2 :]:
-        finish(index)
-    for stream in (1, 0):
-        final(stream)
+    final(0)
     for index in every[group:]:
         finish(index)
+    final(1)
     for mask in range(1, group):
         net.arrived(cat_out.at[mine ^ mask], group_sem.at[0, mask])
         net.arrived(sums_out.at[mine ^ mask], group_sem.at[1, mask])
@@ -1436,7 +1435,8 @@
             scratch(2, shards, token_rows, model),
             scratch(2, token_rows, model),
             scratch(5, *sums.shape, dtype=jnp.float32),
-            scratch(rows, hidden.shape[1] + rows + attn.shape[1]),
+            scratch(rows, max(width, hidden.shape[1] + attn.shape[1])),
+            scratch(hidden.shape[1], rows),
             scratch(attn.shape[1], rows),
             scratch(2, rows, group * block),
             scratch(group * block, rows),

time: 355 us -> 355 us (level)
  no operation moved by 1% of the time
where the time goes in v5:
time: 355 us; the launch traced here: 353 us
  Pallas kernels  289 us (81%)
  matrix products  25.4 us (7%)
  other arithmetic  24.3 us (7%)
  local copies, waits for them, and re-layouts  13.2 us (4%)
    pallas_call x1, Pallas kernels, reduce_wires(): pl.pallas_call(reduce_kernel, in_specs=[hbm] * 3 + [vmem] * 2 + [hbm] * 6...  136 us
    pallas_call x1, Pallas kernels, gather_wires(): pl.pallas_call(gather_kernel, in_specs=[hbm] * 4 + [vmem] * 3, out_specs=...  115 us
    pallas_call x1, Pallas kernels, owner_update(): pl.pallas_call(partial(owner_update_kernel, plan, small_plan, groups, ste...  22.6 us
    pallas_call x1, Pallas kernels, attention(): pl.pallas_call(attention_kernel, grid=(count,), in_specs=[pl.BlockSpec((r...  15 us
    dot_general x1, matrix products, fast_body(): fu = jnp.dot(norm_bf, cat_w, preferred_element_type=jnp.float32) + cat_bias  11.8 us
    dot_general x1, matrix products, fast_body(): grad_hidden = jnp.dot(dy_all, down_w.T, preferred_element_type=jnp.float32)  9.37 us

profile of v5, /device:TPU:0, one launch (start us, length us, event | category | flops | bytes accessed | tf_op | source)
XLA Modules:
  0.0 352.9 jit_solution(2340289471632100745)
XLA Ops:
  0.6 1.3 slice_multiply_fusion
  2.0 1.4 slice_multiply_fusion.4
  3.4 1.4 slice_multiply_fusion.2
  4.8 0.7 convert_bitcast_fusion.1
  5.5 0.7 fusion.26.vectors
  6.2 115.0 %shard_map.193 = (bf16[4,8,64,1792]{3,2,1,0:T(8,128)(2,1)}, bf16[4,64,2048]{2,1,0:T(8,128)(2,1)}, bf16[4,256,2048]{2,1,0:T(8,128)(2,1)}, bf16[8,128,2048]{2,1,0:...) custom-call(f32[3,64,6144]{2,1,0:T(8,128)} %refs_0_.1, f32[3,64,8192]{2,1,0:T(8,128)} %refs_2_.1, ...), custom_call_target="tpu_custom_call" | custom-call | tf_op jit(solution)/shard_map/pallas_call | solution.py:1041
  121.2 3.0 convert_reduce_fusion
  124.2 0.5 copy-done
  124.7 1.2 fusion.1
  126.1 0.1 reshape.302
  126.2 0.7 slice_reduce_fusion.2
  127.1 4.7 %add_convert_fusion.norm = bf16[1024,2048]{1,0:T(8,128)(2,1)} fusion(f32[2048]{0:T(1024)S(1)} %add.213, f32[2048]{0:T(1024)S(1)} %mul.284, f32[1024]{0:T(1024)S(1)} %get-tuple-element.88, f32[1024]{0:T(1024)S(1)} %get-tuple-element.89, bf16[8,128,2048]{2,1,0:T(8,128)(2,1)} %get-tuple-element.32), kind=kLoop, calls=%fused_computation.4 | loop fusion | flops 12582912 | bytes 8413184 | tf_op jit(solution)/shard_map/convert_element_type | solution.py:1549
  131.9 0.1 reshape.306
  132.0 0.1 reshape.299
  132.1 11.8 %convolution_add_fusion.fu_ref = f32[1024,1792]{1,0:T(8,128)S(1)} fusion(bf16[1024,2048]{1,0:T(8,128)(2,1)} %add_convert_fusion.norm, bf16[2048,1792]{1,0:T(8,128)(2,1)} %bitcast.84, f32[1792]{0:T(1024)S(1)} %pad_maximum_fusion.1), kind=kOutput, calls=%fused_computation.15 | convolution fusion | flops 7518027776 | bytes 18881536 | tf_op jit(solution)/shard_map/dot_general | solution.py:1551
  144.0 9.4 %fusion.43 = (f32[1024]{0:T(1024)S(1)}, bf16[1024,1024]{1,0:T(8,128)(2,1)}, bf16[1024,1024]{1,0:T(8,128)(2,1)}) fusion(f32[1024,1792]{1,0:T(8,128)S(1)} %convolution_add_fusion.fu_ref, bf16[1024,2048]{1,0:T(8,128)(2,1)S(1)} %bitcast.91, bf16[1024,2048]{1,0:T(8,128)(2,1)S(1)} %bitcast.88), kind=kOutput, calls=%fused_computation.130 | convolution fusion | flops 4323277824 | bytes 16781312 | tf_op jit(solution)/shard_map/dot_general | solution.py:1554
  153.4 1.0 copy.33.seg_col_ref
  154.5 4.3 %convolution_convert_fusion.do_ref = bf16[1024,256]{1,0:T(8,128)(2,1)} fusion(bf16[1024,2048]{1,0:T(8,128)(2,1)} %bitcast.89, bf16[256,2048]{1,0:T(8,128)(2,1)S(1)} %bitcast.93), kind=kOutput, calls=%fused_computation.21 | convolution fusion | flops 1074003968 | bytes 5767168 | tf_op jit(solution)/shard_map/dot_general | solution.py:1557
  158.8 1.9 fusion.18
  160.7 15.0 %shard_map.194 = (bf16[1024,256]{1,0:T(8,128)(2,1)}, bf16[1024,1792]{1,0:T(8,128)(2,1)}, f32[2,1,768]{2,1,0:T(1,128)}) custom-call(f32[1024,1792]{1,0:T(8,128)} %copy-done.3, bf16[1024,256]{1,0:T(8,128)(2,1)} %convolution_convert_fusion.do_ref, bf16[1024,1024]{1,0:T(8,128)(2,1)} %get-tuple-element.68.du_ref, s32[1024,1]{1,0:T(8,128)} %copy.33.seg_col_ref, ...), custom_call_target="tpu_custom_call" | custom-call | flops 1342177280 | bytes 9437184 | tf_op jit(solution)/shard_map/pallas_call | solution.py:506
  175.7 0.7 reduce_sum.92
  176.5 0.6 fusion.22.sums
  177.1 1.0 copy.35.inverse
  178.2 1.0 copy.34.mean
  179.2 136.2 %shard_map.195 = (bf16[8,64,1792]{2,1,0:T(8,128)(2,1)}, f32[64,2048]{1,0:T(8,128)}, f32[256,2048]{1,0:T(8,128)}, f32[128,2048]{1,0:T(8,128)}, f32[128,2048]{1,0:T(8,128)}, /*index=5*/f32[8,64,128]{2,1,0:T(8,128)}) custom-call(bf16[1024,2048]{1,0:T(8,128)(2,1)} %add_convert_fusion.norm, bf16[1024,1792]{1,0:T(8,128)(2,1)} %get-tuple-element.38.dcat, ...), custom_call_target="tpu_custom_call" | custom-call | tf_op jit(solution)/shard_map/pallas_call | solution.py:1414
  315.4 1.1 reshape.289
  316.7 0.1 copy.39
  316.8 0.1 reshape.294
  316.9 0.8 copy.38
  317.6 0.1 mul.350
  317.7 0.7 copy.40
  318.5 0.1 mul.354
  318.6 0.7 copy.37
  319.3 0.1 reshape_squeeze.2
  319.6 0.1 reshape.291
  319.7 0.7 multiply_subtract_fusion.2
  320.5 0.7 multiply_subtract_fusion.1
  321.4 0.6 pad_maximum_fusion.refs_7_
  322.0 22.6 %shard_map.196 = (f32[1,1,1573568]{2,1,0:T(1,128)}, f32[1,1,1573568]{2,1,0:T(1,128)}, f32[1,1,1573568]{2,1,0:T(1,128)}, f32[64,6144]{1,0:T(8,128)}, f32[64,8192]{1,0:T(8,128)}) custom-call(f32[3,64,6144]{2,1,0:T(8,128)} %refs_0_.1, f32[3,64,2048]{2,1,0:T(8,128)} %refs_1_.1, f32[3,64,8192]{2,1,0:T(8,128)} %refs_2_.1, f32[3,256,2048]{2,1,0:T(8,128)} %refs_3_.1, ...), custom_call_target="tpu_custom_call" | custom-call | flops 31471360 | bytes 44059904 | tf_op jit(solution)/shard_map/pallas_call | solution.py:737
  344.7 0.6 constant_dynamic-update-slice_fusion
  345.2 0.6 constant_dynamic-update-slice_fusion.1
  345.8 0.6 constant_dynamic-update-slice_fusion.2
  346.4 0.2 convert_reduce_fusion.1
  346.6 0.3 fusion.14
  346.9 0.3 multiply_reduce_fusion
  347.4 3.3 fusion.15
  350.8 0.8 copy.49
  351.6 1.3 copy.50
  (87 shorter events, 1.5 us)
Async XLA Ops:
  3.4 2.7 copy-start.18
  4.8 0.7 copy-start.17
  121.2 3.5 copy-start
  121.2 4.7 %copy-start.13 = (f32[4,8,8,128]{3,2,1,0:T(8,128)S(1)}, f32[4,8,8,128]{3,2,1,0:T(8,128)}, u32[]{:S(2)}) copy-start(f32[4,8,8,128]{3,2,1,0:T(8,128)} %get-tuple-element.33) | copy-start | bytes 393220
  127.0 4.8 %copy-start.11 = (f32[2048]{0:T(1024)}, f32[2048]{0:T(1024)S(1)}, u32[]{:S(2)}) copy-start(f32[2048]{0:T(1024)S(1)} %mul.284) | copy-start | bytes 24580
  132.1 11.8 %copy-start.6 = (bf16[4,256,2048]{2,1,0:T(8,128)(2,1)S(1)}, bf16[4,256,2048]{2,1,0:T(8,128)(2,1)}, u32[]{:S(2)}) copy-start(bf16[4,256,2048]{2,1,0:T(8,128)(2,1)} %get-tuple-element.37) | copy-start | bytes 12582916
  132.1 11.8 %copy-start.7 = (bf16[8,128,2048]{2,1,0:T(8,128)(2,1)S(1)}, bf16[8,128,2048]{2,1,0:T(8,128)(2,1)}, u32[]{:S(2)}) copy-start(bf16[8,128,2048]{2,1,0:T(8,128)(2,1)} %get-tuple-element.35) | copy-start | bytes 12582916
  143.9 9.4 %copy-start.3 = (f32[1024,1792]{1,0:T(8,128)}, f32[1024,1792]{1,0:T(8,128)S(1)}, u32[]{:S(2)}) copy-start(f32[1024,1792]{1,0:T(8,128)S(1)} %convolution_add_fusion.fu_ref) | copy-start | bytes 22020100
  144.0 10.5 %copy-start.10 = (bf16[4,64,2048]{2,1,0:T(8,128)(2,1)S(1)}, bf16[4,64,2048]{2,1,0:T(8,128)(2,1)}, u32[]{:S(2)}) copy-start(bf16[4,64,2048]{2,1,0:T(8,128)(2,1)} %get-tuple-element.36) | copy-start | bytes 3145732
  153.4 5.3 %copy-start.16 = (s32[1,2,4,128]{3,2,1,0:T(4,128)}, s32[1,2,4,128]{3,2,1,0:T(4,128)S(1)}, u32[]{:S(2)}) copy-start(s32[1,2,4,128]{3,2,1,0:T(4,128)S(1)} %dynamic-slice_convert_fusion) | copy-start | bytes 12292
  160.7 15.7 %copy-start.4 = (bf16[1,128,2048]{2,1,0:T(8,128)(2,1)S(1)}, bf16[1,128,2048]{2,1,0:T(8,128)(2,1)}, u32[]{:S(2)}) copy-start(bf16[1,128,2048]{2,1,0:T(8,128)(2,1)} %param.12) | copy-start | bytes 1572868
  316.6 28.0 %copy-start.19 = (f32[64,4]{0,1:T(4,128)}, f32[64,4]{0,1:T(4,128)S(1)}, u32[]{:S(2)}) copy-start(f32[64,4]{0,1:T(4,128)S(1)} %pad_maximum_fusion.2) | copy-start | bytes 3076
  319.7 25.0 %copy-start.21 = (f32[1,192]{1,0:T(1,128)}, f32[1,192]{1,0:T(1,128)S(1)}, u32[]{:S(2)}) copy-start(f32[1,192]{1,0:T(1,128)S(1)} %constant_dynamic-slice_fusion.4) | copy-start | bytes 2308
  320.4 24.2 %copy-start.20 = (f32[1,1,256]{2,1,0:T(1,128)}, f32[1,1,256]{2,1,0:T(1,128)S(1)}, u32[]{:S(2)}) copy-start(f32[1,1,256]{2,1,0:T(1,128)S(1)} %constant_dynamic-slice_fusion.3) | copy-start | bytes 3076
  322.0 24.4 %copy-start.1 = (bf16[1,128,2048]{2,1,0:T(8,128)(2,1)S(1)}, bf16[1,128,2048]{2,1,0:T(8,128)(2,1)}, u32[]{:S(2)}) copy-start(bf16[1,128,2048]{2,1,0:T(8,128)(2,1)} %param.10) | copy-start | bytes 1572868
  322.0 24.9 %copy-start.8 = (f32[128,2048]{1,0:T(8,128)S(1)}, f32[128,2048]{1,0:T(8,128)}, u32[]{:S(2)}) copy-start(f32[128,2048]{1,0:T(8,128)} %get-tuple-element.42) | copy-start | bytes 3145732
  322.0 24.9 %copy-start.12 = (f32[2048]{0:T(1024)S(1)}, f32[2048]{0:T(1024)}, u32[]{:S(2)}) copy-start(f32[2048]{0:T(1024)} %copy-done.11) | copy-start | bytes 24580
  322.0 25.3 %copy-start.15 = (f32[32,64]{1,0:T(8,128)S(1)}, f32[32,64]{1,0:T(8,128)}, u32[]{:S(2)}) copy-start(f32[32,64]{1,0:T(8,128)} %get-tuple-element.54) | copy-start | bytes 24580
  322.0 25.3 %copy-start.14 = (f32[32,64]{1,0:T(8,128)S(1)}, f32[32,64]{1,0:T(8,128)}, u32[]{:S(2)}) copy-start(f32[32,64]{1,0:T(8,128)} %get-tuple-element.55) | copy-start | bytes 24580
  322.0 25.4 %copy-start.5 = (bf16[1,128,2048]{2,1,0:T(8,128)(2,1)S(1)}, bf16[1,128,2048]{2,1,0:T(8,128)(2,1)}, u32[]{:S(2)}) copy-start(bf16[1,128,2048]{2,1,0:T(8,128)(2,1)} %param.12) | copy-start | bytes 1572868
  346.4 5.2 %copy-start.2 = (f32[256,2048]{1,0:T(8,128)S(1)}, f32[256,2048]{1,0:T(8,128)}, u32[]{:S(2)}) copy-start(f32[256,2048]{1,0:T(8,128)} %get-tuple-element.118.refs_6_) | copy-start | bytes 6291460
  347.4 3.4 copy-start.9

commit v6 on v5

--- a/solution.py
+++ b/solution.py
@@ -548,9 +548,9 @@
     planes, cores, shards = groups
     qkv_state, dense_state, up_state, down_state, cat_ref, dense_grad, down_grad, small_ref = refs[:8]
     flat = refs[8:11]
-    qkv_out, up_out, cat_buf = refs[11:14]
-    outs = refs[14:17]
-    step_sem, rest_sem = refs[17:]
+    qkv_out, dense_out, up_out, down_out, cat_buf = refs[11:16]
+    outs = refs[16:19]
+    step_sem, rest_sem = refs[19:]
     step = pl.program_id(0)
     lane = lax.broadcasted_iota(jnp.int32, (8, 128), 1)
     sub = lax.broadcasted_iota(jnp.int32, (8, 128), 0)
@@ -641,9 +641,9 @@
         return lambda place, column, size: grad[place, pl.ds(column, size)]
 
     place_rows(qkv_state, qkv_grad, *plan[0], keep=qkv_out)
-    place_rows(dense_state, plain(dense_grad), *plan[1])
+    place_rows(dense_state, plain(dense_grad), *plan[1], keep=dense_out)
     place_rows(up_state, up_grad, *plan[2], keep=up_out)
-    place_rows(down_state, plain(down_grad), *plan[3])
+    place_rows(down_state, plain(down_grad), *plan[3], keep=down_out)
 
     def flush(entry, row, count, sem):
         place = pl.ds(pl.multiple_of(row * 128, 128), count * 128)
@@ -728,25 +728,23 @@
     in_specs = [
         pl.BlockSpec((3, rows, tiles * 128), lambda s: (0, s, 0)) for rows, tiles, start, shifted in plan
     ]
-    qkv_rows, up_rows = plan[0][0], plan[2][0]
+    qkv_rows = plan[0][0]
     in_specs.append(pl.BlockSpec((cat_sum.shape[0], qkv_rows, cat_sum.shape[2]), lambda s: (0, s, 0)))
     in_specs.append(pl.BlockSpec((plan[1][0], plan[1][1] * 128), lambda s: (s, 0)))
     in_specs.append(pl.BlockSpec((plan[3][0], plan[3][1] * 128), lambda s: (s, 0)))
     in_specs.append(pl.BlockSpec((3, small_row, 128), lambda s: (0, 0, 0)))
     whole_rows = entries // 128
-    *outs, qkv_grad, up_grad = pl.pallas_call(
+    *outs, qkv_grad, dense_grad, up_grad, down_grad = pl.pallas_call(
         partial(owner_update_kernel, plan, small_plan, groups, steps, whole_rows),
         grid=(steps,),
         in_specs=in_specs,
         out_specs=[pl.BlockSpec(memory_space=pl.ANY)] * 3
         + [
-            pl.BlockSpec((qkv_rows, plan[0][1] * 128), lambda s: (s, 0)),
-            pl.BlockSpec((up_rows, plan[2][1] * 128), lambda s: (s, 0)),
+            pl.BlockSpec((rows, tiles * 128), lambda s: (s, 0)) for rows, tiles, start, shifted in plan
         ],
         out_shape=[jax.ShapeDtypeStruct((1, 1, entries), jnp.float32)] * 3
         + [
-            jax.ShapeDtypeStruct(states[0].shape[1:], jnp.float32),
-            jax.ShapeDtypeStruct(states[2].shape[1:], jnp.float32),
+            jax.ShapeDtypeStruct(state.shape[1:], jnp.float32) for state in states
         ],
         scratch_shapes=[pltpu.VMEM((cat_sum.shape[0], qkv_rows, cat_sum.shape[2]), jnp.float32)]
         + [pltpu.VMEM((out_rows, 128), jnp.float32)] * 3
@@ -762,7 +760,7 @@
             lax.dynamic_update_slice(out, new[entries_of][-tail:].reshape(1, 1, tail), (0, 0, whole_rows * 128))
             for out, (new, entries_of) in zip(outs, ((small_new[-1], entry) for entry in range(3)))
         ]
-    return tuple(outs), qkv_grad, up_grad
+    return tuple(outs), qkv_grad, dense_grad, up_grad, down_grad
 
 
 class Wires:
@@ -854,9 +852,9 @@
 
 
 def gather_kernel(
-    qkv_state, up_state, dense_state, down_state, tokens, cotangent, vectors,
-    cat_out, dense_out, down_out, x_out, dy_out, vec_out,
-    qkv_buf, up_buf, dense_buf, down_buf, pieces, dense, down,
+    vector_start, qkv_state, up_state, dense_state, down_state, tokens, cotangent, vectors,
+    cat_out, dense_out, down_out, x_out, dy_out, vec_out, normed_out, mean_out, inverse_out,
+    qkv_buf, up_buf, dense_buf, down_buf, pieces, dense, down, x_stage, vec_stage, gain_buf,
     load_sem, send_sems, group_sem, first_sem, second_sem, far_sem, up_sem, low_sem, core_sem, local_sem,
 ):
     net = Wires(send_sems)
@@ -997,36 +995,119 @@
                 hand_on(index)
     hand_on(cat_units[0])
     hand_on(vec_units[0])
-    for distance in range(1, shards):
-        for stream in range(2):
-            hop_arrived(stream, distance)
-            if distance + 1 < shards:
-                hop(stream, distance + 1)
-        for mask in order[1 + (distance - 1) * 3 : 1 + distance * 3]:
-            hand_on(vec_units[mask])
-            hand_on(cat_units[mask])
-
-    for index, (source, place) in enumerate(units):
+    def unit_arrived(index):
+        place = units[index][1]
         if relay_first[index]:
             net.arrived(place(plane ^ 2), second_sem.at[index])
         else:
             net.arrived(place(plane ^ 1), first_sem.at[index])
         net.arrived(place(plane ^ 3), far_sem.at[index])
-    for stream in range(2):
-        other = streams[stream][1]
-        for slot in range(2 * shards):
-            if slot == shards:
+
+    def norm_vectors():
+        for mask in order:
+            unit_arrived(vec_units[mask])
+        copies[5].wait()
+        fetch = pltpu.make_async_copy(vec_out, vec_stage, load_sem.at[4])
+        fetch.start()
+        fetch.wait()
+        lane = lax.broadcasted_iota(jnp.int32, (1, 128), 1)
+        for vector in range(2):
+            row, low = divmod(vector_start + vector * HD, 128)
+            for pair in range(vec_stage.shape[0] * group // 2):
+                halves = []
+                for side in range(2):
+                    owner_plane, owner = divmod(2 * pair + side, group)
+                    half = vec_stage[owner_plane, owner, pl.ds(row, 1), :]
+                    halves.append(half if low == side * HD else pltpu.roll(half, HD, 1))
+                value = jnp.where(lane < HD, halves[0], halves[1])
+                gain_buf[pl.ds(vector, 1), pl.ds(pair * 128, 128)] = value.astype(jnp.bfloat16).astype(
+                    jnp.float32
+                )
+
+    def normalize(source, index):
+        step = 16
+
+        def body(turn, carry):
+            rows = pl.ds(pl.multiple_of(turn * step, step), step)
+            x = source[rows, :].astype(jnp.float32)
+            mean = jnp.mean(x, axis=1, keepdims=True)
+            center = x - mean
+            inverse = lax.rsqrt(jnp.mean(center * center, axis=1, keepdims=True) + norm_eps)
+            normed = center * inverse * gain_buf[0:1, :] + gain_buf[1:2, :]
+            normed_out[index, rows, :] = normed.astype(jnp.bfloat16)
+            mean_out[index, rows, :] = mean
+            inverse_out[index, rows, :] = inverse
+            return carry
+
+        lax.fori_loop(0, source.shape[0] // step, body, 0)
+
+    def normalize_far(which, place, when):
+        index = which * shards + place
+
+        @pl.when(when)
+        def there():
+            fetch = pltpu.make_async_copy(x_out.at[index], x_stage, load_sem.at[4])
+            fetch.start()
+            fetch.wait()
+            normalize(x_stage, index)
+
+    def normalize_at(distance):
+        for upward in (True, False):
+            origin = shard - distance if upward else shard + distance
+            held = (origin >= 0) if upward else (origin < shards)
+            near = jnp.clip(origin, 0, shards - 1)
+            normalize_far(core, near, held)
+
+    def normalize_core(distance):
+        for upward in (True, False):
+            if distance == 0 and not upward:
                 continue
-            origin = shard - slot if slot < shards else shard + (slot - shards)
-            held = None if slot == 0 else ((origin >= 0) & (origin < shards))
+            origin = shard - distance if upward else shard + distance
+            held = (origin >= 0) & (origin < shards)
             near = jnp.clip(origin, 0, shards - 1)
-            net.arrived(other.at[(1 - core) * shards + near], core_sem.at[stream, slot], held)
-    for copy in copies:
+            slot = distance if upward else shards + distance
+            net.arrived(x_out.at[(1 - core) * shards + near], core_sem.at[0, slot], held)
+            normalize_far(1 - core, near, held)
+
+    for distance in range(1, shards):
+        if distance == shards - 1:
+            for mask in order[1 + (distance - 1) * 3 :]:
+                hand_on(vec_units[mask])
+                hand_on(cat_units[mask])
+            norm_vectors()
+            normalize(tokens, mine)
+            normalize_core(0)
+            for nearer in range(1, distance):
+                normalize_at(nearer)
+                normalize_core(nearer)
+        for stream in range(2):
+            hop_arrived(stream, distance)
+            if distance + 1 < shards:
+                hop(stream, distance + 1)
+        if distance < shards - 1:
+            for mask in order[1 + (distance - 1) * 3 : 1 + distance * 3]:
+                hand_on(vec_units[mask])
+                hand_on(cat_units[mask])
+    normalize_at(shards - 1)
+    normalize_core(shards - 1)
+
+    for index in own_units:
+        unit_arrived(index)
+    for mask in order:
+        unit_arrived(cat_units[mask])
+    for slot in range(2 * shards):
+        if slot == shards:
+            continue
+        origin = shard - slot if slot < shards else shard + (slot - shards)
+        held = None if slot == 0 else ((origin >= 0) & (origin < shards))
+        near = jnp.clip(origin, 0, shards - 1)
+        net.arrived(dy_out.at[(1 - core) * shards + near], core_sem.at[1, slot], held)
+    for copy in copies[:5]:
         copy.wait()
     net.drain()
 
 
-def gather_wires(qkv, up, dense, down, tokens, cotangent, vectors):
+def gather_wires(qkv, up, dense, down, tokens, cotangent, vectors, vector_start):
     group, shards = lax.axis_size("core") * lax.axis_size("shard"), lax.axis_size("shard")
     planes = lax.axis_size("plane")
     width = (qkv.shape[2] + up.shape[2]) // group
@@ -1039,9 +1120,9 @@
 
     dma = pltpu.SemaphoreType.DMA
     return pl.pallas_call(
-        gather_kernel,
+        partial(gather_kernel, vector_start),
         in_specs=[hbm] * 4 + [vmem] * 3,
-        out_specs=[hbm] * 6,
+        out_specs=[hbm] * 6 + [vmem] * 3,
         out_shape=[
             out(planes, group, qkv.shape[1], width),
             out(planes, *dense.shape[1:]),
@@ -1049,6 +1130,9 @@
             out(group, *tokens.shape),
             out(group, *cotangent.shape),
             out(planes, group, *vectors.shape, dtype=vectors.dtype),
+            out(group, *tokens.shape),
+            out(group, tokens.shape[0], 1, dtype=jnp.float32),
+            out(group, tokens.shape[0], 1, dtype=jnp.float32),
         ],
         scratch_shapes=[
             pltpu.VMEM(qkv.shape[1:], qkv.dtype),
@@ -1058,7 +1142,10 @@
             pltpu.VMEM((group, qkv.shape[1], width), jnp.bfloat16),
             pltpu.VMEM(dense.shape[1:], jnp.bfloat16),
             pltpu.VMEM(down.shape[1:], jnp.bfloat16),
-            dma((4,)),
+            pltpu.VMEM(tokens.shape, tokens.dtype),
+            pltpu.VMEM((planes, group) + vectors.shape, vectors.dtype),
+            pltpu.VMEM((8, tokens.shape[1]), jnp.float32),
+            dma((5,)),
             dma((2 * (group - 1) + 3 * units + 2 * 2 * (shards - 1) + 2 * (2 * shards - 1),)),
             dma((2, group)),
             dma((units,)),
@@ -1496,7 +1583,7 @@
     vec_rows = -(-sum(vec_sizes) // 1024) * 8
     vec_own = jnp.pad(jnp.concatenate(vec_list), (0, vec_rows * 128 - sum(vec_sizes))).reshape(vec_rows, 128)
 
-    cat_w, dense_w, down_w, x_all, dy_all, vec_all = gather_wires(
+    cat_w, dense_w, down_w, x_all, dy_all, vec_all, norm_bf, x_mean, inverse = gather_wires(
         qkv_weight_state,
         up_weight_state,
         dense_weight_state,
@@ -1504,6 +1591,7 @@
         tokens,
         cotangent,
         vec_own,
+        sum(vec_sizes[:2]),
     )
 
     cat_w = cat_w.reshape(D, 3 * head_width + unit_width)
@@ -1541,12 +1629,9 @@
     segments = segments.astype(jnp.int32).reshape(cores, shards * tokens_here)
     cat_bias = jnp.concatenate([qkv_bias, up_bias])
 
-    x_float = x_all.astype(jnp.float32)
-    x_mean = jnp.mean(x_float, axis=-1, keepdims=True)
-    center = x_float - x_mean
-    inverse = lax.rsqrt(jnp.mean(center * center, axis=-1, keepdims=True) + norm_eps)
-    x_hat = center * inverse
-    norm_bf = lax.optimization_barrier((x_hat * norm_gain + norm_shift).astype(jnp.bfloat16))
+    norm_bf = norm_bf.reshape(rows, D)
+    x_mean = x_mean.reshape(rows, 1)
+    inverse = inverse.reshape(rows, 1)
 
     fu = jnp.dot(norm_bf, cat_w, preferred_element_type=jnp.float32) + cat_bias
     pre_act = fu[:, 3 * head_width :]
@@ -1610,7 +1695,7 @@
     )
     input_grad = cotangent.astype(jnp.float32) + x_grad
 
-    new, qkv_grad, up_grad = owner_update(
+    new, qkv_grad, dense_grad, up_grad, down_grad = owner_update(
         (qkv_weight_state, dense_weight_state, up_weight_state, down_weight_state),
         cat_sum,
         (dense_grad, down_grad),

time: 355 us -> 362 us (1.020)
  Pallas kernels: 289 us -> 312 us
  other arithmetic: 24.3 us -> 14.2 us
  local copies, waits for them, and re-layouts: 13.2 us -> 8.71 us
    pallas_call x1, Pallas kernels: 115 us -> 138 us  [gather_wires(): pl.pallas_call(partial(gather_kernel, vector_start), in_specs=[hbm] * 4 +...]
    convert_element_type x1 -> x0, other arithmetic: 4.74 us -> none  [fast_body(): (x_hat * norm_gain + norm_shift).astype(jnp.bfloat16)]
    reduce_sum x2 -> x0, other arithmetic: 4.17 us -> none  [the longest x1 2.95 us: fast_body(): x_mean = jnp.mean(x_float, axis=-1, keepdims=True)]
where the time goes in v6:
time: 362 us; the launch traced here: 359 us
  Pallas kernels  312 us (86%)
  matrix products  23.3 us (6%)
  other arithmetic  14.2 us (4%)
  local copies, waits for them, and re-layouts  8.71 us (2%)
    pallas_call x1, Pallas kernels, gather_wires(): pl.pallas_call(partial(gather_kernel, vector_start), in_specs=[hbm] * 4 +...  138 us
    pallas_call x1, Pallas kernels, reduce_wires(): pl.pallas_call(reduce_kernel, in_specs=[hbm] * 3 + [vmem] * 2 + [hbm] * 6...  135 us
    pallas_call x1, Pallas kernels, owner_update(): pl.pallas_call(partial(owner_update_kernel, plan, small_plan, groups, ste...  23.4 us
    pallas_call x1, Pallas kernels, attention(): pl.pallas_call(attention_kernel, grid=(count,), in_specs=[pl.BlockSpec((r...  15 us
    dot_general x1, matrix products, fast_body(): fu = jnp.dot(norm_bf, cat_w, preferred_element_type=jnp.float32) + cat_bias  11.8 us
    dot_general x1, matrix products, fast_body(): grad_hidden = jnp.dot(dy_all, down_w.T, preferred_element_type=jnp.float32)  9.37 us

profile of v6, /device:TPU:0, one launch (start us, length us, event | category | flops | bytes accessed | tf_op | source)
XLA Modules:
  0.0 358.9 jit_solution(15535749495232674379)
XLA Ops:
  0.7 1.3 slice_multiply_fusion
  1.9 0.1 reshape.226
  2.0 1.4 slice_multiply_fusion.4
  3.4 1.3 slice_multiply_fusion.2
  4.7 0.7 convert_bitcast_fusion.1
  5.4 0.7 fusion.24.vectors
  6.0 138.1 %shard_map.193 = (bf16[4,8,64,1792]{3,2,1,0:T(8,128)(2,1)}, bf16[4,64,2048]{2,1,0:T(8,128)(2,1)}, bf16[4,256,2048]{2,1,0:T(8,128)(2,1)}, bf16[8,128,2048]{2,1,0:...) custom-call(f32[3,64,6144]{2,1,0:T(8,128)} %refs_0_.1, ...), custom_call_target="tpu_custom_call" | custom-call | tf_op jit(solution)/shard_map/pallas_call | solution.py:1122
  144.1 0.9 reshape.230
  145.1 0.7 slice_convert_fusion
  145.9 0.1 reshape.261
  146.0 0.1 reshape.254
  146.1 11.8 %convolution_add_fusion.fu_ref = f32[1024,1792]{1,0:T(8,128)S(1)} fusion(bf16[1024,2048]{1,0:T(8,128)(2,1)} %bitcast.88, bf16[2048,1792]{1,0:T(8,128)(2,1)} %bitcast.79, f32[1792]{0:T(1024)S(1)} %pad_maximum_fusion.1), kind=kOutput, calls=%fused_computation.10 | convolution fusion | flops 7518027776 | bytes 18881536 | tf_op jit(solution)/shard_map/dot_general | solution.py:1636
  158.0 9.4 %fusion.39 = (f32[1024]{0:T(1024)S(1)}, bf16[1024,1024]{1,0:T(8,128)(2,1)}, bf16[1024,1024]{1,0:T(8,128)(2,1)}) fusion(f32[1024,1792]{1,0:T(8,128)S(1)} %convolution_add_fusion.fu_ref, bf16[1024,2048]{1,0:T(8,128)(2,1)S(1)} %bitcast.86, bf16[1024,2048]{1,0:T(8,128)(2,1)S(1)} %bitcast.83), kind=kOutput, calls=%fused_computation.120 | convolution fusion | flops 4323277824 | bytes 16781312 | tf_op jit(solution)/shard_map/dot_general | solution.py:1639
  167.4 2.1 convolution_convert_fusion.do_ref
  169.5 1.0 copy.31.seg_col_ref
  170.6 1.9 fusion.16
  172.5 15.0 %shard_map.194 = (bf16[1024,256]{1,0:T(8,128)(2,1)}, bf16[1024,1792]{1,0:T(8,128)(2,1)}, f32[2,1,768]{2,1,0:T(1,128)}) custom-call(f32[1024,1792]{1,0:T(8,128)} %copy-done.1, bf16[1024,256]{1,0:T(8,128)(2,1)} %convolution_convert_fusion.do_ref, bf16[1024,1024]{1,0:T(8,128)(2,1)} %get-tuple-element.77.du_ref, s32[1024,1]{1,0:T(8,128)} %copy.31.seg_col_ref, ...), custom_call_target="tpu_custom_call" | custom-call | flops 1342177280 | bytes 9437184 | tf_op jit(solution)/shard_map/pallas_call | solution.py:506
  187.5 0.7 reduce_sum.72
  188.2 0.1 convert_reduce_fusion.1
  188.3 0.6 fusion.20.sums
  188.9 135.2 %shard_map.195 = (bf16[8,64,1792]{2,1,0:T(8,128)(2,1)}, f32[64,2048]{1,0:T(8,128)}, f32[256,2048]{1,0:T(8,128)}, f32[128,2048]{1,0:T(8,128)}, f32[128,2048]{1,0:T(8,128)}, /*index=5*/f32[8,64,128]{2,1,0:T(8,128)}) custom-call(bf16[1024,2048]{1,0:T(8,128)(2,1)} %bitcast.89, bf16[1024,1792]{1,0:T(8,128)(2,1)} %get-tuple-element.43.dcat, ...), custom_call_target="tpu_custom_call" | custom-call | tf_op jit(solution)/shard_map/pallas_call | solution.py:1501
  324.2 1.1 reshape.244
  325.4 0.1 copy.35
  325.5 0.1 reshape.249
  325.6 0.7 copy.34
  326.4 0.1 mul.325
  326.5 0.7 copy.36
  327.2 0.1 mul.329
  327.3 0.7 copy.33
  328.0 0.1 reshape_squeeze.2
  328.1 0.1 reshape.245
  328.3 0.1 reshape.246
  328.4 0.7 multiply_subtract_fusion.2
  329.2 0.6 multiply_subtract_fusion.1
  329.8 0.1 fusion.23
  329.9 0.1 fusion.22
  330.0 0.1 fusion.21
  330.0 0.6 pad_maximum_fusion.refs_7_
  330.7 23.4 %shard_map.196 = (f32[1,1,1573568]{2,1,0:T(1,128)}, f32[1,1,1573568]{2,1,0:T(1,128)}, f32[1,1,1573568]{2,1,0:T(1,128)}, f32[64,6144]{1,0:T(8,128)}, f32[64,2048]...) custom-call(f32[3,64,6144]{2,1,0:T(8,128)} %refs_0_.1, f32[3,64,2048]{2,1,0:T(8,128)} %refs_1_.1, ...), custom_call_target="tpu_custom_call" | custom-call | flops 31471360 | bytes 44059904 | tf_op jit(solution)/shard_map/pallas_call | solution.py:737
  354.1 0.6 constant_dynamic-update-slice_fusion
  354.7 0.6 constant_dynamic-update-slice_fusion.1
  355.3 0.6 constant_dynamic-update-slice_fusion.2
  355.9 0.1 reshape.259
  356.0 0.1 slice_reduce_fusion.1
  356.2 0.2 convert_reduce_fusion
  356.3 0.3 fusion.12
  356.7 0.3 multiply_reduce_fusion
  357.2 1.7 fusion.13
  (65 shorter events, 0.8 us)
Async XLA Ops:
  3.4 2.7 copy-start.12
  4.7 0.7 copy-start.11
  146.1 11.9 %copy-start.4 = (bf16[4,256,2048]{2,1,0:T(8,128)(2,1)S(1)}, bf16[4,256,2048]{2,1,0:T(8,128)(2,1)}, u32[]{:S(2)}) copy-start(bf16[4,256,2048]{2,1,0:T(8,128)(2,1)} %get-tuple-element.42) | copy-start | bytes 12582916
  146.1 11.9 %copy-start.5 = (bf16[8,128,2048]{2,1,0:T(8,128)(2,1)S(1)}, bf16[8,128,2048]{2,1,0:T(8,128)(2,1)}, u32[]{:S(2)}) copy-start(bf16[8,128,2048]{2,1,0:T(8,128)(2,1)} %get-tuple-element.40) | copy-start | bytes 12582916
  158.0 9.4 %copy-start.1 = (f32[1024,1792]{1,0:T(8,128)}, f32[1024,1792]{1,0:T(8,128)S(1)}, u32[]{:S(2)}) copy-start(f32[1024,1792]{1,0:T(8,128)S(1)} %convolution_add_fusion.fu_ref) | copy-start | bytes 22020100
  158.0 9.4 %copy-start.7 = (bf16[4,64,2048]{2,1,0:T(8,128)(2,1)S(1)}, bf16[4,64,2048]{2,1,0:T(8,128)(2,1)}, u32[]{:S(2)}) copy-start(bf16[4,64,2048]{2,1,0:T(8,128)(2,1)} %get-tuple-element.41) | copy-start | bytes 3145732
  169.5 3.0 copy-start.10
  172.5 15.7 %copy-start.2 = (bf16[1,128,2048]{2,1,0:T(8,128)(2,1)S(1)}, bf16[1,128,2048]{2,1,0:T(8,128)(2,1)}, u32[]{:S(2)}) copy-start(bf16[1,128,2048]{2,1,0:T(8,128)(2,1)} %param.12) | copy-start | bytes 1572868
  325.4 28.7 %copy-start.13 = (f32[64,4]{0,1:T(4,128)}, f32[64,4]{0,1:T(4,128)S(1)}, u32[]{:S(2)}) copy-start(f32[64,4]{0,1:T(4,128)S(1)} %pad_maximum_fusion.2) | copy-start | bytes 3076
  328.4 25.7 %copy-start.15 = (f32[1,192]{1,0:T(1,128)}, f32[1,192]{1,0:T(1,128)S(1)}, u32[]{:S(2)}) copy-start(f32[1,192]{1,0:T(1,128)S(1)} %constant_dynamic-slice_fusion.4) | copy-start | bytes 2308
  329.2 24.9 %copy-start.14 = (f32[1,1,256]{2,1,0:T(1,128)}, f32[1,1,256]{2,1,0:T(1,128)S(1)}, u32[]{:S(2)}) copy-start(f32[1,1,256]{2,1,0:T(1,128)S(1)} %constant_dynamic-slice_fusion.3) | copy-start | bytes 3076
  330.7 25.2 %copy-start.9 = (f32[4,2,4,256]{3,2,1,0:T(4,128)S(1)}, f32[4,2,4,256]{3,2,1,0:T(4,128)}, u32[]{:S(2)}) copy-start(f32[4,2,4,256]{3,2,1,0:T(4,128)} %get-tuple-element.81) | copy-start | bytes 98308
  330.7 25.5 %copy-start = (bf16[1,128,2048]{2,1,0:T(8,128)(2,1)S(1)}, bf16[1,128,2048]{2,1,0:T(8,128)(2,1)}, u32[]{:S(2)}) copy-start(bf16[1,128,2048]{2,1,0:T(8,128)(2,1)} %param.10) | copy-start | bytes 1572868
  330.7 26.0 %copy-start.6 = (f32[128,2048]{1,0:T(8,128)S(1)}, f32[128,2048]{1,0:T(8,128)}, u32[]{:S(2)}) copy-start(f32[128,2048]{1,0:T(8,128)} %get-tuple-element.50) | copy-start | bytes 3145732
  330.7 26.5 %copy-start.3 = (bf16[1,128,2048]{2,1,0:T(8,128)(2,1)S(1)}, bf16[1,128,2048]{2,1,0:T(8,128)(2,1)}, u32[]{:S(2)}) copy-start(bf16[1,128,2048]{2,1,0:T(8,128)(2,1)} %param.12) | copy-start | bytes 1572868
  330.7 26.5 %copy-start.8 = (f32[128,2048]{1,0:T(8,128)S(1)}, f32[128,2048]{1,0:T(8,128)}, u32[]{:S(2)}) copy-start(f32[128,2048]{1,0:T(8,128)} %get-tuple-element.49) | copy-start | bytes 3145732

commit v7 on v6

--- a/solution.py
+++ b/solution.py
@@ -993,8 +993,6 @@
         if position == 2:
             for index in own_units:
                 hand_on(index)
-    hand_on(cat_units[0])
-    hand_on(vec_units[0])
     def unit_arrived(index):
         place = units[index][1]
         if relay_first[index]:
@@ -1069,27 +1067,29 @@
             net.arrived(x_out.at[(1 - core) * shards + near], core_sem.at[0, slot], held)
             normalize_far(1 - core, near, held)
 
-    for distance in range(1, shards):
-        if distance == shards - 1:
-            for mask in order[1 + (distance - 1) * 3 :]:
-                hand_on(vec_units[mask])
-                hand_on(cat_units[mask])
-            norm_vectors()
-            normalize(tokens, mine)
-            normalize_core(0)
-            for nearer in range(1, distance):
-                normalize_at(nearer)
-                normalize_core(nearer)
-        for stream in range(2):
-            hop_arrived(stream, distance)
-            if distance + 1 < shards:
-                hop(stream, distance + 1)
+    def advance(stream, distance):
+        hop_arrived(stream, distance)
+        if distance + 1 < shards:
+            hop(stream, distance + 1)
+
+    advance(0, 1)
+    advance(1, 1)
+    for mask in order:
+        hand_on(vec_units[mask])
+    for mask in order:
+        hand_on(cat_units[mask])
+    norm_vectors()
+    normalize(tokens, mine)
+    normalize_core(0)
+    normalize_at(1)
+    for distance in range(2, shards):
+        advance(0, distance)
         if distance < shards - 1:
-            for mask in order[1 + (distance - 1) * 3 : 1 + distance * 3]:
-                hand_on(vec_units[mask])
-                hand_on(cat_units[mask])
-    normalize_at(shards - 1)
+            advance(1, distance)
+        normalize_core(distance - 1)
+        normalize_at(distance)
     normalize_core(shards - 1)
+    advance(1, shards - 1)
 
     for index in own_units:
         unit_arrived(index)

time: 362 us -> 357 us (0.986)
  Pallas kernels: 312 us -> 307 us
    pallas_call x1, Pallas kernels: 138 us -> 133 us  [gather_wires(): pl.pallas_call(partial(gather_kernel, vector_start), in_specs=[hbm] * 4 +...]
where the time goes in v7:
time: 357 us; the launch traced here: 354 us
  Pallas kernels  307 us (86%)
  matrix products  23.3 us (7%)
  other arithmetic  14.2 us (4%)
  local copies, waits for them, and re-layouts  8.71 us (2%)
    pallas_call x1, Pallas kernels, reduce_wires(): pl.pallas_call(reduce_kernel, in_specs=[hbm] * 3 + [vmem] * 2 + [hbm] * 6...  136 us
    pallas_call x1, Pallas kernels, gather_wires(): pl.pallas_call(partial(gather_kernel, vector_start), in_specs=[hbm] * 4 +...  133 us
    pallas_call x1, Pallas kernels, owner_update(): pl.pallas_call(partial(owner_update_kernel, plan, small_plan, groups, ste...  23.4 us
    pallas_call x1, Pallas kernels, attention(): pl.pallas_call(attention_kernel, grid=(count,), in_specs=[pl.BlockSpec((r...  15 us
    dot_general x1, matrix products, fast_body(): fu = jnp.dot(norm_bf, cat_w, preferred_element_type=jnp.float32) + cat_bias  11.8 us
    dot_general x1, matrix products, fast_body(): grad_hidden = jnp.dot(dy_all, down_w.T, preferred_element_type=jnp.float32)  9.37 us

profile of v7, /device:TPU:0, one launch (start us, length us, event | category | flops | bytes accessed | tf_op | source)
XLA Modules:
  0.0 354.5 jit_solution(9313011034155714520)
XLA Ops:
  0.7 1.3 slice_multiply_fusion
  1.9 0.1 reshape.226
  2.0 1.4 slice_multiply_fusion.4
  3.4 1.3 slice_multiply_fusion.2
  4.7 0.7 convert_bitcast_fusion.1
  5.4 0.7 fusion.24.vectors
  6.0 132.6 %shard_map.193 = (bf16[4,8,64,1792]{3,2,1,0:T(8,128)(2,1)}, bf16[4,64,2048]{2,1,0:T(8,128)(2,1)}, bf16[4,256,2048]{2,1,0:T(8,128)(2,1)}, bf16[8,128,2048]{2,1,0:...) custom-call(f32[3,64,6144]{2,1,0:T(8,128)} %refs_0_.1, ...), custom_call_target="tpu_custom_call" | custom-call | tf_op jit(solution)/shard_map/pallas_call | solution.py:1122
  138.6 0.9 reshape.230
  139.6 0.7 slice_convert_fusion
  140.3 0.1 reshape.261
  140.5 0.1 reshape.254
  140.6 11.8 %convolution_add_fusion.fu_ref = f32[1024,1792]{1,0:T(8,128)S(1)} fusion(bf16[1024,2048]{1,0:T(8,128)(2,1)} %bitcast.88, bf16[2048,1792]{1,0:T(8,128)(2,1)} %bitcast.79, f32[1792]{0:T(1024)S(1)} %pad_maximum_fusion.1), kind=kOutput, calls=%fused_computation.10 | convolution fusion | flops 7518027776 | bytes 18881536 | tf_op jit(solution)/shard_map/dot_general | solution.py:1636
  152.5 9.4 %fusion.39 = (f32[1024]{0:T(1024)S(1)}, bf16[1024,1024]{1,0:T(8,128)(2,1)}, bf16[1024,1024]{1,0:T(8,128)(2,1)}) fusion(f32[1024,1792]{1,0:T(8,128)S(1)} %convolution_add_fusion.fu_ref, bf16[1024,2048]{1,0:T(8,128)(2,1)S(1)} %bitcast.86, bf16[1024,2048]{1,0:T(8,128)(2,1)S(1)} %bitcast.83), kind=kOutput, calls=%fused_computation.120 | convolution fusion | flops 4323277824 | bytes 16781312 | tf_op jit(solution)/shard_map/dot_general | solution.py:1639
  161.9 2.1 convolution_convert_fusion.do_ref
  164.0 1.0 copy.31.seg_col_ref
  165.1 1.9 fusion.16
  167.0 15.0 %shard_map.194 = (bf16[1024,256]{1,0:T(8,128)(2,1)}, bf16[1024,1792]{1,0:T(8,128)(2,1)}, f32[2,1,768]{2,1,0:T(1,128)}) custom-call(f32[1024,1792]{1,0:T(8,128)} %copy-done.1, bf16[1024,256]{1,0:T(8,128)(2,1)} %convolution_convert_fusion.do_ref, bf16[1024,1024]{1,0:T(8,128)(2,1)} %get-tuple-element.77.du_ref, s32[1024,1]{1,0:T(8,128)} %copy.31.seg_col_ref, ...), custom_call_target="tpu_custom_call" | custom-call | flops 1342177280 | bytes 9437184 | tf_op jit(solution)/shard_map/pallas_call | solution.py:506
  182.0 0.7 reduce_sum.72
  182.7 0.1 convert_reduce_fusion.1
  182.8 0.6 fusion.20.sums
  183.4 136.3 %shard_map.195 = (bf16[8,64,1792]{2,1,0:T(8,128)(2,1)}, f32[64,2048]{1,0:T(8,128)}, f32[256,2048]{1,0:T(8,128)}, f32[128,2048]{1,0:T(8,128)}, f32[128,2048]{1,0:T(8,128)}, /*index=5*/f32[8,64,128]{2,1,0:T(8,128)}) custom-call(bf16[1024,2048]{1,0:T(8,128)(2,1)} %bitcast.89, bf16[1024,1792]{1,0:T(8,128)(2,1)} %get-tuple-element.43.dcat, ...), custom_call_target="tpu_custom_call" | custom-call | tf_op jit(solution)/shard_map/pallas_call | solution.py:1501
  319.7 1.1 reshape.244
  321.0 0.1 copy.35
  321.1 0.1 reshape.249
  321.2 0.7 copy.34
  321.9 0.1 mul.325
  322.0 0.7 copy.36
  322.7 0.1 mul.329
  322.8 0.7 copy.33
  323.5 0.1 reshape_squeeze.2
  323.7 0.1 reshape.245
  323.8 0.1 reshape.246
  323.9 0.7 multiply_subtract_fusion.2
  324.7 0.6 multiply_subtract_fusion.1
  325.3 0.1 fusion.23
  325.4 0.1 fusion.22
  325.5 0.1 fusion.21
  325.6 0.6 pad_maximum_fusion.refs_7_
  326.2 23.4 %shard_map.196 = (f32[1,1,1573568]{2,1,0:T(1,128)}, f32[1,1,1573568]{2,1,0:T(1,128)}, f32[1,1,1573568]{2,1,0:T(1,128)}, f32[64,6144]{1,0:T(8,128)}, f32[64,2048]...) custom-call(f32[3,64,6144]{2,1,0:T(8,128)} %refs_0_.1, f32[3,64,2048]{2,1,0:T(8,128)} %refs_1_.1, ...), custom_call_target="tpu_custom_call" | custom-call | flops 31471360 | bytes 44059904 | tf_op jit(solution)/shard_map/pallas_call | solution.py:737
  349.7 0.6 constant_dynamic-update-slice_fusion
  350.2 0.6 constant_dynamic-update-slice_fusion.1
  350.8 0.6 constant_dynamic-update-slice_fusion.2
  351.4 0.1 reshape.259
  351.5 0.1 slice_reduce_fusion.1
  351.7 0.2 convert_reduce_fusion
  351.9 0.3 fusion.12
  352.2 0.3 multiply_reduce_fusion
  352.7 1.7 fusion.13
  (65 shorter events, 0.8 us)
Async XLA Ops:
  3.4 2.7 copy-start.12
  4.7 0.7 copy-start.11
  140.6 11.8 %copy-start.4 = (bf16[4,256,2048]{2,1,0:T(8,128)(2,1)S(1)}, bf16[4,256,2048]{2,1,0:T(8,128)(2,1)}, u32[]{:S(2)}) copy-start(bf16[4,256,2048]{2,1,0:T(8,128)(2,1)} %get-tuple-element.42) | copy-start | bytes 12582916
  140.6 11.8 %copy-start.5 = (bf16[8,128,2048]{2,1,0:T(8,128)(2,1)S(1)}, bf16[8,128,2048]{2,1,0:T(8,128)(2,1)}, u32[]{:S(2)}) copy-start(bf16[8,128,2048]{2,1,0:T(8,128)(2,1)} %get-tuple-element.40) | copy-start | bytes 12582916
  152.4 9.4 %copy-start.1 = (f32[1024,1792]{1,0:T(8,128)}, f32[1024,1792]{1,0:T(8,128)S(1)}, u32[]{:S(2)}) copy-start(f32[1024,1792]{1,0:T(8,128)S(1)} %convolution_add_fusion.fu_ref) | copy-start | bytes 22020100
  152.5 9.4 %copy-start.7 = (bf16[4,64,2048]{2,1,0:T(8,128)(2,1)S(1)}, bf16[4,64,2048]{2,1,0:T(8,128)(2,1)}, u32[]{:S(2)}) copy-start(bf16[4,64,2048]{2,1,0:T(8,128)(2,1)} %get-tuple-element.41) | copy-start | bytes 3145732
  164.0 3.0 copy-start.10
  167.0 15.7 %copy-start.2 = (bf16[1,128,2048]{2,1,0:T(8,128)(2,1)S(1)}, bf16[1,128,2048]{2,1,0:T(8,128)(2,1)}, u32[]{:S(2)}) copy-start(bf16[1,128,2048]{2,1,0:T(8,128)(2,1)} %param.12) | copy-start | bytes 1572868
  321.0 28.7 %copy-start.13 = (f32[64,4]{0,1:T(4,128)}, f32[64,4]{0,1:T(4,128)S(1)}, u32[]{:S(2)}) copy-start(f32[64,4]{0,1:T(4,128)S(1)} %pad_maximum_fusion.2) | copy-start | bytes 3076
  323.9 25.7 %copy-start.15 = (f32[1,192]{1,0:T(1,128)}, f32[1,192]{1,0:T(1,128)S(1)}, u32[]{:S(2)}) copy-start(f32[1,192]{1,0:T(1,128)S(1)} %constant_dynamic-slice_fusion.4) | copy-start | bytes 2308
  324.7 24.9 %copy-start.14 = (f32[1,1,256]{2,1,0:T(1,128)}, f32[1,1,256]{2,1,0:T(1,128)S(1)}, u32[]{:S(2)}) copy-start(f32[1,1,256]{2,1,0:T(1,128)S(1)} %constant_dynamic-slice_fusion.3) | copy-start | bytes 3076
  326.2 25.2 %copy-start.9 = (f32[4,2,4,256]{3,2,1,0:T(4,128)S(1)}, f32[4,2,4,256]{3,2,1,0:T(4,128)}, u32[]{:S(2)}) copy-start(f32[4,2,4,256]{3,2,1,0:T(4,128)} %get-tuple-element.81) | copy-start | bytes 98308
  326.2 25.5 %copy-start = (bf16[1,128,2048]{2,1,0:T(8,128)(2,1)S(1)}, bf16[1,128,2048]{2,1,0:T(8,128)(2,1)}, u32[]{:S(2)}) copy-start(bf16[1,128,2048]{2,1,0:T(8,128)(2,1)} %param.10) | copy-start | bytes 1572868
  326.2 26.0 %copy-start.6 = (f32[128,2048]{1,0:T(8,128)S(1)}, f32[128,2048]{1,0:T(8,128)}, u32[]{:S(2)}) copy-start(f32[128,2048]{1,0:T(8,128)} %get-tuple-element.50) | copy-start | bytes 3145732
  326.2 26.5 %copy-start.3 = (bf16[1,128,2048]{2,1,0:T(8,128)(2,1)S(1)}, bf16[1,128,2048]{2,1,0:T(8,128)(2,1)}, u32[]{:S(2)}) copy-start(bf16[1,128,2048]{2,1,0:T(8,128)(2,1)} %param.12) | copy-start | bytes 1572868
  326.2 26.5 %copy-start.8 = (f32[128,2048]{1,0:T(8,128)S(1)}, f32[128,2048]{1,0:T(8,128)}, u32[]{:S(2)}) copy-start(f32[128,2048]{1,0:T(8,128)} %get-tuple-element.49) | copy-start | bytes 3145732

commit v8 on v5

--- a/solution.py
+++ b/solution.py
@@ -548,9 +548,9 @@
     planes, cores, shards = groups
     qkv_state, dense_state, up_state, down_state, cat_ref, dense_grad, down_grad, small_ref = refs[:8]
     flat = refs[8:11]
-    qkv_out, up_out, cat_buf = refs[11:14]
-    outs = refs[14:17]
-    step_sem, rest_sem = refs[17:]
+    qkv_out, dense_out, up_out, down_out, cat_buf = refs[11:16]
+    outs = refs[16:19]
+    step_sem, rest_sem = refs[19:]
     step = pl.program_id(0)
     lane = lax.broadcasted_iota(jnp.int32, (8, 128), 1)
     sub = lax.broadcasted_iota(jnp.int32, (8, 128), 0)
@@ -641,9 +641,9 @@
         return lambda place, column, size: grad[place, pl.ds(column, size)]
 
     place_rows(qkv_state, qkv_grad, *plan[0], keep=qkv_out)
-    place_rows(dense_state, plain(dense_grad), *plan[1])
+    place_rows(dense_state, plain(dense_grad), *plan[1], keep=dense_out)
     place_rows(up_state, up_grad, *plan[2], keep=up_out)
-    place_rows(down_state, plain(down_grad), *plan[3])
+    place_rows(down_state, plain(down_grad), *plan[3], keep=down_out)
 
     def flush(entry, row, count, sem):
         place = pl.ds(pl.multiple_of(row * 128, 128), count * 128)
@@ -728,25 +728,23 @@
     in_specs = [
         pl.BlockSpec((3, rows, tiles * 128), lambda s: (0, s, 0)) for rows, tiles, start, shifted in plan
     ]
-    qkv_rows, up_rows = plan[0][0], plan[2][0]
+    qkv_rows = plan[0][0]
     in_specs.append(pl.BlockSpec((cat_sum.shape[0], qkv_rows, cat_sum.shape[2]), lambda s: (0, s, 0)))
     in_specs.append(pl.BlockSpec((plan[1][0], plan[1][1] * 128), lambda s: (s, 0)))
     in_specs.append(pl.BlockSpec((plan[3][0], plan[3][1] * 128), lambda s: (s, 0)))
     in_specs.append(pl.BlockSpec((3, small_row, 128), lambda s: (0, 0, 0)))
     whole_rows = entries // 128
-    *outs, qkv_grad, up_grad = pl.pallas_call(
+    *outs, qkv_grad, dense_grad, up_grad, down_grad = pl.pallas_call(
         partial(owner_update_kernel, plan, small_plan, groups, steps, whole_rows),
         grid=(steps,),
         in_specs=in_specs,
         out_specs=[pl.BlockSpec(memory_space=pl.ANY)] * 3
         + [
-            pl.BlockSpec((qkv_rows, plan[0][1] * 128), lambda s: (s, 0)),
-            pl.BlockSpec((up_rows, plan[2][1] * 128), lambda s: (s, 0)),
+            pl.BlockSpec((rows, tiles * 128), lambda s: (s, 0)) for rows, tiles, start, shifted in plan
         ],
         out_shape=[jax.ShapeDtypeStruct((1, 1, entries), jnp.float32)] * 3
         + [
-            jax.ShapeDtypeStruct(states[0].shape[1:], jnp.float32),
-            jax.ShapeDtypeStruct(states[2].shape[1:], jnp.float32),
+            jax.ShapeDtypeStruct(state.shape[1:], jnp.float32) for state in states
         ],
         scratch_shapes=[pltpu.VMEM((cat_sum.shape[0], qkv_rows, cat_sum.shape[2]), jnp.float32)]
         + [pltpu.VMEM((out_rows, 128), jnp.float32)] * 3
@@ -762,7 +760,7 @@
             lax.dynamic_update_slice(out, new[entries_of][-tail:].reshape(1, 1, tail), (0, 0, whole_rows * 128))
             for out, (new, entries_of) in zip(outs, ((small_new[-1], entry) for entry in range(3)))
         ]
-    return tuple(outs), qkv_grad, up_grad
+    return tuple(outs), qkv_grad, dense_grad, up_grad, down_grad
 
 
 class Wires:
@@ -1111,10 +1109,10 @@
 
 
 def reduce_kernel(
-    norm, dcat, x_all, mean, inverse, attn, hidden, dy, cat_w, dense_w, down_w, sums,
+    norm, dcat, x_all, mean_rows, inverse_rows, attn, hidden, dy, cat_w, dense_w, down_w, sums,
     cat_out, dense_out, down_out, mixed_out, norm_out, sums_out,
     cat_part, down_part, dense_part, cat_in, down_in, dense_in,
-    tokens, token_in, token_line, token_last, sum_buf,
+    tokens, token_in, token_line, token_last, sum_buf, mean, inverse,
     wide, hidden_turned, attn_turned, norm_chunk, norm_turned, cat_chunk, x_chunk, down_chunk, dense_chunk, dy_chunk,
     send_sems, near_sem, pass_sem, group_sem, core_sem, line_sem, sum_sem, local_sem, chunk_sem,
 ):
@@ -1293,6 +1291,10 @@
     first_sums(0)
 
     sum_buf[4] = sums[...]
+    for flat, column in ((mean_rows, mean), (inverse_rows, inverse)):
+        turned = flat[...].T
+        for member in range(flat.shape[0]):
+            column[pl.ds(member * flat.shape[1], flat.shape[1]), :] = turned[:, member : member + 1]
     gain_row = width // 128
 
     def norm_copies(n, slot):
@@ -1435,6 +1437,8 @@
             scratch(2, shards, token_rows, model),
             scratch(2, token_rows, model),
             scratch(5, *sums.shape, dtype=jnp.float32),
+            scratch(rows, 1, dtype=jnp.float32),
+            scratch(rows, 1, dtype=jnp.float32),
             scratch(rows, max(width, hidden.shape[1] + attn.shape[1])),
             scratch(hidden.shape[1], rows),
             scratch(attn.shape[1], rows),
@@ -1567,8 +1571,8 @@
         norm_bf,
         dcat,
         x_all,
-        x_mean,
-        inverse,
+        x_mean.reshape(group, tokens_here),
+        inverse.reshape(group, tokens_here),
         attn,
         hidden,
         dy_all,
@@ -1610,7 +1614,7 @@
     )
     input_grad = cotangent.astype(jnp.float32) + x_grad
 
-    new, qkv_grad, up_grad = owner_update(
+    new, qkv_grad, dense_grad, up_grad, down_grad = owner_update(
         (qkv_weight_state, dense_weight_state, up_weight_state, down_weight_state),
         cat_sum,
         (dense_grad, down_grad),

time: 355 us -> 350 us (0.986)
  local copies, waits for them, and re-layouts: 13.2 us -> 9.11 us
where the time goes in v8:
time: 350 us; the launch traced here: 348 us
  Pallas kernels  289 us (83%)
  matrix products  25.5 us (7%)
  other arithmetic  23.3 us (7%)
  local copies, waits for them, and re-layouts  9.11 us (3%)
    pallas_call x1, Pallas kernels, reduce_wires(): pl.pallas_call(reduce_kernel, in_specs=[hbm] * 3 + [vmem] * 2 + [hbm] * 6...  136 us
    pallas_call x1, Pallas kernels, gather_wires(): pl.pallas_call(gather_kernel, in_specs=[hbm] * 4 + [vmem] * 3, out_specs=...  115 us
    pallas_call x1, Pallas kernels, owner_update(): pl.pallas_call(partial(owner_update_kernel, plan, small_plan, groups, ste...  23.4 us
    pallas_call x1, Pallas kernels, attention(): pl.pallas_call(attention_kernel, grid=(count,), in_specs=[pl.BlockSpec((r...  15 us
    dot_general x1, matrix products, fast_body(): fu = jnp.dot(norm_bf, cat_w, preferred_element_type=jnp.float32) + cat_bias  11.8 us
    dot_general x1, matrix products, fast_body(): grad_hidden = jnp.dot(dy_all, down_w.T, preferred_element_type=jnp.float32)  9.37 us

profile of v8, /device:TPU:0, one launch (start us, length us, event | category | flops | bytes accessed | tf_op | source)
XLA Modules:
  0.0 348.2 jit_solution(16215793186421290464)
XLA Ops:
  0.6 1.3 slice_multiply_fusion
  2.0 1.4 slice_multiply_fusion.4
  3.4 1.4 slice_multiply_fusion.2
  4.8 0.7 convert_bitcast_fusion.1
  5.5 0.7 fusion.26.vectors
  6.1 115.0 %shard_map.193 = (bf16[4,8,64,1792]{3,2,1,0:T(8,128)(2,1)}, bf16[4,64,2048]{2,1,0:T(8,128)(2,1)}, bf16[4,256,2048]{2,1,0:T(8,128)(2,1)}, bf16[8,128,2048]{2,1,0:...) custom-call(f32[3,64,6144]{2,1,0:T(8,128)} %refs_0_.1, f32[3,64,8192]{2,1,0:T(8,128)} %refs_2_.1, ...), custom_call_target="tpu_custom_call" | custom-call | tf_op jit(solution)/shard_map/pallas_call | solution.py:1039
  121.2 3.0 convert_reduce_fusion
  124.2 0.5 copy-done
  124.6 1.2 fusion.1
  125.9 0.6 add_rsqrt_fusion
  126.5 0.1 convert_bitcast_fusion
  126.6 0.1 reshape.285
  126.7 0.7 slice_reduce_fusion.2
  127.6 4.7 %add_convert_fusion.norm = bf16[1024,2048]{1,0:T(8,128)(2,1)} fusion(f32[2048]{0:T(1024)S(1)} %add.209, f32[2048]{0:T(1024)S(1)} %mul.284, f32[1024]{0:T(1024)S(1)} %get-tuple-element.92, f32[1024]{0:T(1024)S(1)} %get-tuple-element.93, bf16[8,128,2048]{2,1,0:T(8,128)(2,1)} %get-tuple-element.34), kind=kLoop, calls=%fused_computation.4 | loop fusion | flops 12582912 | bytes 8413184 | tf_op jit(solution)/shard_map/convert_element_type | solution.py:1553
  132.4 0.1 reshape.289
  132.5 0.1 reshape.282
  132.7 11.8 %convolution_add_fusion.fu_ref = f32[1024,1792]{1,0:T(8,128)S(1)} fusion(bf16[1024,2048]{1,0:T(8,128)(2,1)} %add_convert_fusion.norm, bf16[2048,1792]{1,0:T(8,128)(2,1)} %bitcast.82, f32[1792]{0:T(1024)S(1)} %pad_maximum_fusion.1), kind=kOutput, calls=%fused_computation.15 | convolution fusion | flops 7518027776 | bytes 18881536 | tf_op jit(solution)/shard_map/dot_general | solution.py:1555
  144.6 9.4 %fusion.43 = (f32[1024]{0:T(1024)S(1)}, bf16[1024,1024]{1,0:T(8,128)(2,1)}, bf16[1024,1024]{1,0:T(8,128)(2,1)}) fusion(f32[1024,1792]{1,0:T(8,128)S(1)} %convolution_add_fusion.fu_ref, bf16[1024,2048]{1,0:T(8,128)(2,1)S(1)} %bitcast.89, bf16[1024,2048]{1,0:T(8,128)(2,1)S(1)} %bitcast.86), kind=kOutput, calls=%fused_computation.130 | convolution fusion | flops 4323277824 | bytes 16781312 | tf_op jit(solution)/shard_map/dot_general | solution.py:1558
  154.0 1.0 copy.31.seg_col_ref
  155.0 4.3 %convolution_convert_fusion.do_ref = bf16[1024,256]{1,0:T(8,128)(2,1)} fusion(bf16[1024,2048]{1,0:T(8,128)(2,1)} %bitcast.87, bf16[256,2048]{1,0:T(8,128)(2,1)S(1)} %bitcast.91), kind=kOutput, calls=%fused_computation.21 | convolution fusion | flops 1074003968 | bytes 5767168 | tf_op jit(solution)/shard_map/dot_general | solution.py:1561
  159.4 1.9 fusion.18
  161.3 15.0 %shard_map.194 = (bf16[1024,256]{1,0:T(8,128)(2,1)}, bf16[1024,1792]{1,0:T(8,128)(2,1)}, f32[2,1,768]{2,1,0:T(1,128)}) custom-call(f32[1024,1792]{1,0:T(8,128)} %copy-done.2, bf16[1024,256]{1,0:T(8,128)(2,1)} %convolution_convert_fusion.do_ref, bf16[1024,1024]{1,0:T(8,128)(2,1)} %get-tuple-element.72.du_ref, s32[1024,1]{1,0:T(8,128)} %copy.31.seg_col_ref, ...), custom_call_target="tpu_custom_call" | custom-call | flops 1342177280 | bytes 9437184 | tf_op jit(solution)/shard_map/pallas_call | solution.py:506
  176.3 0.7 reduce_sum.92
  177.0 0.1 convert_reduce_fusion.2
  177.1 0.6 fusion.22.sums
  177.7 135.8 %shard_map.195 = (bf16[8,64,1792]{2,1,0:T(8,128)(2,1)}, f32[64,2048]{1,0:T(8,128)}, f32[256,2048]{1,0:T(8,128)}, f32[128,2048]{1,0:T(8,128)}, f32[128,2048]{1,0:T(8,128)}, /*index=5*/f32[8,64,128]{2,1,0:T(8,128)}) custom-call(bf16[1024,2048]{1,0:T(8,128)(2,1)} %add_convert_fusion.norm, bf16[1024,1792]{1,0:T(8,128)(2,1)} %get-tuple-element.40.dcat, ...), custom_call_target="tpu_custom_call" | custom-call | tf_op jit(solution)/shard_map/pallas_call | solution.py:1416
  313.5 1.1 reshape.272
  314.8 0.1 copy.35
  314.8 0.1 reshape.277
  315.0 0.8 copy.34
  315.7 0.1 mul.350
  315.8 0.8 copy.36
  316.6 0.1 mul.354
  316.7 0.8 copy.33
  317.5 0.1 reshape_squeeze.2
  317.6 0.1 reshape.273
  317.7 0.1 reshape.274
  317.9 0.7 multiply_subtract_fusion.2
  318.6 0.7 multiply_subtract_fusion.1
  319.6 0.6 pad_maximum_fusion.refs_7_
  320.2 23.4 %shard_map.196 = (f32[1,1,1573568]{2,1,0:T(1,128)}, f32[1,1,1573568]{2,1,0:T(1,128)}, f32[1,1,1573568]{2,1,0:T(1,128)}, f32[64,6144]{1,0:T(8,128)}, f32[64,2048]...) custom-call(f32[3,64,6144]{2,1,0:T(8,128)} %refs_0_.1, f32[3,64,2048]{2,1,0:T(8,128)} %refs_1_.1, ...), custom_call_target="tpu_custom_call" | custom-call | flops 31471360 | bytes 44059904 | tf_op jit(solution)/shard_map/pallas_call | solution.py:737
  343.7 0.6 constant_dynamic-update-slice_fusion
  344.3 0.6 constant_dynamic-update-slice_fusion.1
  344.8 0.6 constant_dynamic-update-slice_fusion.2
  345.4 0.2 convert_reduce_fusion.1
  345.6 0.3 fusion.14
  345.9 0.3 multiply_reduce_fusion
  346.4 1.8 fusion.15
  (83 shorter events, 1.2 us)
Async XLA Ops:
  3.4 2.7 copy-start.18
  4.8 0.7 copy-start.17
  121.2 3.5 copy-start
  121.2 5.3 %copy-start.12 = (f32[4,8,8,128]{3,2,1,0:T(8,128)S(1)}, f32[4,8,8,128]{3,2,1,0:T(8,128)}, u32[]{:S(2)}) copy-start(f32[4,8,8,128]{3,2,1,0:T(8,128)} %get-tuple-element.35) | copy-start | bytes 393220
  124.2 2.3 copy-start.16
  127.5 4.8 %copy-start.10 = (f32[2048]{0:T(1024)}, f32[2048]{0:T(1024)S(1)}, u32[]{:S(2)}) copy-start(f32[2048]{0:T(1024)S(1)} %mul.284) | copy-start | bytes 24580
  132.7 11.9 %copy-start.5 = (bf16[4,256,2048]{2,1,0:T(8,128)(2,1)S(1)}, bf16[4,256,2048]{2,1,0:T(8,128)(2,1)}, u32[]{:S(2)}) copy-start(bf16[4,256,2048]{2,1,0:T(8,128)(2,1)} %get-tuple-element.39) | copy-start | bytes 12582916
  132.7 11.9 %copy-start.6 = (bf16[8,128,2048]{2,1,0:T(8,128)(2,1)S(1)}, bf16[8,128,2048]{2,1,0:T(8,128)(2,1)}, u32[]{:S(2)}) copy-start(bf16[8,128,2048]{2,1,0:T(8,128)(2,1)} %get-tuple-element.37) | copy-start | bytes 12582916
  144.5 9.4 %copy-start.2 = (f32[1024,1792]{1,0:T(8,128)}, f32[1024,1792]{1,0:T(8,128)S(1)}, u32[]{:S(2)}) copy-start(f32[1024,1792]{1,0:T(8,128)S(1)} %convolution_add_fusion.fu_ref) | copy-start | bytes 22020100
  144.5 10.5 %copy-start.8 = (bf16[4,64,2048]{2,1,0:T(8,128)(2,1)S(1)}, bf16[4,64,2048]{2,1,0:T(8,128)(2,1)}, u32[]{:S(2)}) copy-start(bf16[4,64,2048]{2,1,0:T(8,128)(2,1)} %get-tuple-element.38) | copy-start | bytes 3145732
  154.0 5.3 %copy-start.15 = (s32[1,2,4,128]{3,2,1,0:T(4,128)}, s32[1,2,4,128]{3,2,1,0:T(4,128)S(1)}, u32[]{:S(2)}) copy-start(s32[1,2,4,128]{3,2,1,0:T(4,128)S(1)} %dynamic-slice_convert_fusion) | copy-start | bytes 12292
  161.2 15.7 %copy-start.3 = (bf16[1,128,2048]{2,1,0:T(8,128)(2,1)S(1)}, bf16[1,128,2048]{2,1,0:T(8,128)(2,1)}, u32[]{:S(2)}) copy-start(bf16[1,128,2048]{2,1,0:T(8,128)(2,1)} %param.12) | copy-start | bytes 1572868
  314.7 28.9 %copy-start.19 = (f32[64,4]{0,1:T(4,128)}, f32[64,4]{0,1:T(4,128)S(1)}, u32[]{:S(2)}) copy-start(f32[64,4]{0,1:T(4,128)S(1)} %pad_maximum_fusion.2) | copy-start | bytes 3076
  317.9 25.8 %copy-start.21 = (f32[1,192]{1,0:T(1,128)}, f32[1,192]{1,0:T(1,128)S(1)}, u32[]{:S(2)}) copy-start(f32[1,192]{1,0:T(1,128)S(1)} %constant_dynamic-slice_fusion.4) | copy-start | bytes 2308
  318.6 25.0 %copy-start.20 = (f32[1,1,256]{2,1,0:T(1,128)}, f32[1,1,256]{2,1,0:T(1,128)S(1)}, u32[]{:S(2)}) copy-start(f32[1,1,256]{2,1,0:T(1,128)S(1)} %constant_dynamic-slice_fusion.3) | copy-start | bytes 3076
  320.2 25.2 %copy-start.1 = (bf16[1,128,2048]{2,1,0:T(8,128)(2,1)S(1)}, bf16[1,128,2048]{2,1,0:T(8,128)(2,1)}, u32[]{:S(2)}) copy-start(bf16[1,128,2048]{2,1,0:T(8,128)(2,1)} %param.10) | copy-start | bytes 1572868
  320.2 25.7 %copy-start.7 = (f32[128,2048]{1,0:T(8,128)S(1)}, f32[128,2048]{1,0:T(8,128)}, u32[]{:S(2)}) copy-start(f32[128,2048]{1,0:T(8,128)} %get-tuple-element.44) | copy-start | bytes 3145732
  320.2 25.7 %copy-start.11 = (f32[2048]{0:T(1024)S(1)}, f32[2048]{0:T(1024)}, u32[]{:S(2)}) copy-start(f32[2048]{0:T(1024)} %copy-done.10) | copy-start | bytes 24580
  320.2 26.1 %copy-start.14 = (f32[32,64]{1,0:T(8,128)S(1)}, f32[32,64]{1,0:T(8,128)}, u32[]{:S(2)}) copy-start(f32[32,64]{1,0:T(8,128)} %get-tuple-element.58) | copy-start | bytes 24580
  320.2 26.1 %copy-start.13 = (f32[32,64]{1,0:T(8,128)S(1)}, f32[32,64]{1,0:T(8,128)}, u32[]{:S(2)}) copy-start(f32[32,64]{1,0:T(8,128)} %get-tuple-element.59) | copy-start | bytes 24580
  320.2 26.2 %copy-start.4 = (bf16[1,128,2048]{2,1,0:T(8,128)(2,1)S(1)}, bf16[1,128,2048]{2,1,0:T(8,128)(2,1)}, u32[]{:S(2)}) copy-start(bf16[1,128,2048]{2,1,0:T(8,128)(2,1)} %param.12) | copy-start | bytes 1572868
  320.2 26.2 %copy-start.9 = (f32[128,2048]{1,0:T(8,128)S(1)}, f32[128,2048]{1,0:T(8,128)}, u32[]{:S(2)}) copy-start(f32[128,2048]{1,0:T(8,128)} %get-tuple-element.43) | copy-start | bytes 3145732
